TPU v7x, 128 devices: a whole 4x4x4 slice. The times are simulated.
128 devices in a mesh: row: 16 (over y, z), col: 8 (over x, core).
Axes of the slice: x: 4, y: 4, z: 4, core: 2. Of those that a mesh axis runs over, the one named last changes fastest.
Arguments:
- matrix: bfloat16 [3, 8192, 6, 4096], P(None, 'row', None, 'col'), may hold values from -6 to 6
- multiplier: bfloat16 [2, 512, 512], replicated
- checksum_weight: float32 [3, 8192], P(None, 'row')
Outputs:
- factored: bfloat16 [3, 8192, 6, 4096], P(None, 'row', None, 'col')
- group_checksum: float32 [16, 6, 4096], P('row', None, 'col')
- total_checksum: float32 [6, 4096], P(None, 'col')
All inputs are finite; a program needn't handle non-finite values.
Results may differ from a plain program's by a relative error of at most 0.0056.
Values may be sent and summed in bfloat16 or wider, within the bound.
No kernel may reach another device: no remote copies, remote signals or barrier semaphores. Data moves between devices by JAX's collectives and lax.ppermute only.
A program may use at most 192 MiB of HBM per device.

v0:
```python
import jax
import jax.numpy as jnp
from jax import lax
from jax.experimental import pallas as pl
from jax.experimental.pallas import tpu as pltpu
from jax.sharding import Mesh
from jax.sharding import PartitionSpec as P

ROW = ("row_0", "row_1")
F32, BF16 = jnp.float32, jnp.bfloat16


def shifts(axis, pieces, pairs):
    return [pieces[0]] + [lax.ppermute(p, axis, pairs(s)) for s, p in enumerate(pieces) if s > 0]


def from_two(got, place):
    size = len(got)
    return lax.select_n(place, *got), lax.select_n((place + size - 1) % size, *got)


def bands_kernel(info_ref, early_ref, late_ref, *out_refs):
    parts = early_ref.shape[2]
    for s in range(parts):
        out_refs[s][:, 0] = early_ref[0, :, lax.rem(info_ref[2] + s, parts)]
        out_refs[parts + s][:, 0] = late_ref[0, s]


def panels_kernel(info_ref, panel_ref, *out_refs):
    parts = len(out_refs)
    for s in range(parts):
        out_refs[s][...] = panel_ref[:, 0, lax.rem(info_ref[0] + s, parts)]


def in_three(rows):
    high = rows.astype(BF16).astype(F32)
    middle = (rows - high).astype(BF16).astype(F32)
    low = rows - high - middle
    return jnp.concatenate([high, middle, low, jnp.zeros_like(rows)], axis=0).astype(BF16)


def times_rows(rows, right):
    product = jnp.dot(in_three(rows), right, preferred_element_type=F32)
    return product[0:8] + product[8:16] + product[16:24]


def weigh_kernel(weight_ref, tile_ref, out_ref):
    block_rows, _, width, _ = tile_ref.shape
    tile = tile_ref[...].reshape(block_rows * width, width)
    out_ref[0] = times_rows(weight_ref[...], tile)


def left_kernel(info_ref, panel_ref, corner_ref, multiplier_ref, weight_ref, left0_ref, left1_ref, sum_ref):
    step = pl.program_id(0)
    _, _, block_rows, piece, width = panel_ref.shape
    share = block_rows * piece
    row = lax.broadcasted_iota(jnp.int32, (share, width), 0)
    my_row = info_ref[1]

    def keep(value, pivot):
        return jnp.where((row < piece) & (my_row <= pivot), jnp.zeros_like(value), value)

    column0 = panel_ref[0, 0].reshape(share, width)
    column1 = panel_ref[0, 1].reshape(share, width)
    left0 = jnp.dot(column0, multiplier_ref[0], preferred_element_type=F32)
    left0 = keep(left0, 0).astype(BF16)
    column = jnp.dot(left0, corner_ref[...], preferred_element_type=F32)
    column = (column1.astype(F32) - column).astype(BF16)
    left1 = jnp.dot(column, multiplier_ref[1], preferred_element_type=F32)
    left1 = keep(left1, 1).astype(BF16)
    left0_ref[:, 0] = left0.reshape(block_rows, piece, width)
    left1_ref[:, 0] = left1.reshape(block_rows, piece, width)

    @pl.when(step == 0)
    def _():
        sum_ref[...] = jnp.zeros_like(sum_ref)

    sum_ref[0] += times_rows(weight_ref[0], left0)
    sum_ref[1] += times_rows(weight_ref[0], left1)


def trail_kernel(
    info_ref, left0_ref, left1_ref, second_ref, sums_ref, upper_ref, band_ref, base_ref, tile_ref, out_ref, check_ref
):
    width = second_ref.shape[0]
    first = pl.program_id(0) == 0
    my_col, my_row = info_ref[0], info_ref[1]
    upper0 = upper_ref[...].reshape(width, width)
    upper0 = jnp.where(first & (my_col == 0), jnp.zeros_like(upper0), upper0)
    upper1 = band_ref[...].reshape(width, width).astype(F32)
    upper1 = (upper1 - jnp.dot(second_ref[...], upper0, preferred_element_type=F32)).astype(BF16)
    upper1 = jnp.where(first & (my_col < 2), jnp.zeros_like(upper1), upper1)
    check_ref[0] = base_ref[0] - times_rows(sums_ref[0], upper0) - times_rows(sums_ref[1], upper1)
    for a in range(tile_ref.shape[0]):
        rows = slice(a * width, (a + 1) * width)
        product = jnp.dot(left0_ref[rows, :], upper0, preferred_element_type=F32)
        tile = (tile_ref[a, 0].astype(F32) - product).astype(BF16)
        product = jnp.dot(left1_ref[rows, :], upper1, preferred_element_type=F32)
        out_ref[a, 0] = (tile.astype(F32) - product).astype(BF16)
        for pivot, left_ref in enumerate((left0_ref, left1_ref)):
            below = True if a > 0 else my_row > pivot

            @pl.when(first & (my_col == pivot) & below)
            def _():
                out_ref[a, 0] = left_ref[rows, :]


def eliminate(matrix, multiplier, checksum_weight):
    block_rows, block, cols, _ = matrix.shape
    grid_rows, grid_cols = lax.axis_size(ROW), lax.axis_size("col")
    my_row, my_col = lax.axis_index(ROW), lax.axis_index("col")
    info = jnp.stack([my_col, my_row, lax.axis_index("row_1")]).astype(jnp.int32)
    tiles = matrix.transpose(0, 2, 1, 3)
    rows, piece, share = block_rows * block, block // grid_rows, block_rows * block // grid_cols
    weights = jnp.pad(checksum_weight.reshape(1, rows), ((0, 7), (0, 0)))
    smem = pl.BlockSpec(memory_space=pltpu.SMEM)
    column_of_tiles = pl.BlockSpec((block_rows, 1, block, block), lambda c: (0, c, 0, 0))
    one_check = pl.BlockSpec((1, 8, block), lambda c: (c, 0, 0))

    half, sides = cols // 2, lax.axis_size("row_1")
    my_y, my_z = lax.axis_index("row_0"), lax.axis_index("row_1")

    tall = tiles.reshape(block_rows * cols, sides, sides, piece, block)
    cell = jax.ShapeDtypeStruct((sides, half, piece, block), BF16)
    cells = pl.pallas_call(
        bands_kernel,
        out_shape=(cell,) * (2 * sides),
        grid=(half,),
        in_specs=[
            smem,
            pl.BlockSpec((1, sides, sides, piece, block), lambda c: (c, 0, 0, 0, 0)),
            pl.BlockSpec((1, sides, sides, piece, block), lambda c: (c + half, 0, 0, 0, 0)),
        ],
        out_specs=(pl.BlockSpec((sides, 1, piece, block), lambda c: (0, c, 0, 0)),) * (2 * sides),
        cost_estimate=pl.CostEstimate(flops=cols * block * block, bytes_accessed=4 * cols * block * block, transcendentals=0),
        name="bands",
    )(info, tall, tall)
    early = shifts(ROW, cells[:sides], lambda s: [(0, s), (1, (1 + s) % sides)])
    late = shifts(ROW, cells[sides:], lambda s: [(0, sides * s), (1, sides * s + 1)])

    strip = block // grid_cols
    deep = tiles.reshape(block_rows, cols, grid_cols, strip, block)
    cell = jax.ShapeDtypeStruct((block_rows, strip, block), BF16)
    cells = pl.pallas_call(
        panels_kernel,
        out_shape=(cell,) * grid_cols,
        grid=(1,),
        in_specs=[smem, pl.BlockSpec((block_rows, 1, grid_cols, strip, block), lambda j: (0, 0, 0, 0, 0))],
        out_specs=(pl.BlockSpec((block_rows, strip, block), lambda j: (0, 0, 0)),) * grid_cols,
        cost_estimate=pl.CostEstimate(flops=rows * block, bytes_accessed=4 * rows * block, transcendentals=0),
        name="panels",
    )(info, deep)
    panels = shifts("col", cells, lambda s: [(0, s), (1, (1 + s) % grid_cols)])
    panel0, panel1 = from_two(panels, my_col)

    early = jnp.stack(from_two(early, my_z), axis=1)
    early = shifts(ROW, list(early), lambda s: [(z, sides * s + z) for z in range(sides)])
    early = lax.select_n(my_y, *early)
    late = lax.select_n(my_y, *late)
    late = jnp.where(my_z == 1, jnp.roll(late, -1, axis=0), late)
    late = shifts(
        ROW,
        list(late),
        lambda s: [(sides * y + r, sides * y + (r + s) % sides) for y in range(sides) for r in (0, 1)],
    )
    late = jnp.stack(from_two(late, my_z))
    upper = lax.all_gather(jnp.concatenate([early, late], axis=1), ROW)
    upper = upper.reshape(grid_rows, 2 * cols, piece, block)

    corner = jnp.where(my_row == 1, panel0[0], panel1[0])
    corner = shifts("row_1", [corner] * sides, lambda s: [(0, s), (1, (1 + s) % sides)])
    corner = jnp.stack(from_two(corner, my_z))
    corner = shifts("row_0", [corner] * sides, lambda s: [(0, s)])
    corner = lax.select_n(my_y, *corner)
    around = lambda s: [(i, (i + s) % grid_cols) for i in range(grid_cols)]
    corner = shifts("col", [corner] * grid_cols, around)
    ordered = corner[::-1]
    ordered = lax.dynamic_slice_in_dim(jnp.stack(ordered + ordered[:-1]), grid_cols - 1 - my_col, grid_cols, 0)
    corners = ordered.transpose(1, 0, 2, 3).reshape(2, block, block)

    packed = jnp.stack([panel0, panel1])
    packed = jnp.stack(shifts("col", [packed] * grid_cols, around))

    base = pl.pallas_call(
        weigh_kernel,
        out_shape=jax.ShapeDtypeStruct((cols, 8, block), F32),
        grid=(cols,),
        in_specs=[pl.BlockSpec((8, rows), lambda c: (0, 0)), column_of_tiles],
        out_specs=one_check,
        cost_estimate=pl.CostEstimate(flops=64 * tiles.size, bytes_accessed=2 * tiles.size, transcendentals=0),
        name="weigh",
    )(weights, tiles)

    strips = weights.reshape(8, block_rows, grid_cols, strip).transpose(2, 0, 1, 3).reshape(grid_cols, 8, share)
    full = lambda *shape: pl.BlockSpec(shape, lambda j, *_: (0,) * len(shape))
    shared = pl.BlockSpec((block_rows, 1, strip, block), lambda j, info: (0, j, 0, 0))
    left_shape = jax.ShapeDtypeStruct((block_rows, grid_cols, strip, block), BF16)
    left0, left1, sums = pl.pallas_call(
        left_kernel,
        out_shape=(
            left_shape,
            left_shape,
            jax.ShapeDtypeStruct((2, 8, block), F32),
        ),
        grid_spec=pltpu.PrefetchScalarGridSpec(
            num_scalar_prefetch=1,
            grid=(grid_cols,),
            in_specs=[
                pl.BlockSpec((1, 2, block_rows, strip, block), lambda j, info: (lax.rem(info[0] - j + grid_cols, grid_cols), 0, 0, 0, 0)),
                full(block, block),
                full(2, block, block),
                pl.BlockSpec((1, 8, share), lambda j, info: (j, 0, 0)),
            ],
            out_specs=(shared, shared, full(2, 8, block)),
        ),
        cost_estimate=pl.CostEstimate(flops=6 * rows * block * block, bytes_accessed=12 * rows * block, transcendentals=0),
        name="left",
    )(info, packed, corners[0], multiplier, strips)
    left0, left1 = left0.reshape(rows, block), left1.reshape(rows, block)
    second_left = jnp.dot(corners[1], multiplier[0], preferred_element_type=F32).astype(BF16)

    own = jnp.concatenate([base[:, 0], sums[:, 0]], axis=0)
    total = own
    for mask in (1, 2, 4, 8):
        total = total + lax.ppermute(total, ROW, [(i, i ^ mask) for i in range(grid_rows)])
    pair = jnp.pad(jnp.stack([own, total], axis=1), ((0, 0), (0, 6), (0, 0)))

    whole = lambda *shape: pl.BlockSpec(shape, lambda c: (0,) * len(shape))
    out, checks = pl.pallas_call(
        trail_kernel,
        out_shape=(jax.ShapeDtypeStruct(tiles.shape, BF16), jax.ShapeDtypeStruct((cols, 8, block), F32)),
        grid=(cols,),
        in_specs=[
            smem,
            whole(rows, block),
            whole(rows, block),
            whole(block, block),
            whole(2, 8, block),
            pl.BlockSpec((grid_rows, 1, piece, block), lambda c: (0, c, 0, 0)),
            pl.BlockSpec((grid_rows, 1, piece, block), lambda c: (0, c + cols, 0, 0)),
            one_check,
            column_of_tiles,
        ],
        out_specs=(column_of_tiles, one_check),
        cost_estimate=pl.CostEstimate(flops=5 * rows * block * block * cols, bytes_accessed=4 * tiles.size, transcendentals=0),
        name="trail",
    )(info, left0, left1, second_left, pair[cols:], upper, upper, pair[:cols], tiles)
    return out.transpose(0, 2, 1, 3), checks[None, :, 0], checks[:, 1]


def solution(mesh):
    split = Mesh(mesh.devices.reshape(4, 4, mesh.shape["col"]), ("row_0", "row_1", "col"))
    in_specs = (P(None, ROW, None, "col"), P(), P(None, ROW))
    out_specs = (P(None, ROW, None, "col"), P(ROW, None, "col"), P(None, "col"))
    return jax.shard_map(eliminate, mesh=split, in_specs=in_specs, out_specs=out_specs, check_vma=False)
```

profile of v0, /device:TPU:0, one launch (start us, length us, event | category | flops | bytes accessed | tf_op | source)
XLA Modules:
  0.0 254.5 jit_solution(13543322667643312020)
XLA Ops:
  7.8 4.3 %bands.1 = (bf16[4,3,32,512]{3,2,1,0:T(8,128)(2,1)}, bf16[4,3,32,512]{3,2,1,0:T(8,128)(2,1)}, bf16[4,3,32,512]{3,2,1,0:T(8,128)(2,1)}, bf16[4,3,32,512]{3,2,1,0:...) custom-call(s32[3]{0:T(128)} %pad_add_fusion.info_ref, ...), custom_call_target="tpu_custom_call" | custom-call | flops 1572864 | bytes 6291456 | tf_op jit(solution)/shard_map/bands/pallas_call | solution.py:125
  12.1 3.6 %collective-permute-start.37 = (bf16[4,3,32,512]{3,2,1,0:T(8,128)(2,1)}, bf16[4,3,32,512]{3,2,1,0:T(8,128)(2,1)S(1)}, u32[]{:S(2)}, u32[]{:S(2)}) collective-permute-start(bf16[4,3,32,512]{3,2,1,0:T(8,128)(2,1)} %get-tuple-element.40), channel_id=1, source_target_pairs={{0,32},{8,40},{1,33},{9,41},{2,34},{10,42},{3,35},{11,43},{4,36},{... | collective-permute-start | bytes 1179656 | tf_op jit(solution)/shard_map/ppermute | solution.py:14
  19.4 3.8 %collective-permute-start.31 = (bf16[4,3,32,512]{3,2,1,0:T(8,128)(2,1)}, bf16[4,3,32,512]{3,2,1,0:T(8,128)(2,1)S(1)}, u32[]{:S(2)}, u32[]{:S(2)}) collective-permute-start(bf16[4,3,32,512]{3,2,1,0:T(8,128)(2,1)} %get-tuple-element.36), channel_id=1, source_target_pairs={{0,8},{8,16},{1,9},{9,17},{2,10},{10,18},{3,11},{11,19},{4,12},{12... | collective-permute-start | bytes 1179656 | tf_op jit(solution)/shard_map/ppermute | solution.py:14
  27.5 5.4 %collective-permute-done.38 = bf16[4,3,32,512]{3,2,1,0:T(8,128)(2,1)S(1)} collective-permute-done((bf16[4,3,32,512]{3,2,1,0:T(8,128)(2,1)}, bf16[4,3,32,512]{3,2,1,0:T(8,128)(2,1)S(1)}, u32[]{:S(2)}, u32[]{:S(2)}) %collective-permute-start.38) | collective-permute-done | bytes 393248 | tf_op jit(solution)/shard_map/ppermute | solution.py:14
  34.1 3.8 %collective-permute-start.40 = (bf16[3,32,512]{2,1,0:T(8,128)(2,1)S(1)}, bf16[3,32,512]{2,1,0:T(8,128)(2,1)S(1)}, u32[]{:S(2)}, u32[]{:S(2)}) collective-permute-start(bf16[3,32,512]{2,1,0:T(8,128)(2,1)S(1)} %get-tuple-element.54), channel_id=1, source_target_pairs={{0,8},{8,16},{32,40},{40,48},{64,72},{72,80},{96,104},{104,112},{1... | collective-permute-start | bytes 294920 | tf_op jit(solution)/shard_map/ppermute | solution.py:14
  47.6 3.0 %collective-permute-done.34 = bf16[2,3,32,512]{3,2,1,0:T(8,128)(2,1)S(1)} collective-permute-done((bf16[2,3,32,512]{3,2,1,0:T(8,128)(2,1)S(1)}, bf16[2,3,32,512]{3,2,1,0:T(8,128)(2,1)S(1)}, u32[]{:S(2)}, u32[]{:S(2)}) %collective-permute-start.34) | collective-permute-done | bytes 196640 | tf_op jit(solution)/shard_map/ppermute | solution.py:14
  57.6 3.4 %collective-permute-start.1 = (bf16[3,64,512]{2,1,0:T(8,128)(2,1)}, bf16[3,64,512]{2,1,0:T(8,128)(2,1)S(1)}, u32[]{:S(2)}, u32[]{:S(2)}) collective-permute-start(bf16[3,64,512]{2,1,0:T(8,128)(2,1)} %get-tuple-element.26), channel_id=1, source_target_pairs={{0,2},{1,3},{8,10},{9,11},{16,18},{17,19},{24,26},{25,27},{32,34},... | collective-permute-start | bytes 589832 | tf_op jit(solution)/shard_map/ppermute | solution.py:14
  70.8 4.2 %collective-permute-done.3 = bf16[3,64,512]{2,1,0:T(8,128)(2,1)S(1)} collective-permute-done((bf16[3,64,512]{2,1,0:T(8,128)(2,1)}, bf16[3,64,512]{2,1,0:T(8,128)(2,1)S(1)}, u32[]{:S(2)}, u32[]{:S(2)}) %collective-permute-start.3) | collective-permute-done | bytes 196640 | tf_op jit(solution)/shard_map/ppermute | solution.py:14
  77.6 5.5 %collective-permute-start.16 = (bf16[64,512]{1,0:T(8,128)(2,1)S(1)}, bf16[64,512]{1,0:T(8,128)(2,1)S(1)}, u32[]{:S(2)}, u32[]{:S(2)}) collective-permute-start(bf16[64,512]{1,0:T(8,128)(2,1)S(1)} %fusion.11), channel_id=1, source_target_pairs={{0,24},{8,0},{1,25},{9,1},{2,26},{10,2},{3,27},{11,3},{4,28},{12,4... | collective-permute-start | bytes 196616 | tf_op jit(solution)/shard_map/ppermute | solution.py:14
  89.1 7.0 %collective-permute-start.18 = (bf16[2,64,512]{2,1,0:T(8,128)(2,1)S(1)}, bf16[2,64,512]{2,1,0:T(8,128)(2,1)S(1)}, u32[]{:S(2)}, u32[]{:S(2)}) collective-permute-start(bf16[2,64,512]{2,1,0:T(8,128)(2,1)S(1)} %pad_maximum_fusion.2), channel_id=1, source_target_pairs={{0,64},{1,65},{2,66},{3,67},{4,68},{5,69},{6,70},{7,71},{8,72},{9,... | collective-permute-start | bytes 393224 | tf_op jit(solution)/shard_map/ppermute | solution.py:14
  99.4 7.0 %weigh.1 = f32[6,8,512]{2,1,0:T(8,128)} custom-call(f32[8,1536]{1,0:T(8,128)} %copy-done.1, bf16[3,6,512,512]{3,2,1,0:T(8,128)(2,1)} %bitcast.122), custom_call_target="tpu_custom_call" | custom-call | flops 301989888 | bytes 9437184 | tf_op jit(solution)/shard_map/weigh/pallas_call | solution.py:184
  115.4 24.1 %collective-permute-done.21 = bf16[2,64,512]{2,1,0:T(8,128)(2,1)S(1)} collective-permute-done((bf16[2,64,512]{2,1,0:T(8,128)(2,1)S(1)}, bf16[2,64,512]{2,1,0:T(8,128)(2,1)S(1)}, u32[]{:S(2)}, u32[]{:S(2)}) %collective-permute-start.21) | collective-permute-done | bytes 131104 | tf_op jit(solution)/shard_map/ppermute | solution.py:14
  139.6 4.3 %collective-permute-done.22 = bf16[2,64,512]{2,1,0:T(8,128)(2,1)S(1)} collective-permute-done((bf16[2,64,512]{2,1,0:T(8,128)(2,1)S(1)}, bf16[2,64,512]{2,1,0:T(8,128)(2,1)S(1)}, u32[]{:S(2)}, u32[]{:S(2)}) %collective-permute-start.22) | collective-permute-done | bytes 131104 | tf_op jit(solution)/shard_map/ppermute | solution.py:14
  143.9 3.2 %collective-permute-start.23 = (bf16[2,64,512]{2,1,0:T(8,128)(2,1)S(1)}, bf16[2,64,512]{2,1,0:T(8,128)(2,1)S(1)}, u32[]{:S(2)}, u32[]{:S(2)}) collective-permute-start(bf16[2,64,512]{2,1,0:T(8,128)(2,1)S(1)} %select_select_fusion.3), channel_id=1, source_target_pairs={{0,4},{1,5},{2,6},{3,7},{4,0},{5,1},{6,2},{7,3},{8,12},{9,13},{10,... | collective-permute-start | bytes 393224 | tf_op jit(solution)/shard_map/ppermute | solution.py:14
  147.2 4.4 %collective-permute-done.23 = bf16[2,64,512]{2,1,0:T(8,128)(2,1)S(1)} collective-permute-done((bf16[2,64,512]{2,1,0:T(8,128)(2,1)S(1)}, bf16[2,64,512]{2,1,0:T(8,128)(2,1)S(1)}, u32[]{:S(2)}, u32[]{:S(2)}) %collective-permute-start.23) | collective-permute-done | bytes 131104 | tf_op jit(solution)/shard_map/ppermute | solution.py:14
  152.5 6.4 %collective-permute-done.24 = bf16[2,64,512]{2,1,0:T(8,128)(2,1)S(1)} collective-permute-done((bf16[2,64,512]{2,1,0:T(8,128)(2,1)S(1)}, bf16[2,64,512]{2,1,0:T(8,128)(2,1)S(1)}, u32[]{:S(2)}, u32[]{:S(2)}) %collective-permute-start.24) | collective-permute-done | bytes 131104 | tf_op jit(solution)/shard_map/ppermute | solution.py:14
  159.0 6.6 %collective-permute-done.25 = bf16[2,64,512]{2,1,0:T(8,128)(2,1)S(1)} collective-permute-done((bf16[2,64,512]{2,1,0:T(8,128)(2,1)S(1)}, bf16[2,64,512]{2,1,0:T(8,128)(2,1)S(1)}, u32[]{:S(2)}, u32[]{:S(2)}) %collective-permute-start.25) | collective-permute-done | bytes 131104 | tf_op jit(solution)/shard_map/ppermute | solution.py:14
  165.6 5.6 %collective-permute-done.26 = bf16[2,64,512]{2,1,0:T(8,128)(2,1)S(1)} collective-permute-done((bf16[2,64,512]{2,1,0:T(8,128)(2,1)S(1)}, bf16[2,64,512]{2,1,0:T(8,128)(2,1)S(1)}, u32[]{:S(2)}, u32[]{:S(2)}) %collective-permute-start.26) | collective-permute-done | bytes 131104 | tf_op jit(solution)/shard_map/ppermute | solution.py:14
  172.4 8.6 %collective-permute-done.7 = bf16[2,3,64,512]{3,2,1,0:T(8,128)(2,1)S(1)} collective-permute-done((bf16[2,3,64,512]{3,2,1,0:T(8,128)(2,1)S(1)}, bf16[2,3,64,512]{3,2,1,0:T(8,128)(2,1)S(1)}, u32[]{:S(2)}, u32[]{:S(2)}) %collective-permute-start.7) | collective-permute-done | bytes 393248 | tf_op jit(solution)/shard_map/ppermute | solution.py:14
  181.0 10.6 %collective-permute-done.9 = bf16[2,3,64,512]{3,2,1,0:T(8,128)(2,1)S(1)} collective-permute-done((bf16[2,3,64,512]{3,2,1,0:T(8,128)(2,1)S(1)}, bf16[2,3,64,512]{3,2,1,0:T(8,128)(2,1)S(1)}, u32[]{:S(2)}, u32[]{:S(2)}) %collective-permute-start.9) | collective-permute-done | bytes 393248 | tf_op jit(solution)/shard_map/ppermute | solution.py:14
  193.5 10.9 %left.1 = (bf16[3,8,64,512]{3,2,1,0:T(8,128)(2,1)}, bf16[3,8,64,512]{3,2,1,0:T(8,128)(2,1)}, f32[2,8,512]{2,1,0:T(8,128)}) custom-call(s32[3]{0:T(128)} %pad_add_fusion.info_ref, bf16[8,2,3,64,512]{4,3,2,1,0:T(8,128)(2,1)} %copy-done.3, bf16[512,512]{1,0:T(8,128)(2,1)} %bitcast.130, bf16[2,512,512]{2,1,0:T(8,128)(2,1)} %multiplier_ref.1, ...), custom_call_target="tpu_custom_call" | custom-call | flops 2415919104 | bytes 9437184 | tf_op jit(solution)/shard_map/left/pallas_call | solution.py:198
  211.5 3.2 %collective-permute-done.28 = f32[8,512]{1,0:T(8,128)S(1)} collective-permute-done((f32[8,512]{1,0:T(8,128)S(1)}, f32[8,512]{1,0:T(8,128)S(1)}, u32[]{:S(2)}, u32[]{:S(2)}) %collective-permute-start.28) | collective-permute-done | bytes 16416 | tf_op jit(solution)/shard_map/ppermute | solution.py:225
  218.7 5.2 %collective-permute-done.30 = f32[8,512]{1,0:T(8,128)S(1)} collective-permute-done((f32[8,512]{1,0:T(8,128)S(1)}, f32[8,512]{1,0:T(8,128)S(1)}, u32[]{:S(2)}, u32[]{:S(2)}) %collective-permute-start.30) | collective-permute-done | bytes 16416 | tf_op jit(solution)/shard_map/ppermute | solution.py:225
  225.2 20.3 %trail.1 = (bf16[3,6,512,512]{3,2,1,0:T(8,128)(2,1)}, f32[6,8,512]{2,1,0:T(8,128)}) custom-call(s32[3]{0:T(128)} %pad_add_fusion.info_ref, bf16[1536,512]{1,0:T(8,128)(2,1)} %bitcast.140, bf16[1536,512]{1,0:T(8,128)(2,1)} %bitcast.141, bf16[512,512]{1,0:T(8,128)(2,1)} %convolution_convert_fusion.second_ref, f32[2,8,512]{2,1,0:T(8,128)} %slice.62.sums_ref, ...), custom_call_target="tpu_custom_call" | custom-call | flops 12079595520 | bytes 18874368 | tf_op jit(solution)/shard_map/trail/pallas_call | solution.py:229
  (148 shorter events, 75.1 us)
Async XLA Ops:
  7.2 218.0 %all-gather.3.cloned.1.call-start = ((), (), s32[]{:S(2)}) async-start(), calls=%async_computation | async-start | bytes 6684672 | tf_op jit(solution)/shard_map/all_gather | solution.py:167
  12.1 13.4 %collective-permute-start.37 = (bf16[4,3,32,512]{3,2,1,0:T(8,128)(2,1)}, bf16[4,3,32,512]{3,2,1,0:T(8,128)(2,1)S(1)}, u32[]{:S(2)}, u32[]{:S(2)}) collective-permute-start(bf16[4,3,32,512]{3,2,1,0:T(8,128)(2,1)} %get-tuple-element.40), channel_id=1, source_target_pairs={{0,32},{8,40},{1,33},{9,41},{2,34},{10,42},{3,35},{11,43},{4,36},{... | collective-permute-start | bytes 1179656 | tf_op jit(solution)/shard_map/ppermute | solution.py:14
  15.8 17.1 %collective-permute-start.38 = (bf16[4,3,32,512]{3,2,1,0:T(8,128)(2,1)}, bf16[4,3,32,512]{3,2,1,0:T(8,128)(2,1)S(1)}, u32[]{:S(2)}, u32[]{:S(2)}) collective-permute-start(bf16[4,3,32,512]{3,2,1,0:T(8,128)(2,1)} %get-tuple-element.41), channel_id=1, source_target_pairs={{0,64},{8,72},{1,65},{9,73},{2,66},{10,74},{3,67},{11,75},{4,68},{... | collective-permute-start | bytes 1179656 | tf_op jit(solution)/shard_map/ppermute | solution.py:14
  18.1 14.8 %collective-permute-start.39 = (bf16[4,3,32,512]{3,2,1,0:T(8,128)(2,1)}, bf16[4,3,32,512]{3,2,1,0:T(8,128)(2,1)S(1)}, u32[]{:S(2)}, u32[]{:S(2)}) collective-permute-start(bf16[4,3,32,512]{3,2,1,0:T(8,128)(2,1)} %get-tuple-element.42), channel_id=1, source_target_pairs={{0,96},{8,104},{1,97},{9,105},{2,98},{10,106},{3,99},{11,107},{4,1... | collective-permute-start | bytes 1179656 | tf_op jit(solution)/shard_map/ppermute | solution.py:14
  19.4 20.5 %collective-permute-start.31 = (bf16[4,3,32,512]{3,2,1,0:T(8,128)(2,1)}, bf16[4,3,32,512]{3,2,1,0:T(8,128)(2,1)S(1)}, u32[]{:S(2)}, u32[]{:S(2)}) collective-permute-start(bf16[4,3,32,512]{3,2,1,0:T(8,128)(2,1)} %get-tuple-element.36), channel_id=1, source_target_pairs={{0,8},{8,16},{1,9},{9,17},{2,10},{10,18},{3,11},{11,19},{4,12},{12... | collective-permute-start | bytes 1179656 | tf_op jit(solution)/shard_map/ppermute | solution.py:14
  23.2 18.2 %collective-permute-start.32 = (bf16[4,3,32,512]{3,2,1,0:T(8,128)(2,1)}, bf16[4,3,32,512]{3,2,1,0:T(8,128)(2,1)S(1)}, u32[]{:S(2)}, u32[]{:S(2)}) collective-permute-start(bf16[4,3,32,512]{3,2,1,0:T(8,128)(2,1)} %get-tuple-element.37), channel_id=1, source_target_pairs={{0,16},{8,24},{1,17},{9,25},{2,18},{10,26},{3,19},{11,27},{4,20},{... | collective-permute-start | bytes 1179656 | tf_op jit(solution)/shard_map/ppermute | solution.py:14
  25.5 17.4 %collective-permute-start.33 = (bf16[4,3,32,512]{3,2,1,0:T(8,128)(2,1)}, bf16[4,3,32,512]{3,2,1,0:T(8,128)(2,1)S(1)}, u32[]{:S(2)}, u32[]{:S(2)}) collective-permute-start(bf16[4,3,32,512]{3,2,1,0:T(8,128)(2,1)} %get-tuple-element.38), channel_id=1, source_target_pairs={{0,24},{8,0},{1,25},{9,1},{2,26},{10,2},{3,27},{11,3},{4,28},{12,4... | collective-permute-start | bytes 1179656 | tf_op jit(solution)/shard_map/ppermute | solution.py:14
  34.1 11.6 %collective-permute-start.40 = (bf16[3,32,512]{2,1,0:T(8,128)(2,1)S(1)}, bf16[3,32,512]{2,1,0:T(8,128)(2,1)S(1)}, u32[]{:S(2)}, u32[]{:S(2)}) collective-permute-start(bf16[3,32,512]{2,1,0:T(8,128)(2,1)S(1)} %get-tuple-element.54), channel_id=1, source_target_pairs={{0,8},{8,16},{32,40},{40,48},{64,72},{72,80},{96,104},{104,112},{1... | collective-permute-start | bytes 294920 | tf_op jit(solution)/shard_map/ppermute | solution.py:14
  61.0 9.8 %collective-permute-start.2 = (bf16[3,64,512]{2,1,0:T(8,128)(2,1)}, bf16[3,64,512]{2,1,0:T(8,128)(2,1)S(1)}, u32[]{:S(2)}, u32[]{:S(2)}) collective-permute-start(bf16[3,64,512]{2,1,0:T(8,128)(2,1)} %get-tuple-element.27), channel_id=1, source_target_pairs={{0,3},{1,4},{8,11},{9,12},{16,19},{17,20},{24,27},{25,28},{32,35},... | collective-permute-start | bytes 589832 | tf_op jit(solution)/shard_map/ppermute | solution.py:14
  62.4 12.7 %collective-permute-start.3 = (bf16[3,64,512]{2,1,0:T(8,128)(2,1)}, bf16[3,64,512]{2,1,0:T(8,128)(2,1)S(1)}, u32[]{:S(2)}, u32[]{:S(2)}) collective-permute-start(bf16[3,64,512]{2,1,0:T(8,128)(2,1)} %get-tuple-element.28), channel_id=1, source_target_pairs={{0,4},{1,5},{8,12},{9,13},{16,20},{17,21},{24,28},{25,29},{32,36},... | collective-permute-start | bytes 589832 | tf_op jit(solution)/shard_map/ppermute | solution.py:14
  63.9 13.5 %collective-permute-start.4 = (bf16[3,64,512]{2,1,0:T(8,128)(2,1)}, bf16[3,64,512]{2,1,0:T(8,128)(2,1)S(1)}, u32[]{:S(2)}, u32[]{:S(2)}) collective-permute-start(bf16[3,64,512]{2,1,0:T(8,128)(2,1)} %get-tuple-element.29), channel_id=1, source_target_pairs={{0,5},{1,6},{8,13},{9,14},{16,21},{17,22},{24,29},{25,30},{32,37},... | collective-permute-start | bytes 589832 | tf_op jit(solution)/shard_map/ppermute | solution.py:14
  65.3 12.1 %collective-permute-start.5 = (bf16[3,64,512]{2,1,0:T(8,128)(2,1)}, bf16[3,64,512]{2,1,0:T(8,128)(2,1)S(1)}, u32[]{:S(2)}, u32[]{:S(2)}) collective-permute-start(bf16[3,64,512]{2,1,0:T(8,128)(2,1)} %get-tuple-element.30), channel_id=1, source_target_pairs={{0,6},{1,7},{8,14},{9,15},{16,22},{17,23},{24,30},{25,31},{32,38},... | collective-permute-start | bytes 589832 | tf_op jit(solution)/shard_map/ppermute | solution.py:14
  66.6 10.8 %collective-permute-start.6 = (bf16[3,64,512]{2,1,0:T(8,128)(2,1)}, bf16[3,64,512]{2,1,0:T(8,128)(2,1)S(1)}, u32[]{:S(2)}, u32[]{:S(2)}) collective-permute-start(bf16[3,64,512]{2,1,0:T(8,128)(2,1)} %get-tuple-element.31), channel_id=1, source_target_pairs={{0,7},{1,0},{8,15},{9,8},{16,23},{17,16},{24,31},{25,24},{32,39},{... | collective-permute-start | bytes 589832 | tf_op jit(solution)/shard_map/ppermute | solution.py:14
  89.1 19.0 %collective-permute-start.18 = (bf16[2,64,512]{2,1,0:T(8,128)(2,1)S(1)}, bf16[2,64,512]{2,1,0:T(8,128)(2,1)S(1)}, u32[]{:S(2)}, u32[]{:S(2)}) collective-permute-start(bf16[2,64,512]{2,1,0:T(8,128)(2,1)S(1)} %pad_maximum_fusion.2), channel_id=1, source_target_pairs={{0,64},{1,65},{2,66},{3,67},{4,68},{5,69},{6,70},{7,71},{8,72},{9,... | collective-permute-start | bytes 393224 | tf_op jit(solution)/shard_map/ppermute | solution.py:14
  96.2 12.0 %collective-permute-start.19 = (bf16[2,64,512]{2,1,0:T(8,128)(2,1)S(1)}, bf16[2,64,512]{2,1,0:T(8,128)(2,1)S(1)}, u32[]{:S(2)}, u32[]{:S(2)}) collective-permute-start(bf16[2,64,512]{2,1,0:T(8,128)(2,1)S(1)} %pad_maximum_fusion.2), channel_id=1, source_target_pairs={{0,96},{1,97},{2,98},{3,99},{4,100},{5,101},{6,102},{7,103},{8,104... | collective-permute-start | bytes 393224 | tf_op jit(solution)/shard_map/ppermute | solution.py:14
  97.5 10.7 %collective-permute-start.17 = (bf16[2,64,512]{2,1,0:T(8,128)(2,1)S(1)}, bf16[2,64,512]{2,1,0:T(8,128)(2,1)S(1)}, u32[]{:S(2)}, u32[]{:S(2)}) collective-permute-start(bf16[2,64,512]{2,1,0:T(8,128)(2,1)S(1)} %pad_maximum_fusion.2), channel_id=1, source_target_pairs={{0,32},{1,33},{2,34},{3,35},{4,36},{5,37},{6,38},{7,39},{8,40},{9,... | collective-permute-start | bytes 393224 | tf_op jit(solution)/shard_map/ppermute | solution.py:14
  108.3 83.5 %collective-permute-start.12 = (bf16[2,3,64,512]{3,2,1,0:T(8,128)(2,1)S(1)}, bf16[2,3,64,512]{3,2,1,0:T(8,128)(2,1)S(1)}, u32[]{:S(2)}, u32[]{:S(2)}) collective-permute-start(bf16[2,3,64,512]{3,2,1,0:T(8,128)(2,1)S(1)} %pad_maximum_fusion), channel_id=1, source_target_pairs={{0,6},{1,7},{2,0},{3,1},{4,2},{5,3},{6,4},{7,5},{8,14},{9,15},{10,... | collective-permute-start | bytes 1179656 | tf_op jit(solution)/shard_map/ppermute | solution.py:14
  109.5 82.2 %collective-permute-start.11 = (bf16[2,3,64,512]{3,2,1,0:T(8,128)(2,1)S(1)}, bf16[2,3,64,512]{3,2,1,0:T(8,128)(2,1)S(1)}, u32[]{:S(2)}, u32[]{:S(2)}) collective-permute-start(bf16[2,3,64,512]{3,2,1,0:T(8,128)(2,1)S(1)} %pad_maximum_fusion), channel_id=1, source_target_pairs={{0,5},{1,6},{2,7},{3,0},{4,1},{5,2},{6,3},{7,4},{8,13},{9,14},{10,... | collective-permute-start | bytes 1179656 | tf_op jit(solution)/shard_map/ppermute | solution.py:14
  109.5 82.1 %collective-permute-start.10 = (bf16[2,3,64,512]{3,2,1,0:T(8,128)(2,1)S(1)}, bf16[2,3,64,512]{3,2,1,0:T(8,128)(2,1)S(1)}, u32[]{:S(2)}, u32[]{:S(2)}) collective-permute-start(bf16[2,3,64,512]{3,2,1,0:T(8,128)(2,1)S(1)} %pad_maximum_fusion), channel_id=1, source_target_pairs={{0,4},{1,5},{2,6},{3,7},{4,0},{5,1},{6,2},{7,3},{8,12},{9,13},{10,... | collective-permute-start | bytes 1179656 | tf_op jit(solution)/shard_map/ppermute | solution.py:14
  112.0 68.9 %collective-permute-start.8 = (bf16[2,3,64,512]{3,2,1,0:T(8,128)(2,1)S(1)}, bf16[2,3,64,512]{3,2,1,0:T(8,128)(2,1)S(1)}, u32[]{:S(2)}, u32[]{:S(2)}) collective-permute-start(bf16[2,3,64,512]{3,2,1,0:T(8,128)(2,1)S(1)} %pad_maximum_fusion), channel_id=1, source_target_pairs={{0,2},{1,3},{2,4},{3,5},{4,6},{5,7},{6,0},{7,1},{8,10},{9,11},{10,... | collective-permute-start | bytes 1179656 | tf_op jit(solution)/shard_map/ppermute | solution.py:14
  113.7 25.8 %collective-permute-start.21 = (bf16[2,64,512]{2,1,0:T(8,128)(2,1)S(1)}, bf16[2,64,512]{2,1,0:T(8,128)(2,1)S(1)}, u32[]{:S(2)}, u32[]{:S(2)}) collective-permute-start(bf16[2,64,512]{2,1,0:T(8,128)(2,1)S(1)} %select_select_fusion.3), channel_id=1, source_target_pairs={{0,6},{1,7},{2,0},{3,1},{4,2},{5,3},{6,4},{7,5},{8,14},{9,15},{10,... | collective-permute-start | bytes 393224 | tf_op jit(solution)/shard_map/ppermute | solution.py:14
  171.2 9.7 %collective-permute-start.7 = (bf16[2,3,64,512]{3,2,1,0:T(8,128)(2,1)S(1)}, bf16[2,3,64,512]{3,2,1,0:T(8,128)(2,1)S(1)}, u32[]{:S(2)}, u32[]{:S(2)}) collective-permute-start(bf16[2,3,64,512]{3,2,1,0:T(8,128)(2,1)S(1)} %pad_maximum_fusion), channel_id=1, source_target_pairs={{0,1},{1,2},{2,3},{3,4},{4,5},{5,6},{6,7},{7,0},{8,9},{9,10},{10,1... | collective-permute-start | bytes 1179656 | tf_op jit(solution)/shard_map/ppermute | solution.py:14
  180.9 10.7 %collective-permute-start.9 = (bf16[2,3,64,512]{3,2,1,0:T(8,128)(2,1)S(1)}, bf16[2,3,64,512]{3,2,1,0:T(8,128)(2,1)S(1)}, u32[]{:S(2)}, u32[]{:S(2)}) collective-permute-start(bf16[2,3,64,512]{3,2,1,0:T(8,128)(2,1)S(1)} %pad_maximum_fusion), channel_id=1, source_target_pairs={{0,3},{1,4},{2,5},{3,6},{4,7},{5,0},{6,1},{7,2},{8,11},{9,12},{10,... | collective-permute-start | bytes 1179656 | tf_op jit(solution)/shard_map/ppermute | solution.py:14
  181.0 10.8 %collective-permute-start.13 = (bf16[2,3,64,512]{3,2,1,0:T(8,128)(2,1)S(1)}, bf16[2,3,64,512]{3,2,1,0:T(8,128)(2,1)S(1)}, u32[]{:S(2)}, u32[]{:S(2)}) collective-permute-start(bf16[2,3,64,512]{3,2,1,0:T(8,128)(2,1)S(1)} %pad_maximum_fusion), channel_id=1, source_target_pairs={{0,7},{1,0},{2,1},{3,2},{4,3},{5,4},{6,5},{7,6},{8,15},{9,8},{10,9... | collective-permute-start | bytes 1179656 | tf_op jit(solution)/shard_map/ppermute | solution.py:14
  (26 other events, 205.4 us)
Sparse Core Ops, SparseCore 0:
  53.7 66.3 all-gather.2
where the time goes:
time: 256 us; the launch traced here: 254 us
  waiting for transfers between devices  105 us (41%)
  starting transfers between devices  75.2 us (29%)
  Pallas kernels  45.1 us (18%)
  between operations  14.8 us (6%)
  local copies, waits for them, and re-layouts  9.7 us (4%)
  other arithmetic  3.16 us (1%)
    ppermute x39, waiting for transfers between devices, shifts(): lax.ppermute(p, axis, pairs(s))  94.6 us
    ppermute x39, starting transfers between devices, shifts(): lax.ppermute(p, axis, pairs(s))  68.4 us
    pallas_call x1, Pallas kernels, eliminate(): pl.pallas_call(trail_kernel, out_shape=(jax.ShapeDtypeStruct(tiles.shape,...  20.3 us
    pallas_call x1, Pallas kernels, eliminate(): pl.pallas_call(left_kernel, out_shape=(left_shape, left_shape, jax.ShapeD...  10.9 us
    ppermute x4, waiting for transfers between devices, eliminate(): lax.ppermute(total, ROW, [(i, i ^ mask) for i in range(grid_rows)])  10.6 us
    pallas_call x1, Pallas kernels, eliminate(): pl.pallas_call(weigh_kernel, out_shape=jax.ShapeDtypeStruct((cols, 8, blo...  6.97 us
    ppermute x4, starting transfers between devices, eliminate(): lax.ppermute(total, ROW, [(i, i ^ mask) for i in range(grid_rows)])  6.72 us
  transfers between devices with their start and end apart: 44, of which 23 were waited for; matrix products, arithmetic and copies ran while one was open for 3% of the time, Pallas kernels for 8%

commit v1 on v0

--- a/solution.py
+++ b/solution.py
@@ -1,3 +1,5 @@
+import functools
+
 import jax
 import jax.numpy as jnp
 from jax import lax
@@ -51,32 +53,26 @@
 
 
 def left_kernel(info_ref, panel_ref, corner_ref, multiplier_ref, weight_ref, left0_ref, left1_ref, sum_ref):
-    step = pl.program_id(0)
-    _, _, block_rows, piece, width = panel_ref.shape
-    share = block_rows * piece
-    row = lax.broadcasted_iota(jnp.int32, (share, width), 0)
-    my_row = info_ref[1]
-
-    def keep(value, pivot):
-        return jnp.where((row < piece) & (my_row <= pivot), jnp.zeros_like(value), value)
-
-    column0 = panel_ref[0, 0].reshape(share, width)
-    column1 = panel_ref[0, 1].reshape(share, width)
-    left0 = jnp.dot(column0, multiplier_ref[0], preferred_element_type=F32)
-    left0 = keep(left0, 0).astype(BF16)
-    column = jnp.dot(left0, corner_ref[...], preferred_element_type=F32)
-    column = (column1.astype(F32) - column).astype(BF16)
-    left1 = jnp.dot(column, multiplier_ref[1], preferred_element_type=F32)
-    left1 = keep(left1, 1).astype(BF16)
-    left0_ref[:, 0] = left0.reshape(block_rows, piece, width)
-    left1_ref[:, 0] = left1.reshape(block_rows, piece, width)
-
-    @pl.when(step == 0)
-    def _():
-        sum_ref[...] = jnp.zeros_like(sum_ref)
-
-    sum_ref[0] += times_rows(weight_ref[0], left0)
-    sum_ref[1] += times_rows(weight_ref[0], left1)
+    block_rows, width = left0_ref.shape[0] // corner_ref.shape[0], corner_ref.shape[0]
+    strips, _, _, _, _ = panel_ref.shape
+
+    def column(step):
+        parts = [panel_ref[j, step, a] for a in range(block_rows) for j in range(strips)]
+        return jnp.concatenate(parts, axis=0)
+
+    def finish(step, factor, left_ref):
+        left = jnp.dot(factor, multiplier_ref[step], preferred_element_type=F32).astype(BF16)
+        left_ref[...] = left
+
+        @pl.when(info_ref[1] <= step)
+        def _():
+            left_ref[:width] = jnp.zeros((width, width), BF16)
+
+        sum_ref[step] = times_rows(weight_ref[...], left_ref[...])
+
+    finish(0, column(0), left0_ref)
+    update = jnp.dot(left0_ref[...], corner_ref[...], preferred_element_type=F32)
+    finish(1, (column(1).astype(F32) - update).astype(BF16), left1_ref)
 
 
 def trail_kernel(
@@ -93,16 +89,17 @@
     check_ref[0] = base_ref[0] - times_rows(sums_ref[0], upper0) - times_rows(sums_ref[1], upper1)
     for a in range(tile_ref.shape[0]):
         rows = slice(a * width, (a + 1) * width)
-        product = jnp.dot(left0_ref[rows, :], upper0, preferred_element_type=F32)
-        tile = (tile_ref[a, 0].astype(F32) - product).astype(BF16)
-        product = jnp.dot(left1_ref[rows, :], upper1, preferred_element_type=F32)
-        out_ref[a, 0] = (tile.astype(F32) - product).astype(BF16)
+        tile = tile_ref[a, 0].astype(F32) - jnp.dot(left0_ref[rows, :], upper0, preferred_element_type=F32)
+        tile = tile.astype(BF16).astype(F32)
+        tile = tile - jnp.dot(left1_ref[rows, :], upper1, preferred_element_type=F32)
+        out_ref[a, 0] = tile.astype(BF16)
+    for a in range(tile_ref.shape[0]):
         for pivot, left_ref in enumerate((left0_ref, left1_ref)):
             below = True if a > 0 else my_row > pivot
 
             @pl.when(first & (my_col == pivot) & below)
             def _():
-                out_ref[a, 0] = left_ref[rows, :]
+                out_ref[a, 0] = left_ref[a * width : (a + 1) * width, :]
 
 
 def eliminate(matrix, multiplier, checksum_weight):
@@ -111,7 +108,7 @@
     my_row, my_col = lax.axis_index(ROW), lax.axis_index("col")
     info = jnp.stack([my_col, my_row, lax.axis_index("row_1")]).astype(jnp.int32)
     tiles = matrix.transpose(0, 2, 1, 3)
-    rows, piece, share = block_rows * block, block // grid_rows, block_rows * block // grid_cols
+    rows, piece = block_rows * block, block // grid_rows
     weights = jnp.pad(checksum_weight.reshape(1, rows), ((0, 7), (0, 0)))
     smem = pl.BlockSpec(memory_space=pltpu.SMEM)
     column_of_tiles = pl.BlockSpec((block_rows, 1, block, block), lambda c: (0, c, 0, 0))
@@ -119,6 +116,22 @@
 
     half, sides = cols // 2, lax.axis_size("row_1")
     my_y, my_z = lax.axis_index("row_0"), lax.axis_index("row_1")
+
+    strip = block // grid_cols
+    deep = tiles.reshape(block_rows, cols, grid_cols, strip, block)
+    cell = jax.ShapeDtypeStruct((block_rows, strip, block), BF16)
+    cells = pl.pallas_call(
+        panels_kernel,
+        out_shape=(cell,) * grid_cols,
+        grid=(1,),
+        in_specs=[smem, pl.BlockSpec((block_rows, 1, grid_cols, strip, block), lambda j: (0, 0, 0, 0, 0))],
+        out_specs=(pl.BlockSpec((block_rows, strip, block), lambda j: (0, 0, 0)),) * grid_cols,
+        cost_estimate=pl.CostEstimate(flops=rows * block, bytes_accessed=4 * rows * block, transcendentals=0),
+        name="panels",
+    )(info, deep)
+    panels = shifts("col", cells, lambda s: [(0, s), (1, (1 + s) % grid_cols)])
+    panel0, panel1 = from_two(panels, my_col)
+    panels = lax.all_gather(jnp.stack([panel0, panel1]), "col")
 
     tall = tiles.reshape(block_rows * cols, sides, sides, piece, block)
     cell = jax.ShapeDtypeStruct((sides, half, piece, block), BF16)
@@ -138,21 +151,6 @@
     early = shifts(ROW, cells[:sides], lambda s: [(0, s), (1, (1 + s) % sides)])
     late = shifts(ROW, cells[sides:], lambda s: [(0, sides * s), (1, sides * s + 1)])
 
-    strip = block // grid_cols
-    deep = tiles.reshape(block_rows, cols, grid_cols, strip, block)
-    cell = jax.ShapeDtypeStruct((block_rows, strip, block), BF16)
-    cells = pl.pallas_call(
-        panels_kernel,
-        out_shape=(cell,) * grid_cols,
-        grid=(1,),
-        in_specs=[smem, pl.BlockSpec((block_rows, 1, grid_cols, strip, block), lambda j: (0, 0, 0, 0, 0))],
-        out_specs=(pl.BlockSpec((block_rows, strip, block), lambda j: (0, 0, 0)),) * grid_cols,
-        cost_estimate=pl.CostEstimate(flops=rows * block, bytes_accessed=4 * rows * block, transcendentals=0),
-        name="panels",
-    )(info, deep)
-    panels = shifts("col", cells, lambda s: [(0, s), (1, (1 + s) % grid_cols)])
-    panel0, panel1 = from_two(panels, my_col)
-
     early = jnp.stack(from_two(early, my_z), axis=1)
     early = shifts(ROW, list(early), lambda s: [(z, sides * s + z) for z in range(sides)])
     early = lax.select_n(my_y, *early)
@@ -178,9 +176,6 @@
     ordered = lax.dynamic_slice_in_dim(jnp.stack(ordered + ordered[:-1]), grid_cols - 1 - my_col, grid_cols, 0)
     corners = ordered.transpose(1, 0, 2, 3).reshape(2, block, block)
 
-    packed = jnp.stack([panel0, panel1])
-    packed = jnp.stack(shifts("col", [packed] * grid_cols, around))
-
     base = pl.pallas_call(
         weigh_kernel,
         out_shape=jax.ShapeDtypeStruct((cols, 8, block), F32),
@@ -191,38 +186,26 @@
         name="weigh",
     )(weights, tiles)
 
-    strips = weights.reshape(8, block_rows, grid_cols, strip).transpose(2, 0, 1, 3).reshape(grid_cols, 8, share)
-    full = lambda *shape: pl.BlockSpec(shape, lambda j, *_: (0,) * len(shape))
-    shared = pl.BlockSpec((block_rows, 1, strip, block), lambda j, info: (0, j, 0, 0))
-    left_shape = jax.ShapeDtypeStruct((block_rows, grid_cols, strip, block), BF16)
     left0, left1, sums = pl.pallas_call(
         left_kernel,
         out_shape=(
-            left_shape,
-            left_shape,
+            jax.ShapeDtypeStruct((rows, block), BF16),
+            jax.ShapeDtypeStruct((rows, block), BF16),
             jax.ShapeDtypeStruct((2, 8, block), F32),
         ),
-        grid_spec=pltpu.PrefetchScalarGridSpec(
-            num_scalar_prefetch=1,
-            grid=(grid_cols,),
-            in_specs=[
-                pl.BlockSpec((1, 2, block_rows, strip, block), lambda j, info: (lax.rem(info[0] - j + grid_cols, grid_cols), 0, 0, 0, 0)),
-                full(block, block),
-                full(2, block, block),
-                pl.BlockSpec((1, 8, share), lambda j, info: (j, 0, 0)),
-            ],
-            out_specs=(shared, shared, full(2, 8, block)),
-        ),
+        in_specs=[smem] + [pl.BlockSpec(memory_space=pltpu.VMEM)] * 4,
+        out_specs=(pl.BlockSpec(memory_space=pltpu.VMEM),) * 3,
         cost_estimate=pl.CostEstimate(flops=6 * rows * block * block, bytes_accessed=12 * rows * block, transcendentals=0),
+        compiler_params=pltpu.CompilerParams(vmem_limit_bytes=24 << 20),
         name="left",
-    )(info, packed, corners[0], multiplier, strips)
-    left0, left1 = left0.reshape(rows, block), left1.reshape(rows, block)
+    )(info, panels, corners[0], multiplier, weights)
     second_left = jnp.dot(corners[1], multiplier[0], preferred_element_type=F32).astype(BF16)
 
     own = jnp.concatenate([base[:, 0], sums[:, 0]], axis=0)
     total = own
-    for mask in (1, 2, 4, 8):
-        total = total + lax.ppermute(total, ROW, [(i, i ^ mask) for i in range(grid_rows)])
+    for axis in ("row_1", "row_0"):
+        around = lambda s: [(i, (i + s) % sides) for i in range(sides)]
+        total = functools.reduce(jnp.add, shifts(axis, [total] * sides, around))
     pair = jnp.pad(jnp.stack([own, total], axis=1), ((0, 0), (0, 6), (0, 0)))
 
     whole = lambda *shape: pl.BlockSpec(shape, lambda c: (0,) * len(shape))

time: 256 us -> 190 us (0.74)
  waiting for transfers between devices: 105 us -> 48.2 us
  Pallas kernels: 45.1 us -> 36.2 us
    ppermute x39 -> x38, waiting for transfers between devices: 94.6 us -> 48.2 us  [shifts(): lax.ppermute(p, axis, pairs(s))]
    ppermute x4 -> x0, waiting for transfers between devices: 10.6 us -> none  [eliminate(): lax.ppermute(total, ROW, [(i, i ^ mask) for i in range(grid_rows)])]
    pallas_call x1, Pallas kernels: 10.9 us -> 3.97 us  [eliminate(): pl.pallas_call(left_kernel, out_shape=(jax.ShapeDtypeStruct((rows, block)...]
    ppermute x4 -> x0, starting transfers between devices: 6.72 us -> none  [eliminate(): lax.ppermute(total, ROW, [(i, i ^ mask) for i in range(grid_rows)])]
    ppermute x39 -> x38, starting transfers between devices: 68.4 us -> 73.1 us  [shifts(): lax.ppermute(p, axis, pairs(s))]
  transfers between devices with their start and end apart: 44 -> 40, of which waited for: 23 -> 20; matrix products, arithmetic and copies ran while one was open for 3% -> 4% of each run, Pallas kernels for 8% -> 8%
where the time goes in v1:
time: 190 us; the launch traced here: 187 us
  starting transfers between devices  73.2 us (39%)
  waiting for transfers between devices  48.2 us (25%)
  Pallas kernels  36.2 us (19%)
  between operations  14.8 us (8%)
  local copies, waits for them, and re-layouts  9.62 us (5%)
  other arithmetic  3.93 us (2%)
    ppermute x38, starting transfers between devices, shifts(): lax.ppermute(p, axis, pairs(s))  73.1 us
    ppermute x38, waiting for transfers between devices, shifts(): lax.ppermute(p, axis, pairs(s))  48.2 us
    pallas_call x1, Pallas kernels, eliminate(): pl.pallas_call(trail_kernel, out_shape=(jax.ShapeDtypeStruct(tiles.shape,...  18.4 us
    pallas_call x1, Pallas kernels, eliminate(): pl.pallas_call(weigh_kernel, out_shape=jax.ShapeDtypeStruct((cols, 8, blo...  6.8 us
    unnamed x35, local copies, waits for them, and re-layouts  4.99 us
    pallas_call x1, Pallas kernels, eliminate(): pl.pallas_call(bands_kernel, out_shape=(cell,) * (2 * sides), grid=(half,...  4.4 us
    pallas_call x1, Pallas kernels, eliminate(): pl.pallas_call(left_kernel, out_shape=(jax.ShapeDtypeStruct((rows, block)...  3.97 us
  transfers between devices with their start and end apart: 40, of which 20 were waited for; matrix products, arithmetic and copies ran while one was open for 4% of the time, Pallas kernels for 8%

profile of v1, /device:TPU:0, one launch (start us, length us, event | category | flops | bytes accessed | tf_op | source)
XLA Modules:
  0.0 187.1 jit_solution(14197954442063827981)
XLA Ops:
  7.8 2.7 %panels.1 = (bf16[3,64,512]{2,1,0:T(8,128)(2,1)}, bf16[3,64,512]{2,1,0:T(8,128)(2,1)}, bf16[3,64,512]{2,1,0:T(8,128)(2,1)}, bf16[3,64,512]{2,1,0:T(8,128)(2,1)},...) custom-call(s32[3]{0:T(128)} %pad_add_fusion.info_ref, ...), custom_call_target="tpu_custom_call" | custom-call | flops 786432 | bytes 3145728 | tf_op jit(solution)/shard_map/panels/pallas_call | solution.py:123
  11.9 3.5 %collective-permute-start.1 = (bf16[3,64,512]{2,1,0:T(8,128)(2,1)}, bf16[3,64,512]{2,1,0:T(8,128)(2,1)S(1)}, u32[]{:S(2)}, u32[]{:S(2)}) collective-permute-start(bf16[3,64,512]{2,1,0:T(8,128)(2,1)} %get-tuple-element.26), channel_id=1, source_target_pairs={{0,2},{1,3},{8,10},{9,11},{16,18},{17,19},{24,26},{25,27},{32,34},... | collective-permute-start | bytes 589832 | tf_op jit(solution)/shard_map/ppermute | solution.py:16
  25.2 4.2 %collective-permute-done.3 = bf16[3,64,512]{2,1,0:T(8,128)(2,1)S(1)} collective-permute-done((bf16[3,64,512]{2,1,0:T(8,128)(2,1)}, bf16[3,64,512]{2,1,0:T(8,128)(2,1)S(1)}, u32[]{:S(2)}, u32[]{:S(2)}) %collective-permute-start.3) | collective-permute-done | bytes 196640 | tf_op jit(solution)/shard_map/ppermute | solution.py:16
  29.4 2.3 %collective-permute-done.4 = bf16[3,64,512]{2,1,0:T(8,128)(2,1)S(1)} collective-permute-done((bf16[3,64,512]{2,1,0:T(8,128)(2,1)}, bf16[3,64,512]{2,1,0:T(8,128)(2,1)S(1)}, u32[]{:S(2)}, u32[]{:S(2)}) %collective-permute-start.4) | collective-permute-done | bytes 196640 | tf_op jit(solution)/shard_map/ppermute | solution.py:16
  32.8 4.4 %bands.1 = (bf16[4,3,32,512]{3,2,1,0:T(8,128)(2,1)}, bf16[4,3,32,512]{3,2,1,0:T(8,128)(2,1)}, bf16[4,3,32,512]{3,2,1,0:T(8,128)(2,1)}, bf16[4,3,32,512]{3,2,1,0:...) custom-call(s32[3]{0:T(128)} %pad_add_fusion.info_ref, ...), custom_call_target="tpu_custom_call" | custom-call | flops 1572864 | bytes 6291456 | tf_op jit(solution)/shard_map/bands/pallas_call | solution.py:138
  37.2 3.5 %collective-permute-start.32 = (bf16[4,3,32,512]{3,2,1,0:T(8,128)(2,1)}, bf16[4,3,32,512]{3,2,1,0:T(8,128)(2,1)S(1)}, u32[]{:S(2)}, u32[]{:S(2)}) collective-permute-start(bf16[4,3,32,512]{3,2,1,0:T(8,128)(2,1)} %get-tuple-element.40), channel_id=1, source_target_pairs={{0,32},{8,40},{1,33},{9,41},{2,34},{10,42},{3,35},{11,43},{4,36},{... | collective-permute-start | bytes 1179656 | tf_op jit(solution)/shard_map/ppermute | solution.py:16
  44.4 3.8 %collective-permute-start.26 = (bf16[4,3,32,512]{3,2,1,0:T(8,128)(2,1)}, bf16[4,3,32,512]{3,2,1,0:T(8,128)(2,1)S(1)}, u32[]{:S(2)}, u32[]{:S(2)}) collective-permute-start(bf16[4,3,32,512]{3,2,1,0:T(8,128)(2,1)} %get-tuple-element.36), channel_id=1, source_target_pairs={{0,8},{8,16},{1,9},{9,17},{2,10},{10,18},{3,11},{11,19},{4,12},{12... | collective-permute-start | bytes 1179656 | tf_op jit(solution)/shard_map/ppermute | solution.py:16
  52.4 4.7 %collective-permute-done.33 = bf16[4,3,32,512]{3,2,1,0:T(8,128)(2,1)S(1)} collective-permute-done((bf16[4,3,32,512]{3,2,1,0:T(8,128)(2,1)}, bf16[4,3,32,512]{3,2,1,0:T(8,128)(2,1)S(1)}, u32[]{:S(2)}, u32[]{:S(2)}) %collective-permute-start.33) | collective-permute-done | bytes 393248 | tf_op jit(solution)/shard_map/ppermute | solution.py:16
  58.4 3.8 %collective-permute-start.35 = (bf16[3,32,512]{2,1,0:T(8,128)(2,1)S(1)}, bf16[3,32,512]{2,1,0:T(8,128)(2,1)S(1)}, u32[]{:S(2)}, u32[]{:S(2)}) collective-permute-start(bf16[3,32,512]{2,1,0:T(8,128)(2,1)S(1)} %get-tuple-element.54), channel_id=1, source_target_pairs={{0,8},{8,16},{32,40},{40,48},{64,72},{72,80},{96,104},{104,112},{1... | collective-permute-start | bytes 294920 | tf_op jit(solution)/shard_map/ppermute | solution.py:16
  72.5 2.3 %collective-permute-done.29 = bf16[2,3,32,512]{3,2,1,0:T(8,128)(2,1)S(1)} collective-permute-done((bf16[2,3,32,512]{3,2,1,0:T(8,128)(2,1)S(1)}, bf16[2,3,32,512]{3,2,1,0:T(8,128)(2,1)S(1)}, u32[]{:S(2)}, u32[]{:S(2)}) %collective-permute-start.29) | collective-permute-done | bytes 196640 | tf_op jit(solution)/shard_map/ppermute | solution.py:16
  77.9 5.5 %collective-permute-start.9 = (bf16[64,512]{1,0:T(8,128)(2,1)S(1)}, bf16[64,512]{1,0:T(8,128)(2,1)S(1)}, u32[]{:S(2)}, u32[]{:S(2)}) collective-permute-start(bf16[64,512]{1,0:T(8,128)(2,1)S(1)} %fusion.11), channel_id=1, source_target_pairs={{0,24},{8,0},{1,25},{9,1},{2,26},{10,2},{3,27},{11,3},{4,28},{12,4... | collective-permute-start | bytes 196616 | tf_op jit(solution)/shard_map/ppermute | solution.py:16
  84.7 2.8 %collective-permute-start.7 = (bf16[64,512]{1,0:T(8,128)(2,1)S(1)}, bf16[64,512]{1,0:T(8,128)(2,1)S(1)}, u32[]{:S(2)}, u32[]{:S(2)}) collective-permute-start(bf16[64,512]{1,0:T(8,128)(2,1)S(1)} %fusion.11), channel_id=1, source_target_pairs={{0,8},{8,16},{1,9},{9,17},{2,10},{10,18},{3,11},{11,19},{4,12},{12... | collective-permute-start | bytes 196616 | tf_op jit(solution)/shard_map/ppermute | solution.py:16
  89.4 5.9 %collective-permute-start.11 = (bf16[2,64,512]{2,1,0:T(8,128)(2,1)S(1)}, bf16[2,64,512]{2,1,0:T(8,128)(2,1)S(1)}, u32[]{:S(2)}, u32[]{:S(2)}) collective-permute-start(bf16[2,64,512]{2,1,0:T(8,128)(2,1)S(1)} %pad_maximum_fusion.2), channel_id=1, source_target_pairs={{0,64},{1,65},{2,66},{3,67},{4,68},{5,69},{6,70},{7,71},{8,72},{9,... | collective-permute-start | bytes 393224 | tf_op jit(solution)/shard_map/ppermute | solution.py:16
  97.9 3.4 %collective-permute-done.11 = bf16[2,64,512]{2,1,0:T(8,128)(2,1)S(1)} collective-permute-done((bf16[2,64,512]{2,1,0:T(8,128)(2,1)S(1)}, bf16[2,64,512]{2,1,0:T(8,128)(2,1)S(1)}, u32[]{:S(2)}, u32[]{:S(2)}) %collective-permute-start.11) | collective-permute-done | bytes 131104 | tf_op jit(solution)/shard_map/ppermute | solution.py:16
  101.2 3.0 %collective-permute-done.10 = bf16[2,64,512]{2,1,0:T(8,128)(2,1)S(1)} collective-permute-done((bf16[2,64,512]{2,1,0:T(8,128)(2,1)S(1)}, bf16[2,64,512]{2,1,0:T(8,128)(2,1)S(1)}, u32[]{:S(2)}, u32[]{:S(2)}) %collective-permute-start.10) | collective-permute-done | bytes 131104 | tf_op jit(solution)/shard_map/ppermute | solution.py:16
  105.0 6.8 %weigh.1 = f32[6,8,512]{2,1,0:T(8,128)} custom-call(f32[8,1536]{1,0:T(8,128)} %pad.8.weight_ref, bf16[3,6,512,512]{3,2,1,0:T(8,128)(2,1)} %bitcast.103), custom_call_target="tpu_custom_call" | custom-call | flops 301989888 | bytes 9437184 | tf_op jit(solution)/shard_map/weigh/pallas_call | solution.py:179
  113.2 3.0 %collective-permute-start.17 = (bf16[2,64,512]{2,1,0:T(8,128)(2,1)S(1)}, bf16[2,64,512]{2,1,0:T(8,128)(2,1)S(1)}, u32[]{:S(2)}, u32[]{:S(2)}) collective-permute-start(bf16[2,64,512]{2,1,0:T(8,128)(2,1)S(1)} %select_select_fusion.3), channel_id=1, source_target_pairs={{0,3},{1,4},{2,5},{3,6},{4,7},{5,0},{6,1},{7,2},{8,11},{9,12},{10,... | collective-permute-start | bytes 393224 | tf_op jit(solution)/shard_map/ppermute | solution.py:16
  119.5 7.2 %collective-permute-done.14 = bf16[2,64,512]{2,1,0:T(8,128)(2,1)S(1)} collective-permute-done((bf16[2,64,512]{2,1,0:T(8,128)(2,1)S(1)}, bf16[2,64,512]{2,1,0:T(8,128)(2,1)S(1)}, u32[]{:S(2)}, u32[]{:S(2)}) %collective-permute-start.14) | collective-permute-done | bytes 131104 | tf_op jit(solution)/shard_map/ppermute | solution.py:16
  128.8 2.5 %collective-permute-done.15 = bf16[2,64,512]{2,1,0:T(8,128)(2,1)S(1)} collective-permute-done((bf16[2,64,512]{2,1,0:T(8,128)(2,1)S(1)}, bf16[2,64,512]{2,1,0:T(8,128)(2,1)S(1)}, u32[]{:S(2)}, u32[]{:S(2)}) %collective-permute-start.15) | collective-permute-done | bytes 131104 | tf_op jit(solution)/shard_map/ppermute | solution.py:16
  134.8 4.0 %left.1 = (bf16[1536,512]{1,0:T(8,128)(2,1)S(1)}, bf16[1536,512]{1,0:T(8,128)(2,1)S(1)}, f32[2,8,512]{2,1,0:T(8,128)S(1)}) custom-call(s32[3]{0:T(128)S(1)} %copy-done.1, bf16[8,2,3,64,512]{4,3,2,1,0:T(8,128)(2,1)S(1)} %bitcast.99, bf16[512,512]{1,0:T(8,128)(2,1)S(1)} %bitcast.98, bf16[2,512,512]{2,1,0:T(8,128)(2,1)S(1)} %copy-done.3, f32[8,1536]{1,0:T(8,128)S(1)} %copy-done), custom_call_target="tpu_custom_call" | custom-call | flops 2415919104 | bytes 9437184 | tf_op jit(solution)/shard_map/left/pallas_call | solution.py:189
  144.3 2.8 %collective-permute-done.21 = f32[8,512]{1,0:T(8,128)S(1)} collective-permute-done((f32[8,512]{1,0:T(8,128)S(1)}, f32[8,512]{1,0:T(8,128)S(1)}, u32[]{:S(2)}, u32[]{:S(2)}) %collective-permute-start.21) | collective-permute-done | bytes 16416 | tf_op jit(solution)/shard_map/ppermute | solution.py:16
  150.4 3.1 %collective-permute-start.24 = (f32[8,512]{1,0:T(8,128)S(1)}, f32[8,512]{1,0:T(8,128)S(1)}, u32[]{:S(2)}, u32[]{:S(2)}) collective-permute-start(f32[8,512]{1,0:T(8,128)S(1)} %add_add_fusion.1), channel_id=1, source_target_pairs={{0,64},{32,96},{64,0},{96,32},{1,65},{33,97},{65,1},{97,33},{2,66}... | collective-permute-start | bytes 49160 | tf_op jit(solution)/shard_map/ppermute | solution.py:16
  155.6 2.8 %collective-permute-done.23 = f32[8,512]{1,0:T(8,128)S(1)} collective-permute-done((f32[8,512]{1,0:T(8,128)S(1)}, f32[8,512]{1,0:T(8,128)S(1)}, u32[]{:S(2)}, u32[]{:S(2)}) %collective-permute-start.23) | collective-permute-done | bytes 16416 | tf_op jit(solution)/shard_map/ppermute | solution.py:16
  159.8 18.4 %trail.1 = (bf16[3,6,512,512]{3,2,1,0:T(8,128)(2,1)}, f32[6,8,512]{2,1,0:T(8,128)}) custom-call(s32[3]{0:T(128)} %pad_add_fusion.info_ref, bf16[1536,512]{1,0:T(8,128)(2,1)} %copy-done.4, bf16[1536,512]{1,0:T(8,128)(2,1)} %copy-done.5, bf16[512,512]{1,0:T(8,128)(2,1)} %convolution_convert_fusion.second_ref, f32[2,8,512]{2,1,0:T(8,128)} %slice.62.sums_ref, ...), custom_call_target="tpu_custom_call" | custom-call | flops 12079595520 | bytes 18874368 | tf_op jit(solution)/shard_map/trail/pallas_call | solution.py:212
  (133 shorter events, 66.0 us)
Async XLA Ops:
  7.2 124.6 %all-gather.5.cloned.1.call-start = ((), (), s32[]{:S(2)}) async-start(), calls=%async_computation | async-start | bytes 3538944 | tf_op jit(solution)/shard_map/all_gather | solution.py:134
  10.5 9.2 %collective-permute-start = (bf16[3,64,512]{2,1,0:T(8,128)(2,1)}, bf16[3,64,512]{2,1,0:T(8,128)(2,1)S(1)}, u32[]{:S(2)}, u32[]{:S(2)}) collective-permute-start(bf16[3,64,512]{2,1,0:T(8,128)(2,1)} %get-tuple-element.25), channel_id=1, source_target_pairs={{0,1},{1,2},{8,9},{9,10},{16,17},{17,18},{24,25},{25,26},{32,33},{... | collective-permute-start | bytes 589832 | tf_op jit(solution)/shard_map/ppermute | solution.py:16
  15.4 9.8 %collective-permute-start.2 = (bf16[3,64,512]{2,1,0:T(8,128)(2,1)}, bf16[3,64,512]{2,1,0:T(8,128)(2,1)S(1)}, u32[]{:S(2)}, u32[]{:S(2)}) collective-permute-start(bf16[3,64,512]{2,1,0:T(8,128)(2,1)} %get-tuple-element.27), channel_id=1, source_target_pairs={{0,3},{1,4},{8,11},{9,12},{16,19},{17,20},{24,27},{25,28},{32,35},... | collective-permute-start | bytes 589832 | tf_op jit(solution)/shard_map/ppermute | solution.py:16
  16.8 12.7 %collective-permute-start.3 = (bf16[3,64,512]{2,1,0:T(8,128)(2,1)}, bf16[3,64,512]{2,1,0:T(8,128)(2,1)S(1)}, u32[]{:S(2)}, u32[]{:S(2)}) collective-permute-start(bf16[3,64,512]{2,1,0:T(8,128)(2,1)} %get-tuple-element.28), channel_id=1, source_target_pairs={{0,4},{1,5},{8,12},{9,13},{16,20},{17,21},{24,28},{25,29},{32,36},... | collective-permute-start | bytes 589832 | tf_op jit(solution)/shard_map/ppermute | solution.py:16
  18.3 13.5 %collective-permute-start.4 = (bf16[3,64,512]{2,1,0:T(8,128)(2,1)}, bf16[3,64,512]{2,1,0:T(8,128)(2,1)S(1)}, u32[]{:S(2)}, u32[]{:S(2)}) collective-permute-start(bf16[3,64,512]{2,1,0:T(8,128)(2,1)} %get-tuple-element.29), channel_id=1, source_target_pairs={{0,5},{1,6},{8,13},{9,14},{16,21},{17,22},{24,29},{25,30},{32,37},... | collective-permute-start | bytes 589832 | tf_op jit(solution)/shard_map/ppermute | solution.py:16
  19.7 12.1 %collective-permute-start.5 = (bf16[3,64,512]{2,1,0:T(8,128)(2,1)}, bf16[3,64,512]{2,1,0:T(8,128)(2,1)S(1)}, u32[]{:S(2)}, u32[]{:S(2)}) collective-permute-start(bf16[3,64,512]{2,1,0:T(8,128)(2,1)} %get-tuple-element.30), channel_id=1, source_target_pairs={{0,6},{1,7},{8,14},{9,15},{16,22},{17,23},{24,30},{25,31},{32,38},... | collective-permute-start | bytes 589832 | tf_op jit(solution)/shard_map/ppermute | solution.py:16
  21.0 10.8 %collective-permute-start.6 = (bf16[3,64,512]{2,1,0:T(8,128)(2,1)}, bf16[3,64,512]{2,1,0:T(8,128)(2,1)S(1)}, u32[]{:S(2)}, u32[]{:S(2)}) collective-permute-start(bf16[3,64,512]{2,1,0:T(8,128)(2,1)} %get-tuple-element.31), channel_id=1, source_target_pairs={{0,7},{1,0},{8,15},{9,8},{16,23},{17,16},{24,31},{25,24},{32,39},{... | collective-permute-start | bytes 589832 | tf_op jit(solution)/shard_map/ppermute | solution.py:16
  32.8 127.0 %all-gather.7.cloned.1.call-start = ((), (), s32[]{:S(2)}) async-start(), calls=%async_computation.1 | async-start | bytes 6684672 | tf_op jit(solution)/shard_map/all_gather | solution.py:165
  37.2 13.3 %collective-permute-start.32 = (bf16[4,3,32,512]{3,2,1,0:T(8,128)(2,1)}, bf16[4,3,32,512]{3,2,1,0:T(8,128)(2,1)S(1)}, u32[]{:S(2)}, u32[]{:S(2)}) collective-permute-start(bf16[4,3,32,512]{3,2,1,0:T(8,128)(2,1)} %get-tuple-element.40), channel_id=1, source_target_pairs={{0,32},{8,40},{1,33},{9,41},{2,34},{10,42},{3,35},{11,43},{4,36},{... | collective-permute-start | bytes 1179656 | tf_op jit(solution)/shard_map/ppermute | solution.py:16
  40.7 16.4 %collective-permute-start.33 = (bf16[4,3,32,512]{3,2,1,0:T(8,128)(2,1)}, bf16[4,3,32,512]{3,2,1,0:T(8,128)(2,1)S(1)}, u32[]{:S(2)}, u32[]{:S(2)}) collective-permute-start(bf16[4,3,32,512]{3,2,1,0:T(8,128)(2,1)} %get-tuple-element.41), channel_id=1, source_target_pairs={{0,64},{8,72},{1,65},{9,73},{2,66},{10,74},{3,67},{11,75},{4,68},{... | collective-permute-start | bytes 1179656 | tf_op jit(solution)/shard_map/ppermute | solution.py:16
  43.0 14.1 %collective-permute-start.34 = (bf16[4,3,32,512]{3,2,1,0:T(8,128)(2,1)}, bf16[4,3,32,512]{3,2,1,0:T(8,128)(2,1)S(1)}, u32[]{:S(2)}, u32[]{:S(2)}) collective-permute-start(bf16[4,3,32,512]{3,2,1,0:T(8,128)(2,1)} %get-tuple-element.42), channel_id=1, source_target_pairs={{0,96},{8,104},{1,97},{9,105},{2,98},{10,106},{3,99},{11,107},{4,1... | collective-permute-start | bytes 1179656 | tf_op jit(solution)/shard_map/ppermute | solution.py:16
  44.4 19.8 %collective-permute-start.26 = (bf16[4,3,32,512]{3,2,1,0:T(8,128)(2,1)}, bf16[4,3,32,512]{3,2,1,0:T(8,128)(2,1)S(1)}, u32[]{:S(2)}, u32[]{:S(2)}) collective-permute-start(bf16[4,3,32,512]{3,2,1,0:T(8,128)(2,1)} %get-tuple-element.36), channel_id=1, source_target_pairs={{0,8},{8,16},{1,9},{9,17},{2,10},{10,18},{3,11},{11,19},{4,12},{12... | collective-permute-start | bytes 1179656 | tf_op jit(solution)/shard_map/ppermute | solution.py:16
  48.2 18.2 %collective-permute-start.27 = (bf16[4,3,32,512]{3,2,1,0:T(8,128)(2,1)}, bf16[4,3,32,512]{3,2,1,0:T(8,128)(2,1)S(1)}, u32[]{:S(2)}, u32[]{:S(2)}) collective-permute-start(bf16[4,3,32,512]{3,2,1,0:T(8,128)(2,1)} %get-tuple-element.37), channel_id=1, source_target_pairs={{0,16},{8,24},{1,17},{9,25},{2,18},{10,26},{3,19},{11,27},{4,20},{... | collective-permute-start | bytes 1179656 | tf_op jit(solution)/shard_map/ppermute | solution.py:16
  50.5 17.4 %collective-permute-start.28 = (bf16[4,3,32,512]{3,2,1,0:T(8,128)(2,1)}, bf16[4,3,32,512]{3,2,1,0:T(8,128)(2,1)S(1)}, u32[]{:S(2)}, u32[]{:S(2)}) collective-permute-start(bf16[4,3,32,512]{3,2,1,0:T(8,128)(2,1)} %get-tuple-element.38), channel_id=1, source_target_pairs={{0,24},{8,0},{1,25},{9,1},{2,26},{10,2},{3,27},{11,3},{4,28},{12,4... | collective-permute-start | bytes 1179656 | tf_op jit(solution)/shard_map/ppermute | solution.py:16
  58.4 12.2 %collective-permute-start.35 = (bf16[3,32,512]{2,1,0:T(8,128)(2,1)S(1)}, bf16[3,32,512]{2,1,0:T(8,128)(2,1)S(1)}, u32[]{:S(2)}, u32[]{:S(2)}) collective-permute-start(bf16[3,32,512]{2,1,0:T(8,128)(2,1)S(1)} %get-tuple-element.54), channel_id=1, source_target_pairs={{0,8},{8,16},{32,40},{40,48},{64,72},{72,80},{96,104},{104,112},{1... | collective-permute-start | bytes 294920 | tf_op jit(solution)/shard_map/ppermute | solution.py:16
  62.3 9.7 %collective-permute-start.37 = (bf16[3,32,512]{2,1,0:T(8,128)(2,1)S(1)}, bf16[3,32,512]{2,1,0:T(8,128)(2,1)S(1)}, u32[]{:S(2)}, u32[]{:S(2)}) collective-permute-start(bf16[3,32,512]{2,1,0:T(8,128)(2,1)S(1)} %get-tuple-element.55), channel_id=1, source_target_pairs={{0,24},{8,0},{32,56},{40,32},{64,88},{72,64},{96,120},{104,96},{1,... | collective-permute-start | bytes 294920 | tf_op jit(solution)/shard_map/ppermute | solution.py:16
  77.9 9.6 %collective-permute-start.9 = (bf16[64,512]{1,0:T(8,128)(2,1)S(1)}, bf16[64,512]{1,0:T(8,128)(2,1)S(1)}, u32[]{:S(2)}, u32[]{:S(2)}) collective-permute-start(bf16[64,512]{1,0:T(8,128)(2,1)S(1)} %fusion.11), channel_id=1, source_target_pairs={{0,24},{8,0},{1,25},{9,1},{2,26},{10,2},{3,27},{11,3},{4,28},{12,4... | collective-permute-start | bytes 196616 | tf_op jit(solution)/shard_map/ppermute | solution.py:16
  89.4 11.9 %collective-permute-start.11 = (bf16[2,64,512]{2,1,0:T(8,128)(2,1)S(1)}, bf16[2,64,512]{2,1,0:T(8,128)(2,1)S(1)}, u32[]{:S(2)}, u32[]{:S(2)}) collective-permute-start(bf16[2,64,512]{2,1,0:T(8,128)(2,1)S(1)} %pad_maximum_fusion.2), channel_id=1, source_target_pairs={{0,64},{1,65},{2,66},{3,67},{4,68},{5,69},{6,70},{7,71},{8,72},{9,... | collective-permute-start | bytes 393224 | tf_op jit(solution)/shard_map/ppermute | solution.py:16
  104.3 13.0 %collective-permute-start.13 = (bf16[2,64,512]{2,1,0:T(8,128)(2,1)S(1)}, bf16[2,64,512]{2,1,0:T(8,128)(2,1)S(1)}, u32[]{:S(2)}, u32[]{:S(2)}) collective-permute-start(bf16[2,64,512]{2,1,0:T(8,128)(2,1)S(1)} %select_select_fusion.3), channel_id=1, source_target_pairs={{0,7},{1,0},{2,1},{3,2},{4,3},{5,4},{6,5},{7,6},{8,15},{9,8},{10,9... | collective-permute-start | bytes 393224 | tf_op jit(solution)/shard_map/ppermute | solution.py:16
  112.7 18.7 %collective-permute-start.19 = (bf16[2,64,512]{2,1,0:T(8,128)(2,1)S(1)}, bf16[2,64,512]{2,1,0:T(8,128)(2,1)S(1)}, u32[]{:S(2)}, u32[]{:S(2)}) collective-permute-start(bf16[2,64,512]{2,1,0:T(8,128)(2,1)S(1)} %select_select_fusion.3), channel_id=1, source_target_pairs={{0,1},{1,2},{2,3},{3,4},{4,5},{5,6},{6,7},{7,0},{8,9},{9,10},{10,1... | collective-permute-start | bytes 393224 | tf_op jit(solution)/shard_map/ppermute | solution.py:16
  113.2 18.2 %collective-permute-start.18 = (bf16[2,64,512]{2,1,0:T(8,128)(2,1)S(1)}, bf16[2,64,512]{2,1,0:T(8,128)(2,1)S(1)}, u32[]{:S(2)}, u32[]{:S(2)}) collective-permute-start(bf16[2,64,512]{2,1,0:T(8,128)(2,1)S(1)} %select_select_fusion.3), channel_id=1, source_target_pairs={{0,2},{1,3},{2,4},{3,5},{4,6},{5,7},{6,0},{7,1},{8,10},{9,11},{10,... | collective-permute-start | bytes 393224 | tf_op jit(solution)/shard_map/ppermute | solution.py:16
  113.2 18.2 %collective-permute-start.17 = (bf16[2,64,512]{2,1,0:T(8,128)(2,1)S(1)}, bf16[2,64,512]{2,1,0:T(8,128)(2,1)S(1)}, u32[]{:S(2)}, u32[]{:S(2)}) collective-permute-start(bf16[2,64,512]{2,1,0:T(8,128)(2,1)S(1)} %select_select_fusion.3), channel_id=1, source_target_pairs={{0,3},{1,4},{2,5},{3,6},{4,7},{5,0},{6,1},{7,2},{8,11},{9,12},{10,... | collective-permute-start | bytes 393224 | tf_op jit(solution)/shard_map/ppermute | solution.py:16
  116.2 15.1 %collective-permute-start.16 = (bf16[2,64,512]{2,1,0:T(8,128)(2,1)S(1)}, bf16[2,64,512]{2,1,0:T(8,128)(2,1)S(1)}, u32[]{:S(2)}, u32[]{:S(2)}) collective-permute-start(bf16[2,64,512]{2,1,0:T(8,128)(2,1)S(1)} %select_select_fusion.3), channel_id=1, source_target_pairs={{0,4},{1,5},{2,6},{3,7},{4,0},{5,1},{6,2},{7,3},{8,12},{9,13},{10,... | collective-permute-start | bytes 393224 | tf_op jit(solution)/shard_map/ppermute | solution.py:16
  117.3 9.4 %collective-permute-start.14 = (bf16[2,64,512]{2,1,0:T(8,128)(2,1)S(1)}, bf16[2,64,512]{2,1,0:T(8,128)(2,1)S(1)}, u32[]{:S(2)}, u32[]{:S(2)}) collective-permute-start(bf16[2,64,512]{2,1,0:T(8,128)(2,1)S(1)} %select_select_fusion.3), channel_id=1, source_target_pairs={{0,6},{1,7},{2,0},{3,1},{4,2},{5,3},{6,4},{7,5},{8,14},{9,15},{10,... | collective-permute-start | bytes 393224 | tf_op jit(solution)/shard_map/ppermute | solution.py:16
  (25 other events, 175.9 us)
Sparse Core Ops, SparseCore 0:
  32.9 30.3 all-gather.4
  78.0 65.8 all-gather.6

commit v2 on v1

--- a/solution.py
+++ b/solution.py
@@ -21,11 +21,8 @@
     return lax.select_n(place, *got), lax.select_n((place + size - 1) % size, *got)
 
 
-def bands_kernel(info_ref, early_ref, late_ref, *out_refs):
-    parts = early_ref.shape[2]
-    for s in range(parts):
-        out_refs[s][:, 0] = early_ref[0, :, lax.rem(info_ref[2] + s, parts)]
-        out_refs[parts + s][:, 0] = late_ref[0, s]
+def bands_kernel(tile_ref, out_ref):
+    out_ref[:, 0] = tile_ref[0]
 
 
 def panels_kernel(info_ref, panel_ref, *out_refs):
@@ -114,8 +111,20 @@
     column_of_tiles = pl.BlockSpec((block_rows, 1, block, block), lambda c: (0, c, 0, 0))
     one_check = pl.BlockSpec((1, 8, block), lambda c: (c, 0, 0))
 
-    half, sides = cols // 2, lax.axis_size("row_1")
+    sides = lax.axis_size("row_1")
     my_y, my_z = lax.axis_index("row_0"), lax.axis_index("row_1")
+
+    bands = pl.pallas_call(
+        bands_kernel,
+        out_shape=jax.ShapeDtypeStruct((grid_rows, cols, piece, block), BF16),
+        grid=(cols,),
+        in_specs=[pl.BlockSpec((1, grid_rows, piece, block), lambda c: (c, 0, 0, 0))],
+        out_specs=pl.BlockSpec((grid_rows, 1, piece, block), lambda c: (0, c, 0, 0)),
+        cost_estimate=pl.CostEstimate(flops=cols * block * block, bytes_accessed=4 * cols * block * block, transcendentals=0),
+        name="bands",
+    )(tiles.reshape(block_rows * cols, grid_rows, piece, block))
+    bands = lax.all_to_all(bands, ROW, 0, 0)
+    upper = lax.all_gather(bands[:2], ROW).reshape(grid_rows, 2 * cols, piece, block)
 
     strip = block // grid_cols
     deep = tiles.reshape(block_rows, cols, grid_cols, strip, block)
@@ -132,38 +141,6 @@
     panels = shifts("col", cells, lambda s: [(0, s), (1, (1 + s) % grid_cols)])
     panel0, panel1 = from_two(panels, my_col)
     panels = lax.all_gather(jnp.stack([panel0, panel1]), "col")
-
-    tall = tiles.reshape(block_rows * cols, sides, sides, piece, block)
-    cell = jax.ShapeDtypeStruct((sides, half, piece, block), BF16)
-    cells = pl.pallas_call(
-        bands_kernel,
-        out_shape=(cell,) * (2 * sides),
-        grid=(half,),
-        in_specs=[
-            smem,
-            pl.BlockSpec((1, sides, sides, piece, block), lambda c: (c, 0, 0, 0, 0)),
-            pl.BlockSpec((1, sides, sides, piece, block), lambda c: (c + half, 0, 0, 0, 0)),
-        ],
-        out_specs=(pl.BlockSpec((sides, 1, piece, block), lambda c: (0, c, 0, 0)),) * (2 * sides),
-        cost_estimate=pl.CostEstimate(flops=cols * block * block, bytes_accessed=4 * cols * block * block, transcendentals=0),
-        name="bands",
-    )(info, tall, tall)
-    early = shifts(ROW, cells[:sides], lambda s: [(0, s), (1, (1 + s) % sides)])
-    late = shifts(ROW, cells[sides:], lambda s: [(0, sides * s), (1, sides * s + 1)])
-
-    early = jnp.stack(from_two(early, my_z), axis=1)
-    early = shifts(ROW, list(early), lambda s: [(z, sides * s + z) for z in range(sides)])
-    early = lax.select_n(my_y, *early)
-    late = lax.select_n(my_y, *late)
-    late = jnp.where(my_z == 1, jnp.roll(late, -1, axis=0), late)
-    late = shifts(
-        ROW,
-        list(late),
-        lambda s: [(sides * y + r, sides * y + (r + s) % sides) for y in range(sides) for r in (0, 1)],
-    )
-    late = jnp.stack(from_two(late, my_z))
-    upper = lax.all_gather(jnp.concatenate([early, late], axis=1), ROW)
-    upper = upper.reshape(grid_rows, 2 * cols, piece, block)
 
     corner = jnp.where(my_row == 1, panel0[0], panel1[0])
     corner = shifts("row_1", [corner] * sides, lambda s: [(0, s), (1, (1 + s) % sides)])

time: 190 us -> 192 us (1.011)
  blocking collectives: 0 us -> 47 us
  starting transfers between devices: 73.2 us -> 44 us
  waiting for transfers between devices: 48.2 us -> 34.1 us
  other arithmetic: 3.93 us -> 1.66 us
    all_to_all x0 -> x1, blocking collectives: none -> 47 us  [eliminate(): bands = lax.all_to_all(bands, ROW, 0, 0)]
    ppermute x38 -> x26, starting transfers between devices: 73.1 us -> 43.9 us  [shifts(): lax.ppermute(p, axis, pairs(s))]
    ppermute x38 -> x26, waiting for transfers between devices: 48.2 us -> 34 us  [shifts(): lax.ppermute(p, axis, pairs(s))]
    unnamed x35 -> x33, local copies, waits for them, and re-layouts: 4.99 us -> 4.93 us
  transfers between devices with their start and end apart: 40 -> 28, of which waited for: 20 -> 14; matrix products, arithmetic and copies ran while one was open for 4% -> 3% of each run, Pallas kernels for 8% -> 8%
where the time goes in v2:
time: 192 us; the launch traced here: 190 us
  blocking collectives  47 us (24%)
  starting transfers between devices  44 us (23%)
  Pallas kernels  37.1 us (19%)
  waiting for transfers between devices  34.1 us (18%)
  between operations  14.6 us (8%)
  local copies, waits for them, and re-layouts  10.3 us (5%)
    all_to_all x1, blocking collectives, eliminate(): bands = lax.all_to_all(bands, ROW, 0, 0)  47 us
    ppermute x26, starting transfers between devices, shifts(): lax.ppermute(p, axis, pairs(s))  43.9 us
    ppermute x26, waiting for transfers between devices, shifts(): lax.ppermute(p, axis, pairs(s))  34 us
    pallas_call x1, Pallas kernels, eliminate(): pl.pallas_call(trail_kernel, out_shape=(jax.ShapeDtypeStruct(tiles.shape,...  18.4 us
    pallas_call x1, Pallas kernels, eliminate(): pl.pallas_call(weigh_kernel, out_shape=jax.ShapeDtypeStruct((cols, 8, blo...  6.81 us
    pallas_call x1, Pallas kernels, eliminate(): pl.pallas_call(bands_kernel, out_shape=jax.ShapeDtypeStruct((grid_rows, c...  5.28 us
    unnamed x33, local copies, waits for them, and re-layouts  4.93 us
    pallas_call x1, Pallas kernels, eliminate(): pl.pallas_call(left_kernel, out_shape=(jax.ShapeDtypeStruct((rows, block)...  3.98 us
  transfers between devices with their start and end apart: 28, of which 14 were waited for; matrix products, arithmetic and copies ran while one was open for 3% of the time, Pallas kernels for 8%

profile of v2, /device:TPU:0, one launch (start us, length us, event | category | flops | bytes accessed | tf_op | source)
XLA Modules:
  0.0 189.9 jit_solution(16106196265045693126)
XLA Ops:
  7.8 2.6 %panels.1 = (bf16[3,64,512]{2,1,0:T(8,128)(2,1)}, bf16[3,64,512]{2,1,0:T(8,128)(2,1)}, bf16[3,64,512]{2,1,0:T(8,128)(2,1)}, bf16[3,64,512]{2,1,0:T(8,128)(2,1)},...) custom-call(s32[3]{0:T(128)} %pad_add_fusion.info_ref, ...), custom_call_target="tpu_custom_call" | custom-call | flops 786432 | bytes 3145728 | tf_op jit(solution)/shard_map/panels/pallas_call | solution.py:132
  11.9 3.5 %collective-permute-start.1 = (bf16[3,64,512]{2,1,0:T(8,128)(2,1)}, bf16[3,64,512]{2,1,0:T(8,128)(2,1)S(1)}, u32[]{:S(2)}, u32[]{:S(2)}) collective-permute-start(bf16[3,64,512]{2,1,0:T(8,128)(2,1)} %get-tuple-element.18), channel_id=1, source_target_pairs={{0,2},{1,3},{8,10},{9,11},{16,18},{17,19},{24,26},{25,27},{32,34},... | collective-permute-start | bytes 589832 | tf_op jit(solution)/shard_map/ppermute | solution.py:16
  22.9 2.3 %collective-permute-done.2 = bf16[3,64,512]{2,1,0:T(8,128)(2,1)S(1)} collective-permute-done((bf16[3,64,512]{2,1,0:T(8,128)(2,1)}, bf16[3,64,512]{2,1,0:T(8,128)(2,1)S(1)}, u32[]{:S(2)}, u32[]{:S(2)}) %collective-permute-start.2) | collective-permute-done | bytes 196640 | tf_op jit(solution)/shard_map/ppermute | solution.py:16
  25.2 4.2 %collective-permute-done.3 = bf16[3,64,512]{2,1,0:T(8,128)(2,1)S(1)} collective-permute-done((bf16[3,64,512]{2,1,0:T(8,128)(2,1)}, bf16[3,64,512]{2,1,0:T(8,128)(2,1)S(1)}, u32[]{:S(2)}, u32[]{:S(2)}) %collective-permute-start.3) | collective-permute-done | bytes 196640 | tf_op jit(solution)/shard_map/ppermute | solution.py:16
  29.4 2.3 %collective-permute-done.4 = bf16[3,64,512]{2,1,0:T(8,128)(2,1)S(1)} collective-permute-done((bf16[3,64,512]{2,1,0:T(8,128)(2,1)}, bf16[3,64,512]{2,1,0:T(8,128)(2,1)S(1)}, u32[]{:S(2)}, u32[]{:S(2)}) %collective-permute-start.4) | collective-permute-done | bytes 196640 | tf_op jit(solution)/shard_map/ppermute | solution.py:16
  32.8 5.3 %bands.1 = bf16[16,6,32,512]{3,2,1,0:T(8,128)(2,1)} custom-call(bf16[18,16,32,512]{3,2,1,0:T(8,128)(2,1)} %bitcast.67), custom_call_target="tpu_custom_call" | custom-call | flops 1572864 | bytes 6291456 | tf_op jit(solution)/shard_map/bands/pallas_call | solution.py:117
  38.1 47.0 %all_to_all.5 = bf16[16,6,32,512]{3,2,1,0:T(8,128)(2,1)S(1)} all-to-all(bf16[16,6,32,512]{3,2,1,0:T(8,128)(2,1)} %bands.1), channel_id=1, replica_groups=mesh['row_0'=4,'row_1'=4,'col'=8] {'row_0','row_1'}, dimensions={0} | all-to-all | bytes 6291456 | tf_op jit(solution)/shard_map/all_to_all | solution.py:126
  85.9 2.5 %collective-permute-start.9 = (bf16[64,512]{1,0:T(8,128)(2,1)S(1)}, bf16[64,512]{1,0:T(8,128)(2,1)S(1)}, u32[]{:S(2)}, u32[]{:S(2)}) collective-permute-start(bf16[64,512]{1,0:T(8,128)(2,1)S(1)} %fusion.2), channel_id=1, source_target_pairs={{0,24},{8,0},{1,25},{9,1},{2,26},{10,2},{3,27},{11,3},{4,28},{12,4... | collective-permute-start | bytes 196616 | tf_op jit(solution)/shard_map/ppermute | solution.py:16
  89.6 3.4 %collective-permute-start.7 = (bf16[64,512]{1,0:T(8,128)(2,1)S(1)}, bf16[64,512]{1,0:T(8,128)(2,1)S(1)}, u32[]{:S(2)}, u32[]{:S(2)}) collective-permute-start(bf16[64,512]{1,0:T(8,128)(2,1)S(1)} %fusion.2), channel_id=1, source_target_pairs={{0,8},{8,16},{1,9},{9,17},{2,10},{10,18},{3,11},{11,19},{4,12},{12... | collective-permute-start | bytes 196616 | tf_op jit(solution)/shard_map/ppermute | solution.py:16
  95.1 2.9 %collective-permute-start.11 = (bf16[2,64,512]{2,1,0:T(8,128)(2,1)S(1)}, bf16[2,64,512]{2,1,0:T(8,128)(2,1)S(1)}, u32[]{:S(2)}, u32[]{:S(2)}) collective-permute-start(bf16[2,64,512]{2,1,0:T(8,128)(2,1)S(1)} %pad_maximum_fusion.1), channel_id=1, source_target_pairs={{0,64},{1,65},{2,66},{3,67},{4,68},{5,69},{6,70},{7,71},{8,72},{9,... | collective-permute-start | bytes 393224 | tf_op jit(solution)/shard_map/ppermute | solution.py:16
  100.6 2.6 %collective-permute-done.11 = bf16[2,64,512]{2,1,0:T(8,128)(2,1)S(1)} collective-permute-done((bf16[2,64,512]{2,1,0:T(8,128)(2,1)S(1)}, bf16[2,64,512]{2,1,0:T(8,128)(2,1)S(1)}, u32[]{:S(2)}, u32[]{:S(2)}) %collective-permute-start.11) | collective-permute-done | bytes 131104 | tf_op jit(solution)/shard_map/ppermute | solution.py:16
  107.4 6.8 %weigh.1 = f32[6,8,512]{2,1,0:T(8,128)} custom-call(f32[8,1536]{1,0:T(8,128)} %pad.8.weight_ref, bf16[3,6,512,512]{3,2,1,0:T(8,128)(2,1)} %bitcast.68), custom_call_target="tpu_custom_call" | custom-call | flops 301989888 | bytes 9437184 | tf_op jit(solution)/shard_map/weigh/pallas_call | solution.py:156
  115.2 3.3 %collective-permute-start.17 = (bf16[2,64,512]{2,1,0:T(8,128)(2,1)S(1)}, bf16[2,64,512]{2,1,0:T(8,128)(2,1)S(1)}, u32[]{:S(2)}, u32[]{:S(2)}) collective-permute-start(bf16[2,64,512]{2,1,0:T(8,128)(2,1)S(1)} %select_select_fusion.2), channel_id=1, source_target_pairs={{0,3},{1,4},{2,5},{3,6},{4,7},{5,0},{6,1},{7,2},{8,11},{9,12},{10,... | collective-permute-start | bytes 393224 | tf_op jit(solution)/shard_map/ppermute | solution.py:16
  119.6 2.3 %collective-permute-start.14 = (bf16[2,64,512]{2,1,0:T(8,128)(2,1)S(1)}, bf16[2,64,512]{2,1,0:T(8,128)(2,1)S(1)}, u32[]{:S(2)}, u32[]{:S(2)}) collective-permute-start(bf16[2,64,512]{2,1,0:T(8,128)(2,1)S(1)} %select_select_fusion.2), channel_id=1, source_target_pairs={{0,6},{1,7},{2,0},{3,1},{4,2},{5,3},{6,4},{7,5},{8,14},{9,15},{10,... | collective-permute-start | bytes 393224 | tf_op jit(solution)/shard_map/ppermute | solution.py:16
  121.9 7.1 %collective-permute-done.14 = bf16[2,64,512]{2,1,0:T(8,128)(2,1)S(1)} collective-permute-done((bf16[2,64,512]{2,1,0:T(8,128)(2,1)S(1)}, bf16[2,64,512]{2,1,0:T(8,128)(2,1)S(1)}, u32[]{:S(2)}, u32[]{:S(2)}) %collective-permute-start.14) | collective-permute-done | bytes 131104 | tf_op jit(solution)/shard_map/ppermute | solution.py:16
  129.0 2.1 %collective-permute-start.15 = (bf16[2,64,512]{2,1,0:T(8,128)(2,1)S(1)}, bf16[2,64,512]{2,1,0:T(8,128)(2,1)S(1)}, u32[]{:S(2)}, u32[]{:S(2)}) collective-permute-start(bf16[2,64,512]{2,1,0:T(8,128)(2,1)S(1)} %select_select_fusion.2), channel_id=1, source_target_pairs={{0,5},{1,6},{2,7},{3,0},{4,1},{5,2},{6,3},{7,4},{8,13},{9,14},{10,... | collective-permute-start | bytes 393224 | tf_op jit(solution)/shard_map/ppermute | solution.py:16
  131.1 2.5 %collective-permute-done.15 = bf16[2,64,512]{2,1,0:T(8,128)(2,1)S(1)} collective-permute-done((bf16[2,64,512]{2,1,0:T(8,128)(2,1)S(1)}, bf16[2,64,512]{2,1,0:T(8,128)(2,1)S(1)}, u32[]{:S(2)}, u32[]{:S(2)}) %collective-permute-start.15) | collective-permute-done | bytes 131104 | tf_op jit(solution)/shard_map/ppermute | solution.py:16
  137.1 4.0 %left.1 = (bf16[1536,512]{1,0:T(8,128)(2,1)S(1)}, bf16[1536,512]{1,0:T(8,128)(2,1)S(1)}, f32[2,8,512]{2,1,0:T(8,128)S(1)}) custom-call(s32[3]{0:T(128)S(1)} %copy-done.1, bf16[8,2,3,64,512]{4,3,2,1,0:T(8,128)(2,1)S(1)} %bitcast.65, bf16[512,512]{1,0:T(8,128)(2,1)S(1)} %bitcast.64, bf16[2,512,512]{2,1,0:T(8,128)(2,1)S(1)} %copy-done.3, f32[8,1536]{1,0:T(8,128)S(1)} %copy-done), custom_call_target="tpu_custom_call" | custom-call | flops 2415919104 | bytes 9437184 | tf_op jit(solution)/shard_map/left/pallas_call | solution.py:166
  142.4 2.1 %collective-permute-start.22 = (f32[8,512]{1,0:T(8,128)S(1)}, f32[8,512]{1,0:T(8,128)S(1)}, u32[]{:S(2)}, u32[]{:S(2)}) collective-permute-start(f32[8,512]{1,0:T(8,128)S(1)} %pad_maximum_fusion.2), channel_id=1, source_target_pairs={{0,24},{8,0},{16,8},{24,16},{1,25},{9,1},{17,9},{25,17},{2,26},{10... | collective-permute-start | bytes 49160 | tf_op jit(solution)/shard_map/ppermute | solution.py:16
  144.4 2.2 %collective-permute-start.21 = (f32[8,512]{1,0:T(8,128)S(1)}, f32[8,512]{1,0:T(8,128)S(1)}, u32[]{:S(2)}, u32[]{:S(2)}) collective-permute-start(f32[8,512]{1,0:T(8,128)S(1)} %pad_maximum_fusion.2), channel_id=1, source_target_pairs={{0,16},{8,24},{16,0},{24,8},{1,17},{9,25},{17,1},{25,9},{2,18},{10... | collective-permute-start | bytes 49160 | tf_op jit(solution)/shard_map/ppermute | solution.py:16
  146.9 2.9 %collective-permute-done.21 = f32[8,512]{1,0:T(8,128)S(1)} collective-permute-done((f32[8,512]{1,0:T(8,128)S(1)}, f32[8,512]{1,0:T(8,128)S(1)}, u32[]{:S(2)}, u32[]{:S(2)}) %collective-permute-start.21) | collective-permute-done | bytes 16416 | tf_op jit(solution)/shard_map/ppermute | solution.py:16
  153.3 2.9 %collective-permute-start.24 = (f32[8,512]{1,0:T(8,128)S(1)}, f32[8,512]{1,0:T(8,128)S(1)}, u32[]{:S(2)}, u32[]{:S(2)}) collective-permute-start(f32[8,512]{1,0:T(8,128)S(1)} %add_add_fusion.1), channel_id=1, source_target_pairs={{0,64},{32,96},{64,0},{96,32},{1,65},{33,97},{65,1},{97,33},{2,66}... | collective-permute-start | bytes 49160 | tf_op jit(solution)/shard_map/ppermute | solution.py:16
  158.5 2.6 %collective-permute-done.23 = f32[8,512]{1,0:T(8,128)S(1)} collective-permute-done((f32[8,512]{1,0:T(8,128)S(1)}, f32[8,512]{1,0:T(8,128)S(1)}, u32[]{:S(2)}, u32[]{:S(2)}) %collective-permute-start.23) | collective-permute-done | bytes 16416 | tf_op jit(solution)/shard_map/ppermute | solution.py:16
  162.5 18.4 %trail.1 = (bf16[3,6,512,512]{3,2,1,0:T(8,128)(2,1)}, f32[6,8,512]{2,1,0:T(8,128)}) custom-call(s32[3]{0:T(128)} %pad_add_fusion.info_ref, bf16[1536,512]{1,0:T(8,128)(2,1)} %copy-done.4, bf16[1536,512]{1,0:T(8,128)(2,1)} %copy-done.5, bf16[512,512]{1,0:T(8,128)(2,1)} %convolution_convert_fusion.second_ref, f32[2,8,512]{2,1,0:T(8,128)} %slice.56.sums_ref, ...), custom_call_target="tpu_custom_call" | custom-call | flops 12079595520 | bytes 18874368 | tf_op jit(solution)/shard_map/trail/pallas_call | solution.py:189
  (99 shorter events, 37.5 us)
Async XLA Ops:
  7.2 127.0 %all-gather.5.cloned.1.call-start = ((), (), s32[]{:S(2)}) async-start(), calls=%async_computation.1 | async-start | bytes 3538944 | tf_op jit(solution)/shard_map/all_gather | solution.py:143
  10.5 9.2 %collective-permute-start = (bf16[3,64,512]{2,1,0:T(8,128)(2,1)}, bf16[3,64,512]{2,1,0:T(8,128)(2,1)S(1)}, u32[]{:S(2)}, u32[]{:S(2)}) collective-permute-start(bf16[3,64,512]{2,1,0:T(8,128)(2,1)} %get-tuple-element.17), channel_id=1, source_target_pairs={{0,1},{1,2},{8,9},{9,10},{16,17},{17,18},{24,25},{25,26},{32,33},{... | collective-permute-start | bytes 589832 | tf_op jit(solution)/shard_map/ppermute | solution.py:16
  11.9 9.1 %collective-permute-start.1 = (bf16[3,64,512]{2,1,0:T(8,128)(2,1)}, bf16[3,64,512]{2,1,0:T(8,128)(2,1)S(1)}, u32[]{:S(2)}, u32[]{:S(2)}) collective-permute-start(bf16[3,64,512]{2,1,0:T(8,128)(2,1)} %get-tuple-element.18), channel_id=1, source_target_pairs={{0,2},{1,3},{8,10},{9,11},{16,18},{17,19},{24,26},{25,27},{32,34},... | collective-permute-start | bytes 589832 | tf_op jit(solution)/shard_map/ppermute | solution.py:16
  15.4 9.8 %collective-permute-start.2 = (bf16[3,64,512]{2,1,0:T(8,128)(2,1)}, bf16[3,64,512]{2,1,0:T(8,128)(2,1)S(1)}, u32[]{:S(2)}, u32[]{:S(2)}) collective-permute-start(bf16[3,64,512]{2,1,0:T(8,128)(2,1)} %get-tuple-element.19), channel_id=1, source_target_pairs={{0,3},{1,4},{8,11},{9,12},{16,19},{17,20},{24,27},{25,28},{32,35},... | collective-permute-start | bytes 589832 | tf_op jit(solution)/shard_map/ppermute | solution.py:16
  16.7 12.7 %collective-permute-start.3 = (bf16[3,64,512]{2,1,0:T(8,128)(2,1)}, bf16[3,64,512]{2,1,0:T(8,128)(2,1)S(1)}, u32[]{:S(2)}, u32[]{:S(2)}) collective-permute-start(bf16[3,64,512]{2,1,0:T(8,128)(2,1)} %get-tuple-element.20), channel_id=1, source_target_pairs={{0,4},{1,5},{8,12},{9,13},{16,20},{17,21},{24,28},{25,29},{32,36},... | collective-permute-start | bytes 589832 | tf_op jit(solution)/shard_map/ppermute | solution.py:16
  18.3 13.5 %collective-permute-start.4 = (bf16[3,64,512]{2,1,0:T(8,128)(2,1)}, bf16[3,64,512]{2,1,0:T(8,128)(2,1)S(1)}, u32[]{:S(2)}, u32[]{:S(2)}) collective-permute-start(bf16[3,64,512]{2,1,0:T(8,128)(2,1)} %get-tuple-element.21), channel_id=1, source_target_pairs={{0,5},{1,6},{8,13},{9,14},{16,21},{17,22},{24,29},{25,30},{32,37},... | collective-permute-start | bytes 589832 | tf_op jit(solution)/shard_map/ppermute | solution.py:16
  19.6 12.1 %collective-permute-start.5 = (bf16[3,64,512]{2,1,0:T(8,128)(2,1)}, bf16[3,64,512]{2,1,0:T(8,128)(2,1)S(1)}, u32[]{:S(2)}, u32[]{:S(2)}) collective-permute-start(bf16[3,64,512]{2,1,0:T(8,128)(2,1)} %get-tuple-element.22), channel_id=1, source_target_pairs={{0,6},{1,7},{8,14},{9,15},{16,22},{17,23},{24,30},{25,31},{32,38},... | collective-permute-start | bytes 589832 | tf_op jit(solution)/shard_map/ppermute | solution.py:16
  21.0 10.8 %collective-permute-start.6 = (bf16[3,64,512]{2,1,0:T(8,128)(2,1)}, bf16[3,64,512]{2,1,0:T(8,128)(2,1)S(1)}, u32[]{:S(2)}, u32[]{:S(2)}) collective-permute-start(bf16[3,64,512]{2,1,0:T(8,128)(2,1)} %get-tuple-element.23), channel_id=1, source_target_pairs={{0,7},{1,0},{8,15},{9,8},{16,23},{17,16},{24,31},{25,24},{32,39},{... | collective-permute-start | bytes 589832 | tf_op jit(solution)/shard_map/ppermute | solution.py:16
  32.7 129.7 %all-gather.7.cloned.1.call-start = ((), (), s32[]{:S(2)}) async-start(), calls=%async_computation.2 | async-start | bytes 6684672 | tf_op jit(solution)/shard_map/all_gather | solution.py:127
  85.9 7.2 %collective-permute-start.9 = (bf16[64,512]{1,0:T(8,128)(2,1)S(1)}, bf16[64,512]{1,0:T(8,128)(2,1)S(1)}, u32[]{:S(2)}, u32[]{:S(2)}) collective-permute-start(bf16[64,512]{1,0:T(8,128)(2,1)S(1)} %fusion.2), channel_id=1, source_target_pairs={{0,24},{8,0},{1,25},{9,1},{2,26},{10,2},{3,27},{11,3},{4,28},{12,4... | collective-permute-start | bytes 196616 | tf_op jit(solution)/shard_map/ppermute | solution.py:16
  89.6 5.4 %collective-permute-start.7 = (bf16[64,512]{1,0:T(8,128)(2,1)S(1)}, bf16[64,512]{1,0:T(8,128)(2,1)S(1)}, u32[]{:S(2)}, u32[]{:S(2)}) collective-permute-start(bf16[64,512]{1,0:T(8,128)(2,1)S(1)} %fusion.2), channel_id=1, source_target_pairs={{0,8},{8,16},{1,9},{9,17},{2,10},{10,18},{3,11},{11,19},{4,12},{12... | collective-permute-start | bytes 196616 | tf_op jit(solution)/shard_map/ppermute | solution.py:16
  95.1 8.1 %collective-permute-start.11 = (bf16[2,64,512]{2,1,0:T(8,128)(2,1)S(1)}, bf16[2,64,512]{2,1,0:T(8,128)(2,1)S(1)}, u32[]{:S(2)}, u32[]{:S(2)}) collective-permute-start(bf16[2,64,512]{2,1,0:T(8,128)(2,1)S(1)} %pad_maximum_fusion.1), channel_id=1, source_target_pairs={{0,64},{1,65},{2,66},{3,67},{4,68},{5,69},{6,70},{7,71},{8,72},{9,... | collective-permute-start | bytes 393224 | tf_op jit(solution)/shard_map/ppermute | solution.py:16
  97.9 5.8 %collective-permute-start.12 = (bf16[2,64,512]{2,1,0:T(8,128)(2,1)S(1)}, bf16[2,64,512]{2,1,0:T(8,128)(2,1)S(1)}, u32[]{:S(2)}, u32[]{:S(2)}) collective-permute-start(bf16[2,64,512]{2,1,0:T(8,128)(2,1)S(1)} %pad_maximum_fusion.1), channel_id=1, source_target_pairs={{0,96},{1,97},{2,98},{3,99},{4,100},{5,101},{6,102},{7,103},{8,104... | collective-permute-start | bytes 393224 | tf_op jit(solution)/shard_map/ppermute | solution.py:16
  99.2 6.5 %collective-permute-start.10 = (bf16[2,64,512]{2,1,0:T(8,128)(2,1)S(1)}, bf16[2,64,512]{2,1,0:T(8,128)(2,1)S(1)}, u32[]{:S(2)}, u32[]{:S(2)}) collective-permute-start(bf16[2,64,512]{2,1,0:T(8,128)(2,1)S(1)} %pad_maximum_fusion.1), channel_id=1, source_target_pairs={{0,32},{1,33},{2,34},{3,35},{4,36},{5,37},{6,38},{7,39},{8,40},{9,... | collective-permute-start | bytes 393224 | tf_op jit(solution)/shard_map/ppermute | solution.py:16
  105.8 13.8 %collective-permute-start.13 = (bf16[2,64,512]{2,1,0:T(8,128)(2,1)S(1)}, bf16[2,64,512]{2,1,0:T(8,128)(2,1)S(1)}, u32[]{:S(2)}, u32[]{:S(2)}) collective-permute-start(bf16[2,64,512]{2,1,0:T(8,128)(2,1)S(1)} %select_select_fusion.2), channel_id=1, source_target_pairs={{0,7},{1,0},{2,1},{3,2},{4,3},{5,4},{6,5},{7,6},{8,15},{9,8},{10,9... | collective-permute-start | bytes 393224 | tf_op jit(solution)/shard_map/ppermute | solution.py:16
  115.1 18.6 %collective-permute-start.19 = (bf16[2,64,512]{2,1,0:T(8,128)(2,1)S(1)}, bf16[2,64,512]{2,1,0:T(8,128)(2,1)S(1)}, u32[]{:S(2)}, u32[]{:S(2)}) collective-permute-start(bf16[2,64,512]{2,1,0:T(8,128)(2,1)S(1)} %select_select_fusion.2), channel_id=1, source_target_pairs={{0,1},{1,2},{2,3},{3,4},{4,5},{5,6},{6,7},{7,0},{8,9},{9,10},{10,1... | collective-permute-start | bytes 393224 | tf_op jit(solution)/shard_map/ppermute | solution.py:16
  115.2 18.6 %collective-permute-start.18 = (bf16[2,64,512]{2,1,0:T(8,128)(2,1)S(1)}, bf16[2,64,512]{2,1,0:T(8,128)(2,1)S(1)}, u32[]{:S(2)}, u32[]{:S(2)}) collective-permute-start(bf16[2,64,512]{2,1,0:T(8,128)(2,1)S(1)} %select_select_fusion.2), channel_id=1, source_target_pairs={{0,2},{1,3},{2,4},{3,5},{4,6},{5,7},{6,0},{7,1},{8,10},{9,11},{10,... | collective-permute-start | bytes 393224 | tf_op jit(solution)/shard_map/ppermute | solution.py:16
  115.2 18.5 %collective-permute-start.17 = (bf16[2,64,512]{2,1,0:T(8,128)(2,1)S(1)}, bf16[2,64,512]{2,1,0:T(8,128)(2,1)S(1)}, u32[]{:S(2)}, u32[]{:S(2)}) collective-permute-start(bf16[2,64,512]{2,1,0:T(8,128)(2,1)S(1)} %select_select_fusion.2), channel_id=1, source_target_pairs={{0,3},{1,4},{2,5},{3,6},{4,7},{5,0},{6,1},{7,2},{8,11},{9,12},{10,... | collective-permute-start | bytes 393224 | tf_op jit(solution)/shard_map/ppermute | solution.py:16
  118.5 15.1 %collective-permute-start.16 = (bf16[2,64,512]{2,1,0:T(8,128)(2,1)S(1)}, bf16[2,64,512]{2,1,0:T(8,128)(2,1)S(1)}, u32[]{:S(2)}, u32[]{:S(2)}) collective-permute-start(bf16[2,64,512]{2,1,0:T(8,128)(2,1)S(1)} %select_select_fusion.2), channel_id=1, source_target_pairs={{0,4},{1,5},{2,6},{3,7},{4,0},{5,1},{6,2},{7,3},{8,12},{9,13},{10,... | collective-permute-start | bytes 393224 | tf_op jit(solution)/shard_map/ppermute | solution.py:16
  119.6 9.4 %collective-permute-start.14 = (bf16[2,64,512]{2,1,0:T(8,128)(2,1)S(1)}, bf16[2,64,512]{2,1,0:T(8,128)(2,1)S(1)}, u32[]{:S(2)}, u32[]{:S(2)}) collective-permute-start(bf16[2,64,512]{2,1,0:T(8,128)(2,1)S(1)} %select_select_fusion.2), channel_id=1, source_target_pairs={{0,6},{1,7},{2,0},{3,1},{4,2},{5,3},{6,4},{7,5},{8,14},{9,15},{10,... | collective-permute-start | bytes 393224 | tf_op jit(solution)/shard_map/ppermute | solution.py:16
  144.4 5.4 %collective-permute-start.21 = (f32[8,512]{1,0:T(8,128)S(1)}, f32[8,512]{1,0:T(8,128)S(1)}, u32[]{:S(2)}, u32[]{:S(2)}) collective-permute-start(f32[8,512]{1,0:T(8,128)S(1)} %pad_maximum_fusion.2), channel_id=1, source_target_pairs={{0,16},{8,24},{16,0},{24,8},{1,17},{9,25},{17,1},{25,9},{2,18},{10... | collective-permute-start | bytes 49160 | tf_op jit(solution)/shard_map/ppermute | solution.py:16
  146.6 4.9 %collective-permute-start.20 = (f32[8,512]{1,0:T(8,128)S(1)}, f32[8,512]{1,0:T(8,128)S(1)}, u32[]{:S(2)}, u32[]{:S(2)}) collective-permute-start(f32[8,512]{1,0:T(8,128)S(1)} %pad_maximum_fusion.2), channel_id=1, source_target_pairs={{0,8},{8,16},{16,24},{24,0},{1,9},{9,17},{17,25},{25,1},{2,10},{10... | collective-permute-start | bytes 49160 | tf_op jit(solution)/shard_map/ppermute | solution.py:16
  151.6 5.9 %collective-permute-start.25 = (f32[8,512]{1,0:T(8,128)S(1)}, f32[8,512]{1,0:T(8,128)S(1)}, u32[]{:S(2)}, u32[]{:S(2)}) collective-permute-start(f32[8,512]{1,0:T(8,128)S(1)} %add_add_fusion.1), channel_id=1, source_target_pairs={{0,96},{32,0},{64,32},{96,64},{1,97},{33,1},{65,33},{97,65},{2,98}... | collective-permute-start | bytes 49160 | tf_op jit(solution)/shard_map/ppermute | solution.py:16
  153.3 5.2 %collective-permute-start.24 = (f32[8,512]{1,0:T(8,128)S(1)}, f32[8,512]{1,0:T(8,128)S(1)}, u32[]{:S(2)}, u32[]{:S(2)}) collective-permute-start(f32[8,512]{1,0:T(8,128)S(1)} %add_add_fusion.1), channel_id=1, source_target_pairs={{0,64},{32,96},{64,0},{96,32},{1,65},{33,97},{65,1},{97,33},{2,66}... | collective-permute-start | bytes 49160 | tf_op jit(solution)/shard_map/ppermute | solution.py:16
  (12 other events, 83.1 us)
Sparse Core Ops, SparseCore 0:
  32.9 30.3 all-gather.4
  86.0 60.4 all-gather.6

commit v3 on v2

--- a/solution.py
+++ b/solution.py
@@ -22,7 +22,8 @@
 
 
 def bands_kernel(tile_ref, out_ref):
-    out_ref[:, 0] = tile_ref[0]
+    for c in range(tile_ref.shape[0]):
+        out_ref[:, c] = tile_ref[c]
 
 
 def panels_kernel(info_ref, panel_ref, *out_refs):
@@ -49,26 +50,30 @@
     out_ref[0] = times_rows(weight_ref[...], tile)
 
 
-def left_kernel(info_ref, panel_ref, corner_ref, multiplier_ref, weight_ref, left0_ref, left1_ref, sum_ref):
-    block_rows, width = left0_ref.shape[0] // corner_ref.shape[0], corner_ref.shape[0]
-    strips, _, _, _, _ = panel_ref.shape
+def left_kernel(strips, info_ref, corner_ref, multiplier_ref, weight_ref, *refs):
+    panel_refs, (left0_ref, left1_ref, sum_ref) = refs[:strips], refs[strips:]
+    width = corner_ref.shape[0]
+    _, block_rows, strip, _ = panel_refs[0].shape
+    row = lax.broadcasted_iota(jnp.int32, (block_rows * width, width), 0)
 
     def column(step):
-        parts = [panel_ref[j, step, a] for a in range(block_rows) for j in range(strips)]
+        parts = [ref[step, a] for a in range(block_rows) for ref in panel_refs]
         return jnp.concatenate(parts, axis=0)
 
     def finish(step, factor, left_ref):
-        left = jnp.dot(factor, multiplier_ref[step], preferred_element_type=F32).astype(BF16)
-        left_ref[...] = left
-
-        @pl.when(info_ref[1] <= step)
-        def _():
-            left_ref[:width] = jnp.zeros((width, width), BF16)
-
+        left = jnp.dot(factor, multiplier_ref[step], preferred_element_type=F32)
+        left = jnp.where((row < width) & (info_ref[1] <= step), jnp.zeros_like(left), left).astype(BF16)
+        for s in range(strips):
+            place = lax.rem(info_ref[0] - s + strips, strips) * strip
+            for a in range(block_rows):
+                at = pl.multiple_of(a * width + place, strip)
+                start = (a * strips + s) * strip
+                left_ref[pl.ds(at, strip), :] = left[start : start + strip]
         sum_ref[step] = times_rows(weight_ref[...], left_ref[...])
-
-    finish(0, column(0), left0_ref)
-    update = jnp.dot(left0_ref[...], corner_ref[...], preferred_element_type=F32)
+        return left
+
+    left0 = finish(0, column(0), left0_ref)
+    update = jnp.dot(left0, corner_ref[...], preferred_element_type=F32)
     finish(1, (column(1).astype(F32) - update).astype(BF16), left1_ref)
 
 
@@ -117,9 +122,9 @@
     bands = pl.pallas_call(
         bands_kernel,
         out_shape=jax.ShapeDtypeStruct((grid_rows, cols, piece, block), BF16),
-        grid=(cols,),
-        in_specs=[pl.BlockSpec((1, grid_rows, piece, block), lambda c: (c, 0, 0, 0))],
-        out_specs=pl.BlockSpec((grid_rows, 1, piece, block), lambda c: (0, c, 0, 0)),
+        grid=(2,),
+        in_specs=[pl.BlockSpec((cols // 2, grid_rows, piece, block), lambda c: (c, 0, 0, 0))],
+        out_specs=pl.BlockSpec((grid_rows, cols // 2, piece, block), lambda c: (0, c, 0, 0)),
         cost_estimate=pl.CostEstimate(flops=cols * block * block, bytes_accessed=4 * cols * block * block, transcendentals=0),
         name="bands",
     )(tiles.reshape(block_rows * cols, grid_rows, piece, block))
@@ -140,7 +145,9 @@
     )(info, deep)
     panels = shifts("col", cells, lambda s: [(0, s), (1, (1 + s) % grid_cols)])
     panel0, panel1 = from_two(panels, my_col)
-    panels = lax.all_gather(jnp.stack([panel0, panel1]), "col")
+    panels = jnp.stack([panel0, panel1])
+    around = lambda s: [(i, (i + s) % grid_cols) for i in range(grid_cols)]
+    panels = shifts("col", [panels] * grid_cols, around)
 
     corner = jnp.where(my_row == 1, panel0[0], panel1[0])
     corner = shifts("row_1", [corner] * sides, lambda s: [(0, s), (1, (1 + s) % sides)])
@@ -164,18 +171,18 @@
     )(weights, tiles)
 
     left0, left1, sums = pl.pallas_call(
-        left_kernel,
+        functools.partial(left_kernel, grid_cols),
         out_shape=(
             jax.ShapeDtypeStruct((rows, block), BF16),
             jax.ShapeDtypeStruct((rows, block), BF16),
             jax.ShapeDtypeStruct((2, 8, block), F32),
         ),
-        in_specs=[smem] + [pl.BlockSpec(memory_space=pltpu.VMEM)] * 4,
+        in_specs=[smem] + [pl.BlockSpec(memory_space=pltpu.VMEM)] * (3 + grid_cols),
         out_specs=(pl.BlockSpec(memory_space=pltpu.VMEM),) * 3,
         cost_estimate=pl.CostEstimate(flops=6 * rows * block * block, bytes_accessed=12 * rows * block, transcendentals=0),
         compiler_params=pltpu.CompilerParams(vmem_limit_bytes=24 << 20),
         name="left",
-    )(info, panels, corners[0], multiplier, weights)
+    )(info, corners[0], multiplier, weights, *panels)
     second_left = jnp.dot(corners[1], multiplier[0], preferred_element_type=F32).astype(BF16)
 
     own = jnp.concatenate([base[:, 0], sums[:, 0]], axis=0)

time: 192 us -> 258 us (1.34)
  waiting for transfers between devices: 34.1 us -> 108 us
  local copies, waits for them, and re-layouts: 10.3 us -> 7.37 us
    ppermute x26 -> x33, waiting for transfers between devices: 34 us -> 108 us  [shifts(): lax.ppermute(p, axis, pairs(s))]
    unnamed x33 -> x31, local copies, waits for them, and re-layouts: 4.93 us -> 2 us
    ppermute x26 -> x33, starting transfers between devices: 43.9 us -> 42.4 us  [shifts(): lax.ppermute(p, axis, pairs(s))]
  transfers between devices with their start and end apart: 28 -> 34, of which waited for: 14 -> 20; matrix products, arithmetic and copies ran while one was open for 3% -> 2% of each run, Pallas kernels for 8% -> 5%
where the time goes in v3:
time: 258 us; the launch traced here: 257 us
  waiting for transfers between devices  108 us (42%)
  blocking collectives  47.6 us (18%)
  starting transfers between devices  42.4 us (16%)
  Pallas kernels  35.2 us (14%)
  between operations  14.6 us (6%)
  local copies, waits for them, and re-layouts  7.37 us (3%)
    ppermute x33, waiting for transfers between devices, shifts(): lax.ppermute(p, axis, pairs(s))  108 us
    all_to_all x1, blocking collectives, eliminate(): bands = lax.all_to_all(bands, ROW, 0, 0)  47.6 us
    ppermute x33, starting transfers between devices, shifts(): lax.ppermute(p, axis, pairs(s))  42.4 us
    pallas_call x1, Pallas kernels, eliminate(): pl.pallas_call(trail_kernel, out_shape=(jax.ShapeDtypeStruct(tiles.shape,...  18.4 us
    pallas_call x1, Pallas kernels, eliminate(): pl.pallas_call(weigh_kernel, out_shape=jax.ShapeDtypeStruct((cols, 8, blo...  6.9 us
  transfers between devices with their start and end apart: 34, of which 20 were waited for; matrix products, arithmetic and copies ran while one was open for 2% of the time, Pallas kernels for 5%

profile of v3, /device:TPU:0, one launch (start us, length us, event | category | flops | bytes accessed | tf_op | source)
XLA Modules:
  0.0 257.0 jit_solution(615890610459059858)
XLA Ops:
  7.2 3.2 %bands.1 = bf16[16,6,32,512]{3,2,1,0:T(8,128)(2,1)} custom-call(bf16[18,16,32,512]{3,2,1,0:T(8,128)(2,1)} %bitcast.64), custom_call_target="tpu_custom_call" | custom-call | flops 1572864 | bytes 6291456 | tf_op jit(solution)/shard_map/bands/pallas_call | solution.py:122
  10.4 47.6 %all_to_all.5 = bf16[16,6,32,512]{3,2,1,0:T(8,128)(2,1)S(1)} all-to-all(bf16[16,6,32,512]{3,2,1,0:T(8,128)(2,1)} %bands.1), channel_id=1, replica_groups=mesh['row_0'=4,'row_1'=4,'col'=8] {'row_0','row_1'}, dimensions={0} | all-to-all | bytes 6291456 | tf_op jit(solution)/shard_map/all_to_all | solution.py:131
  63.6 3.4 %collective-permute-start.1 = (bf16[3,64,512]{2,1,0:T(8,128)(2,1)}, bf16[3,64,512]{2,1,0:T(8,128)(2,1)S(1)}, u32[]{:S(2)}, u32[]{:S(2)}) collective-permute-start(bf16[3,64,512]{2,1,0:T(8,128)(2,1)} %get-tuple-element.18), channel_id=1, source_target_pairs={{0,2},{1,3},{8,10},{9,11},{16,18},{17,19},{24,26},{25,27},{32,34},... | collective-permute-start | bytes 589832 | tf_op jit(solution)/shard_map/ppermute | solution.py:16
  76.8 4.2 %collective-permute-done.3 = bf16[3,64,512]{2,1,0:T(8,128)(2,1)S(1)} collective-permute-done((bf16[3,64,512]{2,1,0:T(8,128)(2,1)}, bf16[3,64,512]{2,1,0:T(8,128)(2,1)S(1)}, u32[]{:S(2)}, u32[]{:S(2)}) %collective-permute-start.3) | collective-permute-done | bytes 196640 | tf_op jit(solution)/shard_map/ppermute | solution.py:16
  83.5 3.0 %collective-permute-start.9 = (bf16[64,512]{1,0:T(8,128)(2,1)S(1)}, bf16[64,512]{1,0:T(8,128)(2,1)S(1)}, u32[]{:S(2)}, u32[]{:S(2)}) collective-permute-start(bf16[64,512]{1,0:T(8,128)(2,1)S(1)} %fusion.2), channel_id=1, source_target_pairs={{0,24},{8,0},{1,25},{9,1},{2,26},{10,2},{3,27},{11,3},{4,28},{12,4... | collective-permute-start | bytes 196616 | tf_op jit(solution)/shard_map/ppermute | solution.py:16
  90.7 3.2 %collective-permute-done.7 = bf16[64,512]{1,0:T(8,128)(2,1)S(1)} collective-permute-done((bf16[64,512]{1,0:T(8,128)(2,1)S(1)}, bf16[64,512]{1,0:T(8,128)(2,1)S(1)}, u32[]{:S(2)}, u32[]{:S(2)}) %collective-permute-start.7) | collective-permute-done | bytes 65568 | tf_op jit(solution)/shard_map/ppermute | solution.py:16
  100.3 3.4 %collective-permute-done.11 = bf16[2,64,512]{2,1,0:T(8,128)(2,1)S(1)} collective-permute-done((bf16[2,64,512]{2,1,0:T(8,128)(2,1)S(1)}, bf16[2,64,512]{2,1,0:T(8,128)(2,1)S(1)}, u32[]{:S(2)}, u32[]{:S(2)}) %collective-permute-start.11) | collective-permute-done | bytes 131104 | tf_op jit(solution)/shard_map/ppermute | solution.py:16
  103.7 4.3 %collective-permute-done.10 = bf16[2,64,512]{2,1,0:T(8,128)(2,1)S(1)} collective-permute-done((bf16[2,64,512]{2,1,0:T(8,128)(2,1)S(1)}, bf16[2,64,512]{2,1,0:T(8,128)(2,1)S(1)}, u32[]{:S(2)}, u32[]{:S(2)}) %collective-permute-start.10) | collective-permute-done | bytes 131104 | tf_op jit(solution)/shard_map/ppermute | solution.py:16
  108.1 6.9 %weigh.1 = f32[6,8,512]{2,1,0:T(8,128)} custom-call(f32[8,1536]{1,0:T(8,128)} %pad.8.weight_ref, bf16[3,6,512,512]{3,2,1,0:T(8,128)(2,1)} %bitcast.66), custom_call_target="tpu_custom_call" | custom-call | flops 301989888 | bytes 9437184 | tf_op jit(solution)/shard_map/weigh/pallas_call | solution.py:163
  118.9 3.3 %collective-permute-start.23 = (bf16[2,3,64,512]{3,2,1,0:T(8,128)(2,1)S(1)}, bf16[2,3,64,512]{3,2,1,0:T(8,128)(2,1)S(1)}, u32[]{:S(2)}, u32[]{:S(2)}) collective-permute-start(bf16[2,3,64,512]{3,2,1,0:T(8,128)(2,1)S(1)} %pad_maximum_fusion.refs_0_), channel_id=1, source_target_pairs={{0,4},{1,5},{2,6},{3,7},{4,0},{5,1},{6,2},{7,3},{8,12},{9,13},{10,... | collective-permute-start | bytes 1179656 | tf_op jit(solution)/shard_map/ppermute | solution.py:16
  122.4 28.9 %collective-permute-done.14 = bf16[2,64,512]{2,1,0:T(8,128)(2,1)S(1)} collective-permute-done((bf16[2,64,512]{2,1,0:T(8,128)(2,1)S(1)}, bf16[2,64,512]{2,1,0:T(8,128)(2,1)S(1)}, u32[]{:S(2)}, u32[]{:S(2)}) %collective-permute-start.14) | collective-permute-done | bytes 131104 | tf_op jit(solution)/shard_map/ppermute | solution.py:16
  151.4 5.3 %collective-permute-done.15 = bf16[2,64,512]{2,1,0:T(8,128)(2,1)S(1)} collective-permute-done((bf16[2,64,512]{2,1,0:T(8,128)(2,1)S(1)}, bf16[2,64,512]{2,1,0:T(8,128)(2,1)S(1)}, u32[]{:S(2)}, u32[]{:S(2)}) %collective-permute-start.15) | collective-permute-done | bytes 131104 | tf_op jit(solution)/shard_map/ppermute | solution.py:16
  158.4 5.3 %collective-permute-done.16 = bf16[2,64,512]{2,1,0:T(8,128)(2,1)S(1)} collective-permute-done((bf16[2,64,512]{2,1,0:T(8,128)(2,1)S(1)}, bf16[2,64,512]{2,1,0:T(8,128)(2,1)S(1)}, u32[]{:S(2)}, u32[]{:S(2)}) %collective-permute-start.16) | collective-permute-done | bytes 131104 | tf_op jit(solution)/shard_map/ppermute | solution.py:16
  163.6 7.2 %collective-permute-done.17 = bf16[2,64,512]{2,1,0:T(8,128)(2,1)S(1)} collective-permute-done((bf16[2,64,512]{2,1,0:T(8,128)(2,1)S(1)}, bf16[2,64,512]{2,1,0:T(8,128)(2,1)S(1)}, u32[]{:S(2)}, u32[]{:S(2)}) %collective-permute-start.17) | collective-permute-done | bytes 131104 | tf_op jit(solution)/shard_map/ppermute | solution.py:16
  170.9 6.2 %collective-permute-done.18 = bf16[2,64,512]{2,1,0:T(8,128)(2,1)S(1)} collective-permute-done((bf16[2,64,512]{2,1,0:T(8,128)(2,1)S(1)}, bf16[2,64,512]{2,1,0:T(8,128)(2,1)S(1)}, u32[]{:S(2)}, u32[]{:S(2)}) %collective-permute-start.18) | collective-permute-done | bytes 131104 | tf_op jit(solution)/shard_map/ppermute | solution.py:16
  177.1 5.6 %collective-permute-done.19 = bf16[2,64,512]{2,1,0:T(8,128)(2,1)S(1)} collective-permute-done((bf16[2,64,512]{2,1,0:T(8,128)(2,1)S(1)}, bf16[2,64,512]{2,1,0:T(8,128)(2,1)S(1)}, u32[]{:S(2)}, u32[]{:S(2)}) %collective-permute-start.19) | collective-permute-done | bytes 131104 | tf_op jit(solution)/shard_map/ppermute | solution.py:16
  183.2 12.4 %collective-permute-done.22.refs_3_ = bf16[2,3,64,512]{3,2,1,0:T(8,128)(2,1)S(1)} collective-permute-done((bf16[2,3,64,512]{3,2,1,0:T(8,128)(2,1)S(1)}, bf16[2,3,64,512]{3,2,1,0:T(8,128)(2,1)S(1)}, u32[]{:S(2)}, u32[]{:S(2)}) %collective-permute-start.22) | collective-permute-done | bytes 393248 | tf_op jit(solution)/shard_map/ppermute | solution.py:16
  195.6 6.0 %collective-permute-done.21.refs_2_ = bf16[2,3,64,512]{3,2,1,0:T(8,128)(2,1)S(1)} collective-permute-done((bf16[2,3,64,512]{3,2,1,0:T(8,128)(2,1)S(1)}, bf16[2,3,64,512]{3,2,1,0:T(8,128)(2,1)S(1)}, u32[]{:S(2)}, u32[]{:S(2)}) %collective-permute-start.21) | collective-permute-done | bytes 393248 | tf_op jit(solution)/shard_map/ppermute | solution.py:16
  203.9 4.0 %left.1 = (bf16[1536,512]{1,0:T(8,128)(2,1)S(1)}, bf16[1536,512]{1,0:T(8,128)(2,1)S(1)}, f32[2,8,512]{2,1,0:T(8,128)S(1)}) custom-call(s32[3]{0:T(128)S(1)} %copy-done.1, bf16[512,512]{1,0:T(8,128)(2,1)S(1)} %bitcast.63, bf16[2,512,512]{2,1,0:T(8,128)(2,1)S(1)} %copy-done.2, f32[8,1536]{1,0:T(8,128)S(1)} %copy-done, ...), custom_call_target="tpu_custom_call" | custom-call | flops 2415919104 | bytes 9437184 | tf_op jit(solution)/shard_map/left/pallas_call | solution.py:173
  210.3 3.4 %collective-permute-start.28 = (f32[8,512]{1,0:T(8,128)S(1)}, f32[8,512]{1,0:T(8,128)S(1)}, u32[]{:S(2)}, u32[]{:S(2)}) collective-permute-start(f32[8,512]{1,0:T(8,128)S(1)} %pad_maximum_fusion.2), channel_id=1, source_target_pairs={{0,16},{8,24},{16,0},{24,8},{1,17},{9,25},{17,1},{25,9},{2,18},{10... | collective-permute-start | bytes 49160 | tf_op jit(solution)/shard_map/ppermute | solution.py:16
  215.5 3.1 %collective-permute-done.27 = f32[8,512]{1,0:T(8,128)S(1)} collective-permute-done((f32[8,512]{1,0:T(8,128)S(1)}, f32[8,512]{1,0:T(8,128)S(1)}, u32[]{:S(2)}, u32[]{:S(2)}) %collective-permute-start.27) | collective-permute-done | bytes 16416 | tf_op jit(solution)/shard_map/ppermute | solution.py:16
  218.7 4.6 %collective-permute-start.31 = (f32[8,512]{1,0:T(8,128)S(1)}, f32[8,512]{1,0:T(8,128)S(1)}, u32[]{:S(2)}, u32[]{:S(2)}) collective-permute-start(f32[8,512]{1,0:T(8,128)S(1)} %add_add_fusion.1), channel_id=1, source_target_pairs={{0,64},{32,96},{64,0},{96,32},{1,65},{33,97},{65,1},{97,33},{2,66}... | collective-permute-start | bytes 49160 | tf_op jit(solution)/shard_map/ppermute | solution.py:16
  225.0 3.2 %collective-permute-done.30 = f32[8,512]{1,0:T(8,128)S(1)} collective-permute-done((f32[8,512]{1,0:T(8,128)S(1)}, f32[8,512]{1,0:T(8,128)S(1)}, u32[]{:S(2)}, u32[]{:S(2)}) %collective-permute-start.30) | collective-permute-done | bytes 16416 | tf_op jit(solution)/shard_map/ppermute | solution.py:16
  229.6 18.4 %trail.1 = (bf16[3,6,512,512]{3,2,1,0:T(8,128)(2,1)}, f32[6,8,512]{2,1,0:T(8,128)}) custom-call(s32[3]{0:T(128)} %pad_add_fusion.info_ref, bf16[1536,512]{1,0:T(8,128)(2,1)} %copy-done.3, bf16[1536,512]{1,0:T(8,128)(2,1)} %copy-done.4, bf16[512,512]{1,0:T(8,128)(2,1)} %convolution_convert_fusion.second_ref, f32[2,8,512]{2,1,0:T(8,128)} %slice.56.sums_ref, ...), custom_call_target="tpu_custom_call" | custom-call | flops 12079595520 | bytes 18874368 | tf_op jit(solution)/shard_map/trail/pallas_call | solution.py:196
  (108 shorter events, 46.1 us)
Async XLA Ops:
  7.2 222.4 %all-gather.3.cloned.1.call-start = ((), (), s32[]{:S(2)}) async-start(), calls=%async_computation.1 | async-start | bytes 6684672 | tf_op jit(solution)/shard_map/all_gather | solution.py:132
  62.1 9.0 %collective-permute-start = (bf16[3,64,512]{2,1,0:T(8,128)(2,1)}, bf16[3,64,512]{2,1,0:T(8,128)(2,1)S(1)}, u32[]{:S(2)}, u32[]{:S(2)}) collective-permute-start(bf16[3,64,512]{2,1,0:T(8,128)(2,1)} %get-tuple-element.17), channel_id=1, source_target_pairs={{0,1},{1,2},{8,9},{9,10},{16,17},{17,18},{24,25},{25,26},{32,33},{... | collective-permute-start | bytes 589832 | tf_op jit(solution)/shard_map/ppermute | solution.py:16
  63.6 9.0 %collective-permute-start.1 = (bf16[3,64,512]{2,1,0:T(8,128)(2,1)}, bf16[3,64,512]{2,1,0:T(8,128)(2,1)S(1)}, u32[]{:S(2)}, u32[]{:S(2)}) collective-permute-start(bf16[3,64,512]{2,1,0:T(8,128)(2,1)} %get-tuple-element.18), channel_id=1, source_target_pairs={{0,2},{1,3},{8,10},{9,11},{16,18},{17,19},{24,26},{25,27},{32,34},... | collective-permute-start | bytes 589832 | tf_op jit(solution)/shard_map/ppermute | solution.py:16
  67.0 9.8 %collective-permute-start.2 = (bf16[3,64,512]{2,1,0:T(8,128)(2,1)}, bf16[3,64,512]{2,1,0:T(8,128)(2,1)S(1)}, u32[]{:S(2)}, u32[]{:S(2)}) collective-permute-start(bf16[3,64,512]{2,1,0:T(8,128)(2,1)} %get-tuple-element.19), channel_id=1, source_target_pairs={{0,3},{1,4},{8,11},{9,12},{16,19},{17,20},{24,27},{25,28},{32,35},... | collective-permute-start | bytes 589832 | tf_op jit(solution)/shard_map/ppermute | solution.py:16
  68.3 12.7 %collective-permute-start.3 = (bf16[3,64,512]{2,1,0:T(8,128)(2,1)}, bf16[3,64,512]{2,1,0:T(8,128)(2,1)S(1)}, u32[]{:S(2)}, u32[]{:S(2)}) collective-permute-start(bf16[3,64,512]{2,1,0:T(8,128)(2,1)} %get-tuple-element.20), channel_id=1, source_target_pairs={{0,4},{1,5},{8,12},{9,13},{16,20},{17,21},{24,28},{25,29},{32,36},... | collective-permute-start | bytes 589832 | tf_op jit(solution)/shard_map/ppermute | solution.py:16
  69.9 13.5 %collective-permute-start.4 = (bf16[3,64,512]{2,1,0:T(8,128)(2,1)}, bf16[3,64,512]{2,1,0:T(8,128)(2,1)S(1)}, u32[]{:S(2)}, u32[]{:S(2)}) collective-permute-start(bf16[3,64,512]{2,1,0:T(8,128)(2,1)} %get-tuple-element.21), channel_id=1, source_target_pairs={{0,5},{1,6},{8,13},{9,14},{16,21},{17,22},{24,29},{25,30},{32,37},... | collective-permute-start | bytes 589832 | tf_op jit(solution)/shard_map/ppermute | solution.py:16
  71.2 12.1 %collective-permute-start.5 = (bf16[3,64,512]{2,1,0:T(8,128)(2,1)}, bf16[3,64,512]{2,1,0:T(8,128)(2,1)S(1)}, u32[]{:S(2)}, u32[]{:S(2)}) collective-permute-start(bf16[3,64,512]{2,1,0:T(8,128)(2,1)} %get-tuple-element.22), channel_id=1, source_target_pairs={{0,6},{1,7},{8,14},{9,15},{16,22},{17,23},{24,30},{25,31},{32,38},... | collective-permute-start | bytes 589832 | tf_op jit(solution)/shard_map/ppermute | solution.py:16
  72.5 10.8 %collective-permute-start.6 = (bf16[3,64,512]{2,1,0:T(8,128)(2,1)}, bf16[3,64,512]{2,1,0:T(8,128)(2,1)S(1)}, u32[]{:S(2)}, u32[]{:S(2)}) collective-permute-start(bf16[3,64,512]{2,1,0:T(8,128)(2,1)} %get-tuple-element.23), channel_id=1, source_target_pairs={{0,7},{1,0},{8,15},{9,8},{16,23},{17,16},{24,31},{25,24},{32,39},{... | collective-permute-start | bytes 589832 | tf_op jit(solution)/shard_map/ppermute | solution.py:16
  83.5 7.2 %collective-permute-start.9 = (bf16[64,512]{1,0:T(8,128)(2,1)S(1)}, bf16[64,512]{1,0:T(8,128)(2,1)S(1)}, u32[]{:S(2)}, u32[]{:S(2)}) collective-permute-start(bf16[64,512]{1,0:T(8,128)(2,1)S(1)} %fusion.2), channel_id=1, source_target_pairs={{0,24},{8,0},{1,25},{9,1},{2,26},{10,2},{3,27},{11,3},{4,28},{12,4... | collective-permute-start | bytes 196616 | tf_op jit(solution)/shard_map/ppermute | solution.py:16
  94.0 9.7 %collective-permute-start.11 = (bf16[2,64,512]{2,1,0:T(8,128)(2,1)S(1)}, bf16[2,64,512]{2,1,0:T(8,128)(2,1)S(1)}, u32[]{:S(2)}, u32[]{:S(2)}) collective-permute-start(bf16[2,64,512]{2,1,0:T(8,128)(2,1)S(1)} %pad_maximum_fusion.1), channel_id=1, source_target_pairs={{0,64},{1,65},{2,66},{3,67},{4,68},{5,69},{6,70},{7,71},{8,72},{9,... | collective-permute-start | bytes 393224 | tf_op jit(solution)/shard_map/ppermute | solution.py:16
  97.0 6.7 %collective-permute-start.12 = (bf16[2,64,512]{2,1,0:T(8,128)(2,1)S(1)}, bf16[2,64,512]{2,1,0:T(8,128)(2,1)S(1)}, u32[]{:S(2)}, u32[]{:S(2)}) collective-permute-start(bf16[2,64,512]{2,1,0:T(8,128)(2,1)S(1)} %pad_maximum_fusion.1), channel_id=1, source_target_pairs={{0,96},{1,97},{2,98},{3,99},{4,100},{5,101},{6,102},{7,103},{8,104... | collective-permute-start | bytes 393224 | tf_op jit(solution)/shard_map/ppermute | solution.py:16
  98.3 9.7 %collective-permute-start.10 = (bf16[2,64,512]{2,1,0:T(8,128)(2,1)S(1)}, bf16[2,64,512]{2,1,0:T(8,128)(2,1)S(1)}, u32[]{:S(2)}, u32[]{:S(2)}) collective-permute-start(bf16[2,64,512]{2,1,0:T(8,128)(2,1)S(1)} %pad_maximum_fusion.1), channel_id=1, source_target_pairs={{0,32},{1,33},{2,34},{3,35},{4,36},{5,37},{6,38},{7,39},{8,40},{9,... | collective-permute-start | bytes 393224 | tf_op jit(solution)/shard_map/ppermute | solution.py:16
  108.0 14.1 %collective-permute-start.13 = (bf16[2,64,512]{2,1,0:T(8,128)(2,1)S(1)}, bf16[2,64,512]{2,1,0:T(8,128)(2,1)S(1)}, u32[]{:S(2)}, u32[]{:S(2)}) collective-permute-start(bf16[2,64,512]{2,1,0:T(8,128)(2,1)S(1)} %select_select_fusion.2), channel_id=1, source_target_pairs={{0,7},{1,0},{2,1},{3,2},{4,3},{5,4},{6,5},{7,6},{8,15},{9,8},{10,9... | collective-permute-start | bytes 393224 | tf_op jit(solution)/shard_map/ppermute | solution.py:16
  115.9 67.0 %collective-permute-start.26 = (bf16[2,3,64,512]{3,2,1,0:T(8,128)(2,1)S(1)}, bf16[2,3,64,512]{3,2,1,0:T(8,128)(2,1)S(1)}, u32[]{:S(2)}, u32[]{:S(2)}) collective-permute-start(bf16[2,3,64,512]{3,2,1,0:T(8,128)(2,1)S(1)} %pad_maximum_fusion.refs_0_), channel_id=1, source_target_pairs={{0,7},{1,0},{2,1},{3,2},{4,3},{5,4},{6,5},{7,6},{8,15},{9,8},{10,9... | collective-permute-start | bytes 1179656 | tf_op jit(solution)/shard_map/ppermute | solution.py:16
  115.9 67.0 %collective-permute-start.25 = (bf16[2,3,64,512]{3,2,1,0:T(8,128)(2,1)S(1)}, bf16[2,3,64,512]{3,2,1,0:T(8,128)(2,1)S(1)}, u32[]{:S(2)}, u32[]{:S(2)}) collective-permute-start(bf16[2,3,64,512]{3,2,1,0:T(8,128)(2,1)S(1)} %pad_maximum_fusion.refs_0_), channel_id=1, source_target_pairs={{0,6},{1,7},{2,0},{3,1},{4,2},{5,3},{6,4},{7,5},{8,14},{9,15},{10,... | collective-permute-start | bytes 1179656 | tf_op jit(solution)/shard_map/ppermute | solution.py:16
  118.9 64.3 %collective-permute-start.24 = (bf16[2,3,64,512]{3,2,1,0:T(8,128)(2,1)S(1)}, bf16[2,3,64,512]{3,2,1,0:T(8,128)(2,1)S(1)}, u32[]{:S(2)}, u32[]{:S(2)}) collective-permute-start(bf16[2,3,64,512]{3,2,1,0:T(8,128)(2,1)S(1)} %pad_maximum_fusion.refs_0_), channel_id=1, source_target_pairs={{0,5},{1,6},{2,7},{3,0},{4,1},{5,2},{6,3},{7,4},{8,13},{9,14},{10,... | collective-permute-start | bytes 1179656 | tf_op jit(solution)/shard_map/ppermute | solution.py:16
  118.9 64.3 %collective-permute-start.23 = (bf16[2,3,64,512]{3,2,1,0:T(8,128)(2,1)S(1)}, bf16[2,3,64,512]{3,2,1,0:T(8,128)(2,1)S(1)}, u32[]{:S(2)}, u32[]{:S(2)}) collective-permute-start(bf16[2,3,64,512]{3,2,1,0:T(8,128)(2,1)S(1)} %pad_maximum_fusion.refs_0_), channel_id=1, source_target_pairs={{0,4},{1,5},{2,6},{3,7},{4,0},{5,1},{6,2},{7,3},{8,12},{9,13},{10,... | collective-permute-start | bytes 1179656 | tf_op jit(solution)/shard_map/ppermute | solution.py:16
  122.2 29.2 %collective-permute-start.14 = (bf16[2,64,512]{2,1,0:T(8,128)(2,1)S(1)}, bf16[2,64,512]{2,1,0:T(8,128)(2,1)S(1)}, u32[]{:S(2)}, u32[]{:S(2)}) collective-permute-start(bf16[2,64,512]{2,1,0:T(8,128)(2,1)S(1)} %select_select_fusion.2), channel_id=1, source_target_pairs={{0,6},{1,7},{2,0},{3,1},{4,2},{5,3},{6,4},{7,5},{8,14},{9,15},{10,... | collective-permute-start | bytes 393224 | tf_op jit(solution)/shard_map/ppermute | solution.py:16
  156.7 6.9 %collective-permute-start.16 = (bf16[2,64,512]{2,1,0:T(8,128)(2,1)S(1)}, bf16[2,64,512]{2,1,0:T(8,128)(2,1)S(1)}, u32[]{:S(2)}, u32[]{:S(2)}) collective-permute-start(bf16[2,64,512]{2,1,0:T(8,128)(2,1)S(1)} %select_select_fusion.2), channel_id=1, source_target_pairs={{0,4},{1,5},{2,6},{3,7},{4,0},{5,1},{6,2},{7,3},{8,12},{9,13},{10,... | collective-permute-start | bytes 393224 | tf_op jit(solution)/shard_map/ppermute | solution.py:16
  163.6 7.3 %collective-permute-start.17 = (bf16[2,64,512]{2,1,0:T(8,128)(2,1)S(1)}, bf16[2,64,512]{2,1,0:T(8,128)(2,1)S(1)}, u32[]{:S(2)}, u32[]{:S(2)}) collective-permute-start(bf16[2,64,512]{2,1,0:T(8,128)(2,1)S(1)} %select_select_fusion.2), channel_id=1, source_target_pairs={{0,3},{1,4},{2,5},{3,6},{4,7},{5,0},{6,1},{7,2},{8,11},{9,12},{10,... | collective-permute-start | bytes 393224 | tf_op jit(solution)/shard_map/ppermute | solution.py:16
  182.7 12.9 %collective-permute-start.22 = (bf16[2,3,64,512]{3,2,1,0:T(8,128)(2,1)S(1)}, bf16[2,3,64,512]{3,2,1,0:T(8,128)(2,1)S(1)}, u32[]{:S(2)}, u32[]{:S(2)}) collective-permute-start(bf16[2,3,64,512]{3,2,1,0:T(8,128)(2,1)S(1)} %pad_maximum_fusion.refs_0_), channel_id=1, source_target_pairs={{0,3},{1,4},{2,5},{3,6},{4,7},{5,0},{6,1},{7,2},{8,11},{9,12},{10,... | collective-permute-start | bytes 1179656 | tf_op jit(solution)/shard_map/ppermute | solution.py:16
  182.9 18.7 %collective-permute-start.21 = (bf16[2,3,64,512]{3,2,1,0:T(8,128)(2,1)S(1)}, bf16[2,3,64,512]{3,2,1,0:T(8,128)(2,1)S(1)}, u32[]{:S(2)}, u32[]{:S(2)}) collective-permute-start(bf16[2,3,64,512]{3,2,1,0:T(8,128)(2,1)S(1)} %pad_maximum_fusion.refs_0_), channel_id=1, source_target_pairs={{0,2},{1,3},{2,4},{3,5},{4,6},{5,7},{6,0},{7,1},{8,10},{9,11},{10,... | collective-permute-start | bytes 1179656 | tf_op jit(solution)/shard_map/ppermute | solution.py:16
  183.0 20.9 %collective-permute-start.20 = (bf16[2,3,64,512]{3,2,1,0:T(8,128)(2,1)S(1)}, bf16[2,3,64,512]{3,2,1,0:T(8,128)(2,1)S(1)}, u32[]{:S(2)}, u32[]{:S(2)}) collective-permute-start(bf16[2,3,64,512]{3,2,1,0:T(8,128)(2,1)S(1)} %pad_maximum_fusion.refs_0_), channel_id=1, source_target_pairs={{0,1},{1,2},{2,3},{3,4},{4,5},{5,6},{6,7},{7,0},{8,9},{9,10},{10,1... | collective-permute-start | bytes 1179656 | tf_op jit(solution)/shard_map/ppermute | solution.py:16
  218.7 6.4 %collective-permute-start.31 = (f32[8,512]{1,0:T(8,128)S(1)}, f32[8,512]{1,0:T(8,128)S(1)}, u32[]{:S(2)}, u32[]{:S(2)}) collective-permute-start(f32[8,512]{1,0:T(8,128)S(1)} %add_add_fusion.1), channel_id=1, source_target_pairs={{0,64},{32,96},{64,0},{96,32},{1,65},{33,97},{65,1},{97,33},{2,66}... | collective-permute-start | bytes 49160 | tf_op jit(solution)/shard_map/ppermute | solution.py:16
  (17 other events, 170.4 us)
Sparse Core Ops, SparseCore 0:
  58.9 61.3 all-gather.2

commit v4 on v3

--- a/solution.py
+++ b/solution.py
@@ -78,7 +78,7 @@
 
 
 def trail_kernel(
-    info_ref, left0_ref, left1_ref, second_ref, sums_ref, upper_ref, band_ref, base_ref, tile_ref, out_ref, check_ref
+    info_ref, left0_ref, left1_ref, second_ref, own_ref, total_ref, upper_ref, band_ref, tile_ref, out_ref, check_ref, sum_ref
 ):
     width = second_ref.shape[0]
     first = pl.program_id(0) == 0
@@ -88,7 +88,15 @@
     upper1 = band_ref[...].reshape(width, width).astype(F32)
     upper1 = (upper1 - jnp.dot(second_ref[...], upper0, preferred_element_type=F32)).astype(BF16)
     upper1 = jnp.where(first & (my_col < 2), jnp.zeros_like(upper1), upper1)
-    check_ref[0] = base_ref[0] - times_rows(sums_ref[0], upper0) - times_rows(sums_ref[1], upper1)
+    here, cols = pl.program_id(0), pl.num_programs(0)
+
+    def both(index):
+        rows = [own_ref[pl.ds(index, 1), :], total_ref[pl.ds(index, 1), :]]
+        return jnp.concatenate(rows + [jnp.zeros((6, width), F32)], axis=0)
+
+    checks = both(here) - times_rows(both(cols), upper0) - times_rows(both(cols + 1), upper1)
+    check_ref[0] = checks[0:1]
+    sum_ref[pl.ds(here, 1), :] = checks[1:2]
     for a in range(tile_ref.shape[0]):
         rows = slice(a * width, (a + 1) * width)
         tile = tile_ref[a, 0].astype(F32) - jnp.dot(left0_ref[rows, :], upper0, preferred_element_type=F32)
@@ -190,29 +198,32 @@
     for axis in ("row_1", "row_0"):
         around = lambda s: [(i, (i + s) % sides) for i in range(sides)]
         total = functools.reduce(jnp.add, shifts(axis, [total] * sides, around))
-    pair = jnp.pad(jnp.stack([own, total], axis=1), ((0, 0), (0, 6), (0, 0)))
 
     whole = lambda *shape: pl.BlockSpec(shape, lambda c: (0,) * len(shape))
-    out, checks = pl.pallas_call(
+    out, checks, totals = pl.pallas_call(
         trail_kernel,
-        out_shape=(jax.ShapeDtypeStruct(tiles.shape, BF16), jax.ShapeDtypeStruct((cols, 8, block), F32)),
+        out_shape=(
+            jax.ShapeDtypeStruct(tiles.shape, BF16),
+            jax.ShapeDtypeStruct((cols, 1, block), F32),
+            jax.ShapeDtypeStruct((cols, block), F32),
+        ),
         grid=(cols,),
         in_specs=[
             smem,
             whole(rows, block),
             whole(rows, block),
             whole(block, block),
-            whole(2, 8, block),
+            whole(cols + 2, block),
+            whole(cols + 2, block),
             pl.BlockSpec((grid_rows, 1, piece, block), lambda c: (0, c, 0, 0)),
             pl.BlockSpec((grid_rows, 1, piece, block), lambda c: (0, c + cols, 0, 0)),
-            one_check,
             column_of_tiles,
         ],
-        out_specs=(column_of_tiles, one_check),
+        out_specs=(column_of_tiles, pl.BlockSpec((1, 1, block), lambda c: (c, 0, 0)), whole(cols, block)),
         cost_estimate=pl.CostEstimate(flops=5 * rows * block * block * cols, bytes_accessed=4 * tiles.size, transcendentals=0),
         name="trail",
-    )(info, left0, left1, second_left, pair[cols:], upper, upper, pair[:cols], tiles)
-    return out.transpose(0, 2, 1, 3), checks[None, :, 0], checks[:, 1]
+    )(info, left0, left1, second_left, own, total, upper, upper, tiles)
+    return out.transpose(0, 2, 1, 3), checks.transpose(1, 0, 2), totals
 
 
 def solution(mesh):

time: 258 us -> 255 us (0.988)
  local copies, waits for them, and re-layouts: 7.37 us -> 3.9 us
    slice x3 -> x0, local copies, waits for them, and re-layouts: 2.84 us -> none  [the longest x1 1.58 us: eliminate(): return (out.transpose(0, 2, 1, 3), checks[None, :, 0], checks[:, 1])]
where the time goes in v4:
time: 255 us; the launch traced here: 254 us
  waiting for transfers between devices  108 us (42%)
  blocking collectives  47.6 us (19%)
  starting transfers between devices  42.5 us (17%)
  Pallas kernels  35.2 us (14%)
  between operations  14.6 us (6%)
  local copies, waits for them, and re-layouts  3.9 us (2%)
    ppermute x33, waiting for transfers between devices, shifts(): lax.ppermute(p, axis, pairs(s))  108 us
    all_to_all x1, blocking collectives, eliminate(): bands = lax.all_to_all(bands, ROW, 0, 0)  47.6 us
    ppermute x33, starting transfers between devices, shifts(): lax.ppermute(p, axis, pairs(s))  42.5 us
    pallas_call x1, Pallas kernels, eliminate(): pl.pallas_call(trail_kernel, out_shape=(jax.ShapeDtypeStruct(tiles.shape,...  18.4 us
    pallas_call x1, Pallas kernels, eliminate(): pl.pallas_call(weigh_kernel, out_shape=jax.ShapeDtypeStruct((cols, 8, blo...  6.91 us
  transfers between devices with their start and end apart: 34, of which 20 were waited for; matrix products, arithmetic and copies ran while one was open for 2% of the time, Pallas kernels for 5%

profile of v4, /device:TPU:0, one launch (start us, length us, event | category | flops | bytes accessed | tf_op | source)
XLA Modules:
  0.0 254.1 jit_solution(4150056280529758782)
XLA Ops:
  7.2 3.2 %bands.1 = bf16[16,6,32,512]{3,2,1,0:T(8,128)(2,1)} custom-call(bf16[18,16,32,512]{3,2,1,0:T(8,128)(2,1)} %bitcast.59), custom_call_target="tpu_custom_call" | custom-call | flops 1572864 | bytes 6291456 | tf_op jit(solution)/shard_map/bands/pallas_call | solution.py:130
  10.4 47.6 %all_to_all.5 = bf16[16,6,32,512]{3,2,1,0:T(8,128)(2,1)S(1)} all-to-all(bf16[16,6,32,512]{3,2,1,0:T(8,128)(2,1)} %bands.1), channel_id=1, replica_groups=mesh['row_0'=4,'row_1'=4,'col'=8] {'row_0','row_1'}, dimensions={0} | all-to-all | bytes 6291456 | tf_op jit(solution)/shard_map/all_to_all | solution.py:139
  63.6 3.4 %collective-permute-start.1 = (bf16[3,64,512]{2,1,0:T(8,128)(2,1)}, bf16[3,64,512]{2,1,0:T(8,128)(2,1)S(1)}, u32[]{:S(2)}, u32[]{:S(2)}) collective-permute-start(bf16[3,64,512]{2,1,0:T(8,128)(2,1)} %get-tuple-element.19), channel_id=1, source_target_pairs={{0,2},{1,3},{8,10},{9,11},{16,18},{17,19},{24,26},{25,27},{32,34},... | collective-permute-start | bytes 589832 | tf_op jit(solution)/shard_map/ppermute | solution.py:16
  76.8 4.2 %collective-permute-done.3 = bf16[3,64,512]{2,1,0:T(8,128)(2,1)S(1)} collective-permute-done((bf16[3,64,512]{2,1,0:T(8,128)(2,1)}, bf16[3,64,512]{2,1,0:T(8,128)(2,1)S(1)}, u32[]{:S(2)}, u32[]{:S(2)}) %collective-permute-start.3) | collective-permute-done | bytes 196640 | tf_op jit(solution)/shard_map/ppermute | solution.py:16
  90.8 3.1 %collective-permute-done.7 = bf16[64,512]{1,0:T(8,128)(2,1)S(1)} collective-permute-done((bf16[64,512]{1,0:T(8,128)(2,1)S(1)}, bf16[64,512]{1,0:T(8,128)(2,1)S(1)}, u32[]{:S(2)}, u32[]{:S(2)}) %collective-permute-start.7) | collective-permute-done | bytes 65568 | tf_op jit(solution)/shard_map/ppermute | solution.py:16
  94.0 3.1 %collective-permute-start.11 = (bf16[2,64,512]{2,1,0:T(8,128)(2,1)S(1)}, bf16[2,64,512]{2,1,0:T(8,128)(2,1)S(1)}, u32[]{:S(2)}, u32[]{:S(2)}) collective-permute-start(bf16[2,64,512]{2,1,0:T(8,128)(2,1)S(1)} %pad_maximum_fusion.1), channel_id=1, source_target_pairs={{0,64},{1,65},{2,66},{3,67},{4,68},{5,69},{6,70},{7,71},{8,72},{9,... | collective-permute-start | bytes 393224 | tf_op jit(solution)/shard_map/ppermute | solution.py:16
  100.3 3.4 %collective-permute-done.11 = bf16[2,64,512]{2,1,0:T(8,128)(2,1)S(1)} collective-permute-done((bf16[2,64,512]{2,1,0:T(8,128)(2,1)S(1)}, bf16[2,64,512]{2,1,0:T(8,128)(2,1)S(1)}, u32[]{:S(2)}, u32[]{:S(2)}) %collective-permute-start.11) | collective-permute-done | bytes 131104 | tf_op jit(solution)/shard_map/ppermute | solution.py:16
  103.8 4.3 %collective-permute-done.10 = bf16[2,64,512]{2,1,0:T(8,128)(2,1)S(1)} collective-permute-done((bf16[2,64,512]{2,1,0:T(8,128)(2,1)S(1)}, bf16[2,64,512]{2,1,0:T(8,128)(2,1)S(1)}, u32[]{:S(2)}, u32[]{:S(2)}) %collective-permute-start.10) | collective-permute-done | bytes 131104 | tf_op jit(solution)/shard_map/ppermute | solution.py:16
  108.1 6.9 %weigh.1 = f32[6,8,512]{2,1,0:T(8,128)} custom-call(f32[8,1536]{1,0:T(8,128)} %pad.4.weight_ref, bf16[3,6,512,512]{3,2,1,0:T(8,128)(2,1)} %bitcast.61), custom_call_target="tpu_custom_call" | custom-call | flops 301989888 | bytes 9437184 | tf_op jit(solution)/shard_map/weigh/pallas_call | solution.py:171
  118.9 3.3 %collective-permute-start.23 = (bf16[2,3,64,512]{3,2,1,0:T(8,128)(2,1)S(1)}, bf16[2,3,64,512]{3,2,1,0:T(8,128)(2,1)S(1)}, u32[]{:S(2)}, u32[]{:S(2)}) collective-permute-start(bf16[2,3,64,512]{3,2,1,0:T(8,128)(2,1)S(1)} %pad_maximum_fusion.refs_0_), channel_id=1, source_target_pairs={{0,4},{1,5},{2,6},{3,7},{4,0},{5,1},{6,2},{7,3},{8,12},{9,13},{10,... | collective-permute-start | bytes 1179656 | tf_op jit(solution)/shard_map/ppermute | solution.py:16
  122.5 29.0 %collective-permute-done.14 = bf16[2,64,512]{2,1,0:T(8,128)(2,1)S(1)} collective-permute-done((bf16[2,64,512]{2,1,0:T(8,128)(2,1)S(1)}, bf16[2,64,512]{2,1,0:T(8,128)(2,1)S(1)}, u32[]{:S(2)}, u32[]{:S(2)}) %collective-permute-start.14) | collective-permute-done | bytes 131104 | tf_op jit(solution)/shard_map/ppermute | solution.py:16
  151.5 5.3 %collective-permute-done.15 = bf16[2,64,512]{2,1,0:T(8,128)(2,1)S(1)} collective-permute-done((bf16[2,64,512]{2,1,0:T(8,128)(2,1)S(1)}, bf16[2,64,512]{2,1,0:T(8,128)(2,1)S(1)}, u32[]{:S(2)}, u32[]{:S(2)}) %collective-permute-start.15) | collective-permute-done | bytes 131104 | tf_op jit(solution)/shard_map/ppermute | solution.py:16
  158.4 5.3 %collective-permute-done.16 = bf16[2,64,512]{2,1,0:T(8,128)(2,1)S(1)} collective-permute-done((bf16[2,64,512]{2,1,0:T(8,128)(2,1)S(1)}, bf16[2,64,512]{2,1,0:T(8,128)(2,1)S(1)}, u32[]{:S(2)}, u32[]{:S(2)}) %collective-permute-start.16) | collective-permute-done | bytes 131104 | tf_op jit(solution)/shard_map/ppermute | solution.py:16
  163.7 7.2 %collective-permute-done.17 = bf16[2,64,512]{2,1,0:T(8,128)(2,1)S(1)} collective-permute-done((bf16[2,64,512]{2,1,0:T(8,128)(2,1)S(1)}, bf16[2,64,512]{2,1,0:T(8,128)(2,1)S(1)}, u32[]{:S(2)}, u32[]{:S(2)}) %collective-permute-start.17) | collective-permute-done | bytes 131104 | tf_op jit(solution)/shard_map/ppermute | solution.py:16
  170.9 6.2 %collective-permute-done.18 = bf16[2,64,512]{2,1,0:T(8,128)(2,1)S(1)} collective-permute-done((bf16[2,64,512]{2,1,0:T(8,128)(2,1)S(1)}, bf16[2,64,512]{2,1,0:T(8,128)(2,1)S(1)}, u32[]{:S(2)}, u32[]{:S(2)}) %collective-permute-start.18) | collective-permute-done | bytes 131104 | tf_op jit(solution)/shard_map/ppermute | solution.py:16
  177.1 5.6 %collective-permute-done.19 = bf16[2,64,512]{2,1,0:T(8,128)(2,1)S(1)} collective-permute-done((bf16[2,64,512]{2,1,0:T(8,128)(2,1)S(1)}, bf16[2,64,512]{2,1,0:T(8,128)(2,1)S(1)}, u32[]{:S(2)}, u32[]{:S(2)}) %collective-permute-start.19) | collective-permute-done | bytes 131104 | tf_op jit(solution)/shard_map/ppermute | solution.py:16
  183.2 12.4 %collective-permute-done.22.refs_3_ = bf16[2,3,64,512]{3,2,1,0:T(8,128)(2,1)S(1)} collective-permute-done((bf16[2,3,64,512]{3,2,1,0:T(8,128)(2,1)S(1)}, bf16[2,3,64,512]{3,2,1,0:T(8,128)(2,1)S(1)}, u32[]{:S(2)}, u32[]{:S(2)}) %collective-permute-start.22) | collective-permute-done | bytes 393248 | tf_op jit(solution)/shard_map/ppermute | solution.py:16
  195.6 6.0 %collective-permute-done.21.refs_2_ = bf16[2,3,64,512]{3,2,1,0:T(8,128)(2,1)S(1)} collective-permute-done((bf16[2,3,64,512]{3,2,1,0:T(8,128)(2,1)S(1)}, bf16[2,3,64,512]{3,2,1,0:T(8,128)(2,1)S(1)}, u32[]{:S(2)}, u32[]{:S(2)}) %collective-permute-start.21) | collective-permute-done | bytes 393248 | tf_op jit(solution)/shard_map/ppermute | solution.py:16
  203.9 4.0 %left.1 = (bf16[1536,512]{1,0:T(8,128)(2,1)S(1)}, bf16[1536,512]{1,0:T(8,128)(2,1)S(1)}, f32[2,8,512]{2,1,0:T(8,128)S(1)}) custom-call(s32[3]{0:T(128)S(1)} %copy-done.1, bf16[512,512]{1,0:T(8,128)(2,1)S(1)} %bitcast.58, bf16[2,512,512]{2,1,0:T(8,128)(2,1)S(1)} %copy-done.2, f32[8,1536]{1,0:T(8,128)S(1)} %copy-done, ...), custom_call_target="tpu_custom_call" | custom-call | flops 2415919104 | bytes 9437184 | tf_op jit(solution)/shard_map/left/pallas_call | solution.py:181
  210.3 3.4 %collective-permute-start.28 = (f32[8,512]{1,0:T(8,128)S(1)}, f32[8,512]{1,0:T(8,128)S(1)}, u32[]{:S(2)}, u32[]{:S(2)}) collective-permute-start(f32[8,512]{1,0:T(8,128)S(1)} %pad_maximum_fusion.2.own_ref), channel_id=1, source_target_pairs={{0,16},{8,24},{16,0},{24,8},{1,17},{9,25},{17,1},{25,9},{2,18},{10... | collective-permute-start | bytes 49160 | tf_op jit(solution)/shard_map/ppermute | solution.py:16
  215.6 3.2 %collective-permute-done.27 = f32[8,512]{1,0:T(8,128)S(1)} collective-permute-done((f32[8,512]{1,0:T(8,128)S(1)}, f32[8,512]{1,0:T(8,128)S(1)}, u32[]{:S(2)}, u32[]{:S(2)}) %collective-permute-start.27) | collective-permute-done | bytes 16416 | tf_op jit(solution)/shard_map/ppermute | solution.py:16
  218.7 4.6 %collective-permute-start.31 = (f32[8,512]{1,0:T(8,128)S(1)}, f32[8,512]{1,0:T(8,128)S(1)}, u32[]{:S(2)}, u32[]{:S(2)}) collective-permute-start(f32[8,512]{1,0:T(8,128)S(1)} %add_add_fusion.1), channel_id=1, source_target_pairs={{0,64},{32,96},{64,0},{96,32},{1,65},{33,97},{65,1},{97,33},{2,66}... | collective-permute-start | bytes 49160 | tf_op jit(solution)/shard_map/ppermute | solution.py:16
  225.1 3.2 %collective-permute-done.30 = f32[8,512]{1,0:T(8,128)S(1)} collective-permute-done((f32[8,512]{1,0:T(8,128)S(1)}, f32[8,512]{1,0:T(8,128)S(1)}, u32[]{:S(2)}, u32[]{:S(2)}) %collective-permute-start.30) | collective-permute-done | bytes 16416 | tf_op jit(solution)/shard_map/ppermute | solution.py:16
  228.9 18.4 %trail.1 = (bf16[3,6,512,512]{3,2,1,0:T(8,128)(2,1)}, f32[6,1,512]{2,1,0:T(1,128)}, f32[6,512]{1,0:T(8,128)}) custom-call(s32[3]{0:T(128)} %pad_add_fusion.info_ref, bf16[1536,512]{1,0:T(8,128)(2,1)} %copy-done.3, bf16[1536,512]{1,0:T(8,128)(2,1)} %copy-done.4, bf16[512,512]{1,0:T(8,128)(2,1)} %convolution_convert_fusion.second_ref, f32[8,512]{1,0:T(8,128)} %copy-done.6, ...), custom_call_target="tpu_custom_call" | custom-call | flops 12079595520 | bytes 18874368 | tf_op jit(solution)/shard_map/trail/pallas_call | solution.py:203
  (103 shorter events, 43.3 us)
Async XLA Ops:
  7.2 221.8 %all-gather.3.cloned.1.call-start = ((), (), s32[]{:S(2)}) async-start(), calls=%async_computation.1 | async-start | bytes 6684672 | tf_op jit(solution)/shard_map/all_gather | solution.py:140
  62.2 9.0 %collective-permute-start = (bf16[3,64,512]{2,1,0:T(8,128)(2,1)}, bf16[3,64,512]{2,1,0:T(8,128)(2,1)S(1)}, u32[]{:S(2)}, u32[]{:S(2)}) collective-permute-start(bf16[3,64,512]{2,1,0:T(8,128)(2,1)} %get-tuple-element.18), channel_id=1, source_target_pairs={{0,1},{1,2},{8,9},{9,10},{16,17},{17,18},{24,25},{25,26},{32,33},{... | collective-permute-start | bytes 589832 | tf_op jit(solution)/shard_map/ppermute | solution.py:16
  63.6 9.0 %collective-permute-start.1 = (bf16[3,64,512]{2,1,0:T(8,128)(2,1)}, bf16[3,64,512]{2,1,0:T(8,128)(2,1)S(1)}, u32[]{:S(2)}, u32[]{:S(2)}) collective-permute-start(bf16[3,64,512]{2,1,0:T(8,128)(2,1)} %get-tuple-element.19), channel_id=1, source_target_pairs={{0,2},{1,3},{8,10},{9,11},{16,18},{17,19},{24,26},{25,27},{32,34},... | collective-permute-start | bytes 589832 | tf_op jit(solution)/shard_map/ppermute | solution.py:16
  67.0 9.8 %collective-permute-start.2 = (bf16[3,64,512]{2,1,0:T(8,128)(2,1)}, bf16[3,64,512]{2,1,0:T(8,128)(2,1)S(1)}, u32[]{:S(2)}, u32[]{:S(2)}) collective-permute-start(bf16[3,64,512]{2,1,0:T(8,128)(2,1)} %get-tuple-element.20), channel_id=1, source_target_pairs={{0,3},{1,4},{8,11},{9,12},{16,19},{17,20},{24,27},{25,28},{32,35},... | collective-permute-start | bytes 589832 | tf_op jit(solution)/shard_map/ppermute | solution.py:16
  68.3 12.7 %collective-permute-start.3 = (bf16[3,64,512]{2,1,0:T(8,128)(2,1)}, bf16[3,64,512]{2,1,0:T(8,128)(2,1)S(1)}, u32[]{:S(2)}, u32[]{:S(2)}) collective-permute-start(bf16[3,64,512]{2,1,0:T(8,128)(2,1)} %get-tuple-element.21), channel_id=1, source_target_pairs={{0,4},{1,5},{8,12},{9,13},{16,20},{17,21},{24,28},{25,29},{32,36},... | collective-permute-start | bytes 589832 | tf_op jit(solution)/shard_map/ppermute | solution.py:16
  69.9 13.5 %collective-permute-start.4 = (bf16[3,64,512]{2,1,0:T(8,128)(2,1)}, bf16[3,64,512]{2,1,0:T(8,128)(2,1)S(1)}, u32[]{:S(2)}, u32[]{:S(2)}) collective-permute-start(bf16[3,64,512]{2,1,0:T(8,128)(2,1)} %get-tuple-element.22), channel_id=1, source_target_pairs={{0,5},{1,6},{8,13},{9,14},{16,21},{17,22},{24,29},{25,30},{32,37},... | collective-permute-start | bytes 589832 | tf_op jit(solution)/shard_map/ppermute | solution.py:16
  71.2 12.1 %collective-permute-start.5 = (bf16[3,64,512]{2,1,0:T(8,128)(2,1)}, bf16[3,64,512]{2,1,0:T(8,128)(2,1)S(1)}, u32[]{:S(2)}, u32[]{:S(2)}) collective-permute-start(bf16[3,64,512]{2,1,0:T(8,128)(2,1)} %get-tuple-element.23), channel_id=1, source_target_pairs={{0,6},{1,7},{8,14},{9,15},{16,22},{17,23},{24,30},{25,31},{32,38},... | collective-permute-start | bytes 589832 | tf_op jit(solution)/shard_map/ppermute | solution.py:16
  72.6 10.8 %collective-permute-start.6 = (bf16[3,64,512]{2,1,0:T(8,128)(2,1)}, bf16[3,64,512]{2,1,0:T(8,128)(2,1)S(1)}, u32[]{:S(2)}, u32[]{:S(2)}) collective-permute-start(bf16[3,64,512]{2,1,0:T(8,128)(2,1)} %get-tuple-element.24), channel_id=1, source_target_pairs={{0,7},{1,0},{8,15},{9,8},{16,23},{17,16},{24,31},{25,24},{32,39},{... | collective-permute-start | bytes 589832 | tf_op jit(solution)/shard_map/ppermute | solution.py:16
  83.6 7.2 %collective-permute-start.9 = (bf16[64,512]{1,0:T(8,128)(2,1)S(1)}, bf16[64,512]{1,0:T(8,128)(2,1)S(1)}, u32[]{:S(2)}, u32[]{:S(2)}) collective-permute-start(bf16[64,512]{1,0:T(8,128)(2,1)S(1)} %fusion.2), channel_id=1, source_target_pairs={{0,24},{8,0},{1,25},{9,1},{2,26},{10,2},{3,27},{11,3},{4,28},{12,4... | collective-permute-start | bytes 196616 | tf_op jit(solution)/shard_map/ppermute | solution.py:16
  94.0 9.8 %collective-permute-start.11 = (bf16[2,64,512]{2,1,0:T(8,128)(2,1)S(1)}, bf16[2,64,512]{2,1,0:T(8,128)(2,1)S(1)}, u32[]{:S(2)}, u32[]{:S(2)}) collective-permute-start(bf16[2,64,512]{2,1,0:T(8,128)(2,1)S(1)} %pad_maximum_fusion.1), channel_id=1, source_target_pairs={{0,64},{1,65},{2,66},{3,67},{4,68},{5,69},{6,70},{7,71},{8,72},{9,... | collective-permute-start | bytes 393224 | tf_op jit(solution)/shard_map/ppermute | solution.py:16
  97.1 6.7 %collective-permute-start.12 = (bf16[2,64,512]{2,1,0:T(8,128)(2,1)S(1)}, bf16[2,64,512]{2,1,0:T(8,128)(2,1)S(1)}, u32[]{:S(2)}, u32[]{:S(2)}) collective-permute-start(bf16[2,64,512]{2,1,0:T(8,128)(2,1)S(1)} %pad_maximum_fusion.1), channel_id=1, source_target_pairs={{0,96},{1,97},{2,98},{3,99},{4,100},{5,101},{6,102},{7,103},{8,104... | collective-permute-start | bytes 393224 | tf_op jit(solution)/shard_map/ppermute | solution.py:16
  98.4 9.7 %collective-permute-start.10 = (bf16[2,64,512]{2,1,0:T(8,128)(2,1)S(1)}, bf16[2,64,512]{2,1,0:T(8,128)(2,1)S(1)}, u32[]{:S(2)}, u32[]{:S(2)}) collective-permute-start(bf16[2,64,512]{2,1,0:T(8,128)(2,1)S(1)} %pad_maximum_fusion.1), channel_id=1, source_target_pairs={{0,32},{1,33},{2,34},{3,35},{4,36},{5,37},{6,38},{7,39},{8,40},{9,... | collective-permute-start | bytes 393224 | tf_op jit(solution)/shard_map/ppermute | solution.py:16
  108.1 14.1 %collective-permute-start.13 = (bf16[2,64,512]{2,1,0:T(8,128)(2,1)S(1)}, bf16[2,64,512]{2,1,0:T(8,128)(2,1)S(1)}, u32[]{:S(2)}, u32[]{:S(2)}) collective-permute-start(bf16[2,64,512]{2,1,0:T(8,128)(2,1)S(1)} %select_select_fusion.2), channel_id=1, source_target_pairs={{0,7},{1,0},{2,1},{3,2},{4,3},{5,4},{6,5},{7,6},{8,15},{9,8},{10,9... | collective-permute-start | bytes 393224 | tf_op jit(solution)/shard_map/ppermute | solution.py:16
  116.0 66.9 %collective-permute-start.26 = (bf16[2,3,64,512]{3,2,1,0:T(8,128)(2,1)S(1)}, bf16[2,3,64,512]{3,2,1,0:T(8,128)(2,1)S(1)}, u32[]{:S(2)}, u32[]{:S(2)}) collective-permute-start(bf16[2,3,64,512]{3,2,1,0:T(8,128)(2,1)S(1)} %pad_maximum_fusion.refs_0_), channel_id=1, source_target_pairs={{0,7},{1,0},{2,1},{3,2},{4,3},{5,4},{6,5},{7,6},{8,15},{9,8},{10,9... | collective-permute-start | bytes 1179656 | tf_op jit(solution)/shard_map/ppermute | solution.py:16
  116.0 67.0 %collective-permute-start.25 = (bf16[2,3,64,512]{3,2,1,0:T(8,128)(2,1)S(1)}, bf16[2,3,64,512]{3,2,1,0:T(8,128)(2,1)S(1)}, u32[]{:S(2)}, u32[]{:S(2)}) collective-permute-start(bf16[2,3,64,512]{3,2,1,0:T(8,128)(2,1)S(1)} %pad_maximum_fusion.refs_0_), channel_id=1, source_target_pairs={{0,6},{1,7},{2,0},{3,1},{4,2},{5,3},{6,4},{7,5},{8,14},{9,15},{10,... | collective-permute-start | bytes 1179656 | tf_op jit(solution)/shard_map/ppermute | solution.py:16
  118.9 64.3 %collective-permute-start.24 = (bf16[2,3,64,512]{3,2,1,0:T(8,128)(2,1)S(1)}, bf16[2,3,64,512]{3,2,1,0:T(8,128)(2,1)S(1)}, u32[]{:S(2)}, u32[]{:S(2)}) collective-permute-start(bf16[2,3,64,512]{3,2,1,0:T(8,128)(2,1)S(1)} %pad_maximum_fusion.refs_0_), channel_id=1, source_target_pairs={{0,5},{1,6},{2,7},{3,0},{4,1},{5,2},{6,3},{7,4},{8,13},{9,14},{10,... | collective-permute-start | bytes 1179656 | tf_op jit(solution)/shard_map/ppermute | solution.py:16
  118.9 64.3 %collective-permute-start.23 = (bf16[2,3,64,512]{3,2,1,0:T(8,128)(2,1)S(1)}, bf16[2,3,64,512]{3,2,1,0:T(8,128)(2,1)S(1)}, u32[]{:S(2)}, u32[]{:S(2)}) collective-permute-start(bf16[2,3,64,512]{3,2,1,0:T(8,128)(2,1)S(1)} %pad_maximum_fusion.refs_0_), channel_id=1, source_target_pairs={{0,4},{1,5},{2,6},{3,7},{4,0},{5,1},{6,2},{7,3},{8,12},{9,13},{10,... | collective-permute-start | bytes 1179656 | tf_op jit(solution)/shard_map/ppermute | solution.py:16
  122.2 29.3 %collective-permute-start.14 = (bf16[2,64,512]{2,1,0:T(8,128)(2,1)S(1)}, bf16[2,64,512]{2,1,0:T(8,128)(2,1)S(1)}, u32[]{:S(2)}, u32[]{:S(2)}) collective-permute-start(bf16[2,64,512]{2,1,0:T(8,128)(2,1)S(1)} %select_select_fusion.2), channel_id=1, source_target_pairs={{0,6},{1,7},{2,0},{3,1},{4,2},{5,3},{6,4},{7,5},{8,14},{9,15},{10,... | collective-permute-start | bytes 393224 | tf_op jit(solution)/shard_map/ppermute | solution.py:16
  156.8 6.9 %collective-permute-start.16 = (bf16[2,64,512]{2,1,0:T(8,128)(2,1)S(1)}, bf16[2,64,512]{2,1,0:T(8,128)(2,1)S(1)}, u32[]{:S(2)}, u32[]{:S(2)}) collective-permute-start(bf16[2,64,512]{2,1,0:T(8,128)(2,1)S(1)} %select_select_fusion.2), channel_id=1, source_target_pairs={{0,4},{1,5},{2,6},{3,7},{4,0},{5,1},{6,2},{7,3},{8,12},{9,13},{10,... | collective-permute-start | bytes 393224 | tf_op jit(solution)/shard_map/ppermute | solution.py:16
  163.7 7.2 %collective-permute-start.17 = (bf16[2,64,512]{2,1,0:T(8,128)(2,1)S(1)}, bf16[2,64,512]{2,1,0:T(8,128)(2,1)S(1)}, u32[]{:S(2)}, u32[]{:S(2)}) collective-permute-start(bf16[2,64,512]{2,1,0:T(8,128)(2,1)S(1)} %select_select_fusion.2), channel_id=1, source_target_pairs={{0,3},{1,4},{2,5},{3,6},{4,7},{5,0},{6,1},{7,2},{8,11},{9,12},{10,... | collective-permute-start | bytes 393224 | tf_op jit(solution)/shard_map/ppermute | solution.py:16
  182.7 12.9 %collective-permute-start.22 = (bf16[2,3,64,512]{3,2,1,0:T(8,128)(2,1)S(1)}, bf16[2,3,64,512]{3,2,1,0:T(8,128)(2,1)S(1)}, u32[]{:S(2)}, u32[]{:S(2)}) collective-permute-start(bf16[2,3,64,512]{3,2,1,0:T(8,128)(2,1)S(1)} %pad_maximum_fusion.refs_0_), channel_id=1, source_target_pairs={{0,3},{1,4},{2,5},{3,6},{4,7},{5,0},{6,1},{7,2},{8,11},{9,12},{10,... | collective-permute-start | bytes 1179656 | tf_op jit(solution)/shard_map/ppermute | solution.py:16
  182.9 18.7 %collective-permute-start.21 = (bf16[2,3,64,512]{3,2,1,0:T(8,128)(2,1)S(1)}, bf16[2,3,64,512]{3,2,1,0:T(8,128)(2,1)S(1)}, u32[]{:S(2)}, u32[]{:S(2)}) collective-permute-start(bf16[2,3,64,512]{3,2,1,0:T(8,128)(2,1)S(1)} %pad_maximum_fusion.refs_0_), channel_id=1, source_target_pairs={{0,2},{1,3},{2,4},{3,5},{4,6},{5,7},{6,0},{7,1},{8,10},{9,11},{10,... | collective-permute-start | bytes 1179656 | tf_op jit(solution)/shard_map/ppermute | solution.py:16
  183.0 20.9 %collective-permute-start.20 = (bf16[2,3,64,512]{3,2,1,0:T(8,128)(2,1)S(1)}, bf16[2,3,64,512]{3,2,1,0:T(8,128)(2,1)S(1)}, u32[]{:S(2)}, u32[]{:S(2)}) collective-permute-start(bf16[2,3,64,512]{3,2,1,0:T(8,128)(2,1)S(1)} %pad_maximum_fusion.refs_0_), channel_id=1, source_target_pairs={{0,1},{1,2},{2,3},{3,4},{4,5},{5,6},{6,7},{7,0},{8,9},{9,10},{10,1... | collective-permute-start | bytes 1179656 | tf_op jit(solution)/shard_map/ppermute | solution.py:16
  218.7 6.3 %collective-permute-start.31 = (f32[8,512]{1,0:T(8,128)S(1)}, f32[8,512]{1,0:T(8,128)S(1)}, u32[]{:S(2)}, u32[]{:S(2)}) collective-permute-start(f32[8,512]{1,0:T(8,128)S(1)} %add_add_fusion.1), channel_id=1, source_target_pairs={{0,64},{32,96},{64,0},{96,32},{1,65},{33,97},{65,1},{97,33},{2,66}... | collective-permute-start | bytes 49160 | tf_op jit(solution)/shard_map/ppermute | solution.py:16
  (18 other events, 190.1 us)
Sparse Core Ops, SparseCore 0:
  58.9 61.3 all-gather.2

commit v5 on v4

--- a/solution.py
+++ b/solution.py
@@ -78,31 +78,46 @@
 
 
 def trail_kernel(
-    info_ref, left0_ref, left1_ref, second_ref, own_ref, total_ref, upper_ref, band_ref, tile_ref, out_ref, check_ref, sum_ref
+    info_ref, left0_ref, left1_ref, second_ref, own_ref, total_ref, upper_ref, band_ref, tile_ref,
+    out_ref, check_ref, sum_ref, longer0_ref, longer1_ref
 ):
     width = second_ref.shape[0]
     first = pl.program_id(0) == 0
     my_col, my_row = info_ref[0], info_ref[1]
-    upper0 = upper_ref[...].reshape(width, width)
-    upper0 = jnp.where(first & (my_col == 0), jnp.zeros_like(upper0), upper0)
-    upper1 = band_ref[...].reshape(width, width).astype(F32)
-    upper1 = (upper1 - jnp.dot(second_ref[...], upper0, preferred_element_type=F32)).astype(BF16)
-    upper1 = jnp.where(first & (my_col < 2), jnp.zeros_like(upper1), upper1)
-    here, cols = pl.program_id(0), pl.num_programs(0)
+    here, cols, last = pl.program_id(0), pl.num_programs(0), tile_ref.shape[0] - 1
 
     def both(index):
         rows = [own_ref[pl.ds(index, 1), :], total_ref[pl.ds(index, 1), :]]
         return jnp.concatenate(rows + [jnp.zeros((6, width), F32)], axis=0)
 
-    checks = both(here) - times_rows(both(cols), upper0) - times_rows(both(cols + 1), upper1)
-    check_ref[0] = checks[0:1]
-    sum_ref[pl.ds(here, 1), :] = checks[1:2]
-    for a in range(tile_ref.shape[0]):
+    @pl.when(first)
+    def _():
+        longer0_ref[:width] = second_ref[...]
+        longer0_ref[width:] = in_three(both(cols))
+        longer1_ref[:width] = left1_ref[last * width :, :]
+        longer1_ref[width:] = in_three(both(cols + 1))
+
+    def split(product):
+        rows = product[width:]
+        return product[:width], rows[0:8] + rows[8:16] + rows[16:24]
+
+    upper0 = upper_ref[...].reshape(width, width)
+    upper0 = jnp.where(first & (my_col == 0), jnp.zeros_like(upper0), upper0)
+    product, checks0 = split(jnp.dot(longer0_ref[...], upper0, preferred_element_type=F32))
+    upper1 = (band_ref[...].reshape(width, width).astype(F32) - product).astype(BF16)
+    upper1 = jnp.where(first & (my_col < 2), jnp.zeros_like(upper1), upper1)
+    for a in range(last + 1):
         rows = slice(a * width, (a + 1) * width)
         tile = tile_ref[a, 0].astype(F32) - jnp.dot(left0_ref[rows, :], upper0, preferred_element_type=F32)
         tile = tile.astype(BF16).astype(F32)
-        tile = tile - jnp.dot(left1_ref[rows, :], upper1, preferred_element_type=F32)
-        out_ref[a, 0] = tile.astype(BF16)
+        if a < last:
+            product = jnp.dot(left1_ref[rows, :], upper1, preferred_element_type=F32)
+        else:
+            product, checks1 = split(jnp.dot(longer1_ref[...], upper1, preferred_element_type=F32))
+        out_ref[a, 0] = (tile - product).astype(BF16)
+    checks = both(here) - checks0 - checks1
+    check_ref[0] = checks[0:1]
+    sum_ref[pl.ds(here, 1), :] = checks[1:2]
     for a in range(tile_ref.shape[0]):
         for pivot, left_ref in enumerate((left0_ref, left1_ref)):
             below = True if a > 0 else my_row > pivot
@@ -220,6 +235,7 @@
             column_of_tiles,
         ],
         out_specs=(column_of_tiles, pl.BlockSpec((1, 1, block), lambda c: (c, 0, 0)), whole(cols, block)),
+        scratch_shapes=[pltpu.VMEM((block + 32, block), BF16)] * 2,
         cost_estimate=pl.CostEstimate(flops=5 * rows * block * block * cols, bytes_accessed=4 * tiles.size, transcendentals=0),
         name="trail",
     )(info, left0, left1, second_left, own, total, upper, upper, tiles)

time: 255 us -> 254 us (level)
  no operation moved by 1% of the time
where the time goes in v5:
time: 254 us; the launch traced here: 253 us
  waiting for transfers between devices  108 us (43%)
  blocking collectives  47.6 us (19%)
  starting transfers between devices  42.5 us (17%)
  Pallas kernels  34.3 us (14%)
  between operations  14.6 us (6%)
  local copies, waits for them, and re-layouts  3.9 us (2%)
    ppermute x33, waiting for transfers between devices, shifts(): lax.ppermute(p, axis, pairs(s))  108 us
    all_to_all x1, blocking collectives, eliminate(): bands = lax.all_to_all(bands, ROW, 0, 0)  47.6 us
    ppermute x33, starting transfers between devices, shifts(): lax.ppermute(p, axis, pairs(s))  42.5 us
    pallas_call x1, Pallas kernels, eliminate(): pl.pallas_call(trail_kernel, out_shape=(jax.ShapeDtypeStruct(tiles.shape,...  17.5 us
    pallas_call x1, Pallas kernels, eliminate(): pl.pallas_call(weigh_kernel, out_shape=jax.ShapeDtypeStruct((cols, 8, blo...  6.91 us
  transfers between devices with their start and end apart: 34, of which 20 were waited for; matrix products, arithmetic and copies ran while one was open for 2% of the time, Pallas kernels for 5%

profile of v5, /device:TPU:0, one launch (start us, length us, event | category | flops | bytes accessed | tf_op | source)
XLA Modules:
  0.0 253.2 jit_solution(15325364834711769277)
XLA Ops:
  7.2 3.2 %bands.1 = bf16[16,6,32,512]{3,2,1,0:T(8,128)(2,1)} custom-call(bf16[18,16,32,512]{3,2,1,0:T(8,128)(2,1)} %bitcast.59), custom_call_target="tpu_custom_call" | custom-call | flops 1572864 | bytes 6291456 | tf_op jit(solution)/shard_map/bands/pallas_call | solution.py:145
  10.4 47.6 %all_to_all.5 = bf16[16,6,32,512]{3,2,1,0:T(8,128)(2,1)S(1)} all-to-all(bf16[16,6,32,512]{3,2,1,0:T(8,128)(2,1)} %bands.1), channel_id=1, replica_groups=mesh['row_0'=4,'row_1'=4,'col'=8] {'row_0','row_1'}, dimensions={0} | all-to-all | bytes 6291456 | tf_op jit(solution)/shard_map/all_to_all | solution.py:154
  63.6 3.4 %collective-permute-start.1 = (bf16[3,64,512]{2,1,0:T(8,128)(2,1)}, bf16[3,64,512]{2,1,0:T(8,128)(2,1)S(1)}, u32[]{:S(2)}, u32[]{:S(2)}) collective-permute-start(bf16[3,64,512]{2,1,0:T(8,128)(2,1)} %get-tuple-element.19), channel_id=1, source_target_pairs={{0,2},{1,3},{8,10},{9,11},{16,18},{17,19},{24,26},{25,27},{32,34},... | collective-permute-start | bytes 589832 | tf_op jit(solution)/shard_map/ppermute | solution.py:16
  76.8 4.2 %collective-permute-done.3 = bf16[3,64,512]{2,1,0:T(8,128)(2,1)S(1)} collective-permute-done((bf16[3,64,512]{2,1,0:T(8,128)(2,1)}, bf16[3,64,512]{2,1,0:T(8,128)(2,1)S(1)}, u32[]{:S(2)}, u32[]{:S(2)}) %collective-permute-start.3) | collective-permute-done | bytes 196640 | tf_op jit(solution)/shard_map/ppermute | solution.py:16
  90.8 3.1 %collective-permute-done.7 = bf16[64,512]{1,0:T(8,128)(2,1)S(1)} collective-permute-done((bf16[64,512]{1,0:T(8,128)(2,1)S(1)}, bf16[64,512]{1,0:T(8,128)(2,1)S(1)}, u32[]{:S(2)}, u32[]{:S(2)}) %collective-permute-start.7) | collective-permute-done | bytes 65568 | tf_op jit(solution)/shard_map/ppermute | solution.py:16
  94.0 3.1 %collective-permute-start.11 = (bf16[2,64,512]{2,1,0:T(8,128)(2,1)S(1)}, bf16[2,64,512]{2,1,0:T(8,128)(2,1)S(1)}, u32[]{:S(2)}, u32[]{:S(2)}) collective-permute-start(bf16[2,64,512]{2,1,0:T(8,128)(2,1)S(1)} %pad_maximum_fusion.1), channel_id=1, source_target_pairs={{0,64},{1,65},{2,66},{3,67},{4,68},{5,69},{6,70},{7,71},{8,72},{9,... | collective-permute-start | bytes 393224 | tf_op jit(solution)/shard_map/ppermute | solution.py:16
  100.3 3.4 %collective-permute-done.11 = bf16[2,64,512]{2,1,0:T(8,128)(2,1)S(1)} collective-permute-done((bf16[2,64,512]{2,1,0:T(8,128)(2,1)S(1)}, bf16[2,64,512]{2,1,0:T(8,128)(2,1)S(1)}, u32[]{:S(2)}, u32[]{:S(2)}) %collective-permute-start.11) | collective-permute-done | bytes 131104 | tf_op jit(solution)/shard_map/ppermute | solution.py:16
  103.8 4.3 %collective-permute-done.10 = bf16[2,64,512]{2,1,0:T(8,128)(2,1)S(1)} collective-permute-done((bf16[2,64,512]{2,1,0:T(8,128)(2,1)S(1)}, bf16[2,64,512]{2,1,0:T(8,128)(2,1)S(1)}, u32[]{:S(2)}, u32[]{:S(2)}) %collective-permute-start.10) | collective-permute-done | bytes 131104 | tf_op jit(solution)/shard_map/ppermute | solution.py:16
  108.1 6.9 %weigh.1 = f32[6,8,512]{2,1,0:T(8,128)} custom-call(f32[8,1536]{1,0:T(8,128)} %pad.4.weight_ref, bf16[3,6,512,512]{3,2,1,0:T(8,128)(2,1)} %bitcast.61), custom_call_target="tpu_custom_call" | custom-call | flops 301989888 | bytes 9437184 | tf_op jit(solution)/shard_map/weigh/pallas_call | solution.py:186
  118.9 3.3 %collective-permute-start.23 = (bf16[2,3,64,512]{3,2,1,0:T(8,128)(2,1)S(1)}, bf16[2,3,64,512]{3,2,1,0:T(8,128)(2,1)S(1)}, u32[]{:S(2)}, u32[]{:S(2)}) collective-permute-start(bf16[2,3,64,512]{3,2,1,0:T(8,128)(2,1)S(1)} %pad_maximum_fusion.refs_0_), channel_id=1, source_target_pairs={{0,4},{1,5},{2,6},{3,7},{4,0},{5,1},{6,2},{7,3},{8,12},{9,13},{10,... | collective-permute-start | bytes 1179656 | tf_op jit(solution)/shard_map/ppermute | solution.py:16
  122.5 29.0 %collective-permute-done.14 = bf16[2,64,512]{2,1,0:T(8,128)(2,1)S(1)} collective-permute-done((bf16[2,64,512]{2,1,0:T(8,128)(2,1)S(1)}, bf16[2,64,512]{2,1,0:T(8,128)(2,1)S(1)}, u32[]{:S(2)}, u32[]{:S(2)}) %collective-permute-start.14) | collective-permute-done | bytes 131104 | tf_op jit(solution)/shard_map/ppermute | solution.py:16
  151.5 5.3 %collective-permute-done.15 = bf16[2,64,512]{2,1,0:T(8,128)(2,1)S(1)} collective-permute-done((bf16[2,64,512]{2,1,0:T(8,128)(2,1)S(1)}, bf16[2,64,512]{2,1,0:T(8,128)(2,1)S(1)}, u32[]{:S(2)}, u32[]{:S(2)}) %collective-permute-start.15) | collective-permute-done | bytes 131104 | tf_op jit(solution)/shard_map/ppermute | solution.py:16
  158.4 5.3 %collective-permute-done.16 = bf16[2,64,512]{2,1,0:T(8,128)(2,1)S(1)} collective-permute-done((bf16[2,64,512]{2,1,0:T(8,128)(2,1)S(1)}, bf16[2,64,512]{2,1,0:T(8,128)(2,1)S(1)}, u32[]{:S(2)}, u32[]{:S(2)}) %collective-permute-start.16) | collective-permute-done | bytes 131104 | tf_op jit(solution)/shard_map/ppermute | solution.py:16
  163.7 7.2 %collective-permute-done.17 = bf16[2,64,512]{2,1,0:T(8,128)(2,1)S(1)} collective-permute-done((bf16[2,64,512]{2,1,0:T(8,128)(2,1)S(1)}, bf16[2,64,512]{2,1,0:T(8,128)(2,1)S(1)}, u32[]{:S(2)}, u32[]{:S(2)}) %collective-permute-start.17) | collective-permute-done | bytes 131104 | tf_op jit(solution)/shard_map/ppermute | solution.py:16
  170.9 6.2 %collective-permute-done.18 = bf16[2,64,512]{2,1,0:T(8,128)(2,1)S(1)} collective-permute-done((bf16[2,64,512]{2,1,0:T(8,128)(2,1)S(1)}, bf16[2,64,512]{2,1,0:T(8,128)(2,1)S(1)}, u32[]{:S(2)}, u32[]{:S(2)}) %collective-permute-start.18) | collective-permute-done | bytes 131104 | tf_op jit(solution)/shard_map/ppermute | solution.py:16
  177.1 5.6 %collective-permute-done.19 = bf16[2,64,512]{2,1,0:T(8,128)(2,1)S(1)} collective-permute-done((bf16[2,64,512]{2,1,0:T(8,128)(2,1)S(1)}, bf16[2,64,512]{2,1,0:T(8,128)(2,1)S(1)}, u32[]{:S(2)}, u32[]{:S(2)}) %collective-permute-start.19) | collective-permute-done | bytes 131104 | tf_op jit(solution)/shard_map/ppermute | solution.py:16
  183.2 12.4 %collective-permute-done.22.refs_3_ = bf16[2,3,64,512]{3,2,1,0:T(8,128)(2,1)S(1)} collective-permute-done((bf16[2,3,64,512]{3,2,1,0:T(8,128)(2,1)S(1)}, bf16[2,3,64,512]{3,2,1,0:T(8,128)(2,1)S(1)}, u32[]{:S(2)}, u32[]{:S(2)}) %collective-permute-start.22) | collective-permute-done | bytes 393248 | tf_op jit(solution)/shard_map/ppermute | solution.py:16
  195.6 6.0 %collective-permute-done.21.refs_2_ = bf16[2,3,64,512]{3,2,1,0:T(8,128)(2,1)S(1)} collective-permute-done((bf16[2,3,64,512]{3,2,1,0:T(8,128)(2,1)S(1)}, bf16[2,3,64,512]{3,2,1,0:T(8,128)(2,1)S(1)}, u32[]{:S(2)}, u32[]{:S(2)}) %collective-permute-start.21) | collective-permute-done | bytes 393248 | tf_op jit(solution)/shard_map/ppermute | solution.py:16
  203.9 4.0 %left.1 = (bf16[1536,512]{1,0:T(8,128)(2,1)S(1)}, bf16[1536,512]{1,0:T(8,128)(2,1)S(1)}, f32[2,8,512]{2,1,0:T(8,128)S(1)}) custom-call(s32[3]{0:T(128)S(1)} %copy-done.1, bf16[512,512]{1,0:T(8,128)(2,1)S(1)} %bitcast.58, bf16[2,512,512]{2,1,0:T(8,128)(2,1)S(1)} %copy-done.2, f32[8,1536]{1,0:T(8,128)S(1)} %copy-done, ...), custom_call_target="tpu_custom_call" | custom-call | flops 2415919104 | bytes 9437184 | tf_op jit(solution)/shard_map/left/pallas_call | solution.py:196
  210.3 3.4 %collective-permute-start.28 = (f32[8,512]{1,0:T(8,128)S(1)}, f32[8,512]{1,0:T(8,128)S(1)}, u32[]{:S(2)}, u32[]{:S(2)}) collective-permute-start(f32[8,512]{1,0:T(8,128)S(1)} %pad_maximum_fusion.2.own_ref), channel_id=1, source_target_pairs={{0,16},{8,24},{16,0},{24,8},{1,17},{9,25},{17,1},{25,9},{2,18},{10... | collective-permute-start | bytes 49160 | tf_op jit(solution)/shard_map/ppermute | solution.py:16
  215.6 3.2 %collective-permute-done.27 = f32[8,512]{1,0:T(8,128)S(1)} collective-permute-done((f32[8,512]{1,0:T(8,128)S(1)}, f32[8,512]{1,0:T(8,128)S(1)}, u32[]{:S(2)}, u32[]{:S(2)}) %collective-permute-start.27) | collective-permute-done | bytes 16416 | tf_op jit(solution)/shard_map/ppermute | solution.py:16
  218.7 4.6 %collective-permute-start.31 = (f32[8,512]{1,0:T(8,128)S(1)}, f32[8,512]{1,0:T(8,128)S(1)}, u32[]{:S(2)}, u32[]{:S(2)}) collective-permute-start(f32[8,512]{1,0:T(8,128)S(1)} %add_add_fusion.1), channel_id=1, source_target_pairs={{0,64},{32,96},{64,0},{96,32},{1,65},{33,97},{65,1},{97,33},{2,66}... | collective-permute-start | bytes 49160 | tf_op jit(solution)/shard_map/ppermute | solution.py:16
  225.1 3.2 %collective-permute-done.30 = f32[8,512]{1,0:T(8,128)S(1)} collective-permute-done((f32[8,512]{1,0:T(8,128)S(1)}, f32[8,512]{1,0:T(8,128)S(1)}, u32[]{:S(2)}, u32[]{:S(2)}) %collective-permute-start.30) | collective-permute-done | bytes 16416 | tf_op jit(solution)/shard_map/ppermute | solution.py:16
  228.9 17.5 %trail.1 = (bf16[3,6,512,512]{3,2,1,0:T(8,128)(2,1)}, f32[6,1,512]{2,1,0:T(1,128)}, f32[6,512]{1,0:T(8,128)}) custom-call(s32[3]{0:T(128)} %pad_add_fusion.info_ref, bf16[1536,512]{1,0:T(8,128)(2,1)} %copy-done.3, bf16[1536,512]{1,0:T(8,128)(2,1)} %copy-done.4, bf16[512,512]{1,0:T(8,128)(2,1)} %convolution_convert_fusion.second_ref, f32[8,512]{1,0:T(8,128)} %copy-done.6, ...), custom_call_target="tpu_custom_call" | custom-call | flops 12079595520 | bytes 18874368 | tf_op jit(solution)/shard_map/trail/pallas_call | solution.py:218
  (103 shorter events, 43.3 us)
Async XLA Ops:
  7.2 221.8 %all-gather.3.cloned.1.call-start = ((), (), s32[]{:S(2)}) async-start(), calls=%async_computation.1 | async-start | bytes 6684672 | tf_op jit(solution)/shard_map/all_gather | solution.py:155
  62.2 9.0 %collective-permute-start = (bf16[3,64,512]{2,1,0:T(8,128)(2,1)}, bf16[3,64,512]{2,1,0:T(8,128)(2,1)S(1)}, u32[]{:S(2)}, u32[]{:S(2)}) collective-permute-start(bf16[3,64,512]{2,1,0:T(8,128)(2,1)} %get-tuple-element.18), channel_id=1, source_target_pairs={{0,1},{1,2},{8,9},{9,10},{16,17},{17,18},{24,25},{25,26},{32,33},{... | collective-permute-start | bytes 589832 | tf_op jit(solution)/shard_map/ppermute | solution.py:16
  63.6 9.0 %collective-permute-start.1 = (bf16[3,64,512]{2,1,0:T(8,128)(2,1)}, bf16[3,64,512]{2,1,0:T(8,128)(2,1)S(1)}, u32[]{:S(2)}, u32[]{:S(2)}) collective-permute-start(bf16[3,64,512]{2,1,0:T(8,128)(2,1)} %get-tuple-element.19), channel_id=1, source_target_pairs={{0,2},{1,3},{8,10},{9,11},{16,18},{17,19},{24,26},{25,27},{32,34},... | collective-permute-start | bytes 589832 | tf_op jit(solution)/shard_map/ppermute | solution.py:16
  67.0 9.8 %collective-permute-start.2 = (bf16[3,64,512]{2,1,0:T(8,128)(2,1)}, bf16[3,64,512]{2,1,0:T(8,128)(2,1)S(1)}, u32[]{:S(2)}, u32[]{:S(2)}) collective-permute-start(bf16[3,64,512]{2,1,0:T(8,128)(2,1)} %get-tuple-element.20), channel_id=1, source_target_pairs={{0,3},{1,4},{8,11},{9,12},{16,19},{17,20},{24,27},{25,28},{32,35},... | collective-permute-start | bytes 589832 | tf_op jit(solution)/shard_map/ppermute | solution.py:16
  68.3 12.7 %collective-permute-start.3 = (bf16[3,64,512]{2,1,0:T(8,128)(2,1)}, bf16[3,64,512]{2,1,0:T(8,128)(2,1)S(1)}, u32[]{:S(2)}, u32[]{:S(2)}) collective-permute-start(bf16[3,64,512]{2,1,0:T(8,128)(2,1)} %get-tuple-element.21), channel_id=1, source_target_pairs={{0,4},{1,5},{8,12},{9,13},{16,20},{17,21},{24,28},{25,29},{32,36},... | collective-permute-start | bytes 589832 | tf_op jit(solution)/shard_map/ppermute | solution.py:16
  69.9 13.5 %collective-permute-start.4 = (bf16[3,64,512]{2,1,0:T(8,128)(2,1)}, bf16[3,64,512]{2,1,0:T(8,128)(2,1)S(1)}, u32[]{:S(2)}, u32[]{:S(2)}) collective-permute-start(bf16[3,64,512]{2,1,0:T(8,128)(2,1)} %get-tuple-element.22), channel_id=1, source_target_pairs={{0,5},{1,6},{8,13},{9,14},{16,21},{17,22},{24,29},{25,30},{32,37},... | collective-permute-start | bytes 589832 | tf_op jit(solution)/shard_map/ppermute | solution.py:16
  71.2 12.1 %collective-permute-start.5 = (bf16[3,64,512]{2,1,0:T(8,128)(2,1)}, bf16[3,64,512]{2,1,0:T(8,128)(2,1)S(1)}, u32[]{:S(2)}, u32[]{:S(2)}) collective-permute-start(bf16[3,64,512]{2,1,0:T(8,128)(2,1)} %get-tuple-element.23), channel_id=1, source_target_pairs={{0,6},{1,7},{8,14},{9,15},{16,22},{17,23},{24,30},{25,31},{32,38},... | collective-permute-start | bytes 589832 | tf_op jit(solution)/shard_map/ppermute | solution.py:16
  72.6 10.8 %collective-permute-start.6 = (bf16[3,64,512]{2,1,0:T(8,128)(2,1)}, bf16[3,64,512]{2,1,0:T(8,128)(2,1)S(1)}, u32[]{:S(2)}, u32[]{:S(2)}) collective-permute-start(bf16[3,64,512]{2,1,0:T(8,128)(2,1)} %get-tuple-element.24), channel_id=1, source_target_pairs={{0,7},{1,0},{8,15},{9,8},{16,23},{17,16},{24,31},{25,24},{32,39},{... | collective-permute-start | bytes 589832 | tf_op jit(solution)/shard_map/ppermute | solution.py:16
  83.6 7.2 %collective-permute-start.9 = (bf16[64,512]{1,0:T(8,128)(2,1)S(1)}, bf16[64,512]{1,0:T(8,128)(2,1)S(1)}, u32[]{:S(2)}, u32[]{:S(2)}) collective-permute-start(bf16[64,512]{1,0:T(8,128)(2,1)S(1)} %fusion.2), channel_id=1, source_target_pairs={{0,24},{8,0},{1,25},{9,1},{2,26},{10,2},{3,27},{11,3},{4,28},{12,4... | collective-permute-start | bytes 196616 | tf_op jit(solution)/shard_map/ppermute | solution.py:16
  94.0 9.8 %collective-permute-start.11 = (bf16[2,64,512]{2,1,0:T(8,128)(2,1)S(1)}, bf16[2,64,512]{2,1,0:T(8,128)(2,1)S(1)}, u32[]{:S(2)}, u32[]{:S(2)}) collective-permute-start(bf16[2,64,512]{2,1,0:T(8,128)(2,1)S(1)} %pad_maximum_fusion.1), channel_id=1, source_target_pairs={{0,64},{1,65},{2,66},{3,67},{4,68},{5,69},{6,70},{7,71},{8,72},{9,... | collective-permute-start | bytes 393224 | tf_op jit(solution)/shard_map/ppermute | solution.py:16
  97.1 6.7 %collective-permute-start.12 = (bf16[2,64,512]{2,1,0:T(8,128)(2,1)S(1)}, bf16[2,64,512]{2,1,0:T(8,128)(2,1)S(1)}, u32[]{:S(2)}, u32[]{:S(2)}) collective-permute-start(bf16[2,64,512]{2,1,0:T(8,128)(2,1)S(1)} %pad_maximum_fusion.1), channel_id=1, source_target_pairs={{0,96},{1,97},{2,98},{3,99},{4,100},{5,101},{6,102},{7,103},{8,104... | collective-permute-start | bytes 393224 | tf_op jit(solution)/shard_map/ppermute | solution.py:16
  98.4 9.7 %collective-permute-start.10 = (bf16[2,64,512]{2,1,0:T(8,128)(2,1)S(1)}, bf16[2,64,512]{2,1,0:T(8,128)(2,1)S(1)}, u32[]{:S(2)}, u32[]{:S(2)}) collective-permute-start(bf16[2,64,512]{2,1,0:T(8,128)(2,1)S(1)} %pad_maximum_fusion.1), channel_id=1, source_target_pairs={{0,32},{1,33},{2,34},{3,35},{4,36},{5,37},{6,38},{7,39},{8,40},{9,... | collective-permute-start | bytes 393224 | tf_op jit(solution)/shard_map/ppermute | solution.py:16
  108.1 14.1 %collective-permute-start.13 = (bf16[2,64,512]{2,1,0:T(8,128)(2,1)S(1)}, bf16[2,64,512]{2,1,0:T(8,128)(2,1)S(1)}, u32[]{:S(2)}, u32[]{:S(2)}) collective-permute-start(bf16[2,64,512]{2,1,0:T(8,128)(2,1)S(1)} %select_select_fusion.2), channel_id=1, source_target_pairs={{0,7},{1,0},{2,1},{3,2},{4,3},{5,4},{6,5},{7,6},{8,15},{9,8},{10,9... | collective-permute-start | bytes 393224 | tf_op jit(solution)/shard_map/ppermute | solution.py:16
  116.0 66.9 %collective-permute-start.26 = (bf16[2,3,64,512]{3,2,1,0:T(8,128)(2,1)S(1)}, bf16[2,3,64,512]{3,2,1,0:T(8,128)(2,1)S(1)}, u32[]{:S(2)}, u32[]{:S(2)}) collective-permute-start(bf16[2,3,64,512]{3,2,1,0:T(8,128)(2,1)S(1)} %pad_maximum_fusion.refs_0_), channel_id=1, source_target_pairs={{0,7},{1,0},{2,1},{3,2},{4,3},{5,4},{6,5},{7,6},{8,15},{9,8},{10,9... | collective-permute-start | bytes 1179656 | tf_op jit(solution)/shard_map/ppermute | solution.py:16
  116.0 67.0 %collective-permute-start.25 = (bf16[2,3,64,512]{3,2,1,0:T(8,128)(2,1)S(1)}, bf16[2,3,64,512]{3,2,1,0:T(8,128)(2,1)S(1)}, u32[]{:S(2)}, u32[]{:S(2)}) collective-permute-start(bf16[2,3,64,512]{3,2,1,0:T(8,128)(2,1)S(1)} %pad_maximum_fusion.refs_0_), channel_id=1, source_target_pairs={{0,6},{1,7},{2,0},{3,1},{4,2},{5,3},{6,4},{7,5},{8,14},{9,15},{10,... | collective-permute-start | bytes 1179656 | tf_op jit(solution)/shard_map/ppermute | solution.py:16
  118.9 64.3 %collective-permute-start.24 = (bf16[2,3,64,512]{3,2,1,0:T(8,128)(2,1)S(1)}, bf16[2,3,64,512]{3,2,1,0:T(8,128)(2,1)S(1)}, u32[]{:S(2)}, u32[]{:S(2)}) collective-permute-start(bf16[2,3,64,512]{3,2,1,0:T(8,128)(2,1)S(1)} %pad_maximum_fusion.refs_0_), channel_id=1, source_target_pairs={{0,5},{1,6},{2,7},{3,0},{4,1},{5,2},{6,3},{7,4},{8,13},{9,14},{10,... | collective-permute-start | bytes 1179656 | tf_op jit(solution)/shard_map/ppermute | solution.py:16
  118.9 64.3 %collective-permute-start.23 = (bf16[2,3,64,512]{3,2,1,0:T(8,128)(2,1)S(1)}, bf16[2,3,64,512]{3,2,1,0:T(8,128)(2,1)S(1)}, u32[]{:S(2)}, u32[]{:S(2)}) collective-permute-start(bf16[2,3,64,512]{3,2,1,0:T(8,128)(2,1)S(1)} %pad_maximum_fusion.refs_0_), channel_id=1, source_target_pairs={{0,4},{1,5},{2,6},{3,7},{4,0},{5,1},{6,2},{7,3},{8,12},{9,13},{10,... | collective-permute-start | bytes 1179656 | tf_op jit(solution)/shard_map/ppermute | solution.py:16
  122.2 29.3 %collective-permute-start.14 = (bf16[2,64,512]{2,1,0:T(8,128)(2,1)S(1)}, bf16[2,64,512]{2,1,0:T(8,128)(2,1)S(1)}, u32[]{:S(2)}, u32[]{:S(2)}) collective-permute-start(bf16[2,64,512]{2,1,0:T(8,128)(2,1)S(1)} %select_select_fusion.2), channel_id=1, source_target_pairs={{0,6},{1,7},{2,0},{3,1},{4,2},{5,3},{6,4},{7,5},{8,14},{9,15},{10,... | collective-permute-start | bytes 393224 | tf_op jit(solution)/shard_map/ppermute | solution.py:16
  156.8 6.9 %collective-permute-start.16 = (bf16[2,64,512]{2,1,0:T(8,128)(2,1)S(1)}, bf16[2,64,512]{2,1,0:T(8,128)(2,1)S(1)}, u32[]{:S(2)}, u32[]{:S(2)}) collective-permute-start(bf16[2,64,512]{2,1,0:T(8,128)(2,1)S(1)} %select_select_fusion.2), channel_id=1, source_target_pairs={{0,4},{1,5},{2,6},{3,7},{4,0},{5,1},{6,2},{7,3},{8,12},{9,13},{10,... | collective-permute-start | bytes 393224 | tf_op jit(solution)/shard_map/ppermute | solution.py:16
  163.7 7.2 %collective-permute-start.17 = (bf16[2,64,512]{2,1,0:T(8,128)(2,1)S(1)}, bf16[2,64,512]{2,1,0:T(8,128)(2,1)S(1)}, u32[]{:S(2)}, u32[]{:S(2)}) collective-permute-start(bf16[2,64,512]{2,1,0:T(8,128)(2,1)S(1)} %select_select_fusion.2), channel_id=1, source_target_pairs={{0,3},{1,4},{2,5},{3,6},{4,7},{5,0},{6,1},{7,2},{8,11},{9,12},{10,... | collective-permute-start | bytes 393224 | tf_op jit(solution)/shard_map/ppermute | solution.py:16
  182.7 12.9 %collective-permute-start.22 = (bf16[2,3,64,512]{3,2,1,0:T(8,128)(2,1)S(1)}, bf16[2,3,64,512]{3,2,1,0:T(8,128)(2,1)S(1)}, u32[]{:S(2)}, u32[]{:S(2)}) collective-permute-start(bf16[2,3,64,512]{3,2,1,0:T(8,128)(2,1)S(1)} %pad_maximum_fusion.refs_0_), channel_id=1, source_target_pairs={{0,3},{1,4},{2,5},{3,6},{4,7},{5,0},{6,1},{7,2},{8,11},{9,12},{10,... | collective-permute-start | bytes 1179656 | tf_op jit(solution)/shard_map/ppermute | solution.py:16
  182.9 18.7 %collective-permute-start.21 = (bf16[2,3,64,512]{3,2,1,0:T(8,128)(2,1)S(1)}, bf16[2,3,64,512]{3,2,1,0:T(8,128)(2,1)S(1)}, u32[]{:S(2)}, u32[]{:S(2)}) collective-permute-start(bf16[2,3,64,512]{3,2,1,0:T(8,128)(2,1)S(1)} %pad_maximum_fusion.refs_0_), channel_id=1, source_target_pairs={{0,2},{1,3},{2,4},{3,5},{4,6},{5,7},{6,0},{7,1},{8,10},{9,11},{10,... | collective-permute-start | bytes 1179656 | tf_op jit(solution)/shard_map/ppermute | solution.py:16
  183.0 20.9 %collective-permute-start.20 = (bf16[2,3,64,512]{3,2,1,0:T(8,128)(2,1)S(1)}, bf16[2,3,64,512]{3,2,1,0:T(8,128)(2,1)S(1)}, u32[]{:S(2)}, u32[]{:S(2)}) collective-permute-start(bf16[2,3,64,512]{3,2,1,0:T(8,128)(2,1)S(1)} %pad_maximum_fusion.refs_0_), channel_id=1, source_target_pairs={{0,1},{1,2},{2,3},{3,4},{4,5},{5,6},{6,7},{7,0},{8,9},{9,10},{10,1... | collective-permute-start | bytes 1179656 | tf_op jit(solution)/shard_map/ppermute | solution.py:16
  218.7 6.3 %collective-permute-start.31 = (f32[8,512]{1,0:T(8,128)S(1)}, f32[8,512]{1,0:T(8,128)S(1)}, u32[]{:S(2)}, u32[]{:S(2)}) collective-permute-start(f32[8,512]{1,0:T(8,128)S(1)} %add_add_fusion.1), channel_id=1, source_target_pairs={{0,64},{32,96},{64,0},{96,32},{1,65},{33,97},{65,1},{97,33},{2,66}... | collective-permute-start | bytes 49160 | tf_op jit(solution)/shard_map/ppermute | solution.py:16
  (18 other events, 190.1 us)
Sparse Core Ops, SparseCore 0:
  58.9 61.3 all-gather.2
